TPU v7x, 32 devices: a whole 2x2x4 slice. The times are simulated.
32 devices in a mesh: band: 2 (over x), vis: 16 (over z, y, core).
Axes of the slice: x: 2, y: 2, z: 4, core: 2. Of those that a mesh axis runs over, the one named last changes fastest.
Arguments:
- sky_image: float32 [4096, 4096], P(('band', 'vis')), as said below
- coef_dual: float32 [4, 2048, 2048], P(None, ('band', 'vis')), may hold values from -12 to 12
- vis_dual: float32 [2, 16, 16, 4, 2, 32], P('band', 'vis'), may hold values from -12 to 12
- visibilities: float32 [2, 16, 16, 4, 2, 32], P('band', 'vis')
- kernel_blocks: bfloat16 [2, 16, 16, 4, 2, 32, 256], P('band', 'vis'), may hold values from -0.375 to 0.375
- tile_rows: int32 [2, 16, 16, 4], P('band', 'vis'), may hold values from 0 to 2047
- tile_counts: int32 [2, 16, 16], P('band', 'vis'), may hold values from 1 to 4, as said below
Outputs:
- new_image: float32 [4096, 4096], P(('band', 'vis'))
- new_coef_dual: float32 [4, 2048, 2048], P(None, ('band', 'vis'))
- new_vis_dual: float32 [2, 16, 16, 4, 2, 32], P('band', 'vis')
Inputs may be any that keep to these rules, and one draw needn't show every extreme that they name: `sky_image`: nonnegative. `tile_counts`: in every band some owner q has all 4 slots live from every device of that band.
All inputs are finite; a program needn't handle non-finite values.
Results may differ from a plain program's by a relative error of at most 0.0018.
Values may be sent and summed in bfloat16 or wider, within the bound.
A program may use at most 128 MiB of HBM per device.

v0:
```python
import math

import jax
import numpy as np
import jax.numpy as jnp
from jax import lax
from jax.experimental import pallas as pl
from jax.experimental.pallas import tpu as pltpu
from jax.sharding import PartitionSpec as P

IMG = 4096


low_taps = (
    -0.010597401784997278,
    0.032883011666982945,
    0.030841381835986965,
    -0.18703481171888114,
    -0.02798376941698385,
    0.6308807679295904,
    0.7148465705525415,
    0.23037781330885523,
)
high_taps = tuple(((-1.0) ** offset * low_taps[7 - offset] for offset in range(8)))
highest = lax.Precision.HIGHEST


def shifted(block, axis, distance):
    devices = range(lax.axis_size(axis))
    route = [((i - distance) % len(devices), i) for i in devices]
    return lax.ppermute(block, axis, route)


def dft_table(table_size, sign):
    positions = jnp.arange(table_size, dtype=jnp.int32)
    phase = positions[:, None] * positions[None, :] % table_size
    angle = 2.0 * math.pi / table_size * phase.astype(jnp.float32)
    return (jnp.cos(angle), sign * jnp.sin(angle))


def section_one(table, values):
    return jnp.einsum("kn,...nm->...km", table, values, precision=highest)


def section_two(table, values):
    return jnp.einsum("qm,...km->...qk", table, values, precision=highest)


def dft_last(real_in, imag_in, sign):
    leading = real_in.shape[:-1]
    length = real_in.shape[-1]
    inner_len = 64
    outer_len = length // inner_len
    split_real = real_in.reshape(leading + (outer_len, inner_len))
    table_real, table_imag = dft_table(outer_len, sign)
    first_real = section_one(table_real, split_real)
    first_imag = section_one(table_imag, split_real)
    if imag_in is not None:
        split_imag = imag_in.reshape(leading + (outer_len, inner_len))
        first_real = first_real - section_one(table_imag, split_imag)
        first_imag = first_imag + section_one(table_real, split_imag)
    outer_index = jnp.arange(outer_len, dtype=jnp.int32)
    inner_index = jnp.arange(inner_len, dtype=jnp.int32)
    twist_phase = outer_index[:, None] * inner_index[None, :] % length
    twist_angle = 2.0 * math.pi / length * twist_phase.astype(jnp.float32)
    twist_real = jnp.cos(twist_angle)
    twist_imag = sign * jnp.sin(twist_angle)
    mid_real = first_real * twist_real - first_imag * twist_imag
    mid_imag = first_real * twist_imag + first_imag * twist_real
    last_real, last_imag = dft_table(inner_len, sign)
    out_real = section_two(last_real, mid_real) - section_two(last_imag, mid_imag)
    out_imag = section_two(last_real, mid_imag) + section_two(last_imag, mid_real)
    factor = 1.0 / math.sqrt(length)
    return (
        (out_real * factor).reshape(leading + (length,)),
        (out_imag * factor).reshape(leading + (length,)),
    )


def pieces_from_image(extrap, band_count, group_count):
    rows_dev = extrap.shape[0]
    image_width = extrap.shape[1]
    stripe = image_width // band_count
    piece_cols = stripe // group_count
    piece_rows = image_width // group_count
    col_real, col_imag = dft_last(extrap, None, -1.0)
    shaped = jnp.stack([col_real, col_imag]).reshape(
        2, 1, 1, rows_dev, band_count, group_count, piece_cols
    )
    moved = lax.all_to_all(
        lax.all_to_all(shaped, "band", split_axis=4, concat_axis=1, tiled=True),
        "vis",
        split_axis=5,
        concat_axis=2,
        tiled=True,
    )
    columns = jnp.transpose(moved.reshape(2, image_width, piece_cols), (2, 0, 1))
    row_real, row_imag = dft_last(columns[:, 0], columns[:, 1], -1.0)
    stacked = (
        jnp.stack([row_real, row_imag], axis=1)
        .astype(jnp.bfloat16)
        .reshape(piece_cols, 2, group_count, piece_rows)
    )
    pieces = lax.all_to_all(stacked, "vis", split_axis=2, concat_axis=0, tiled=True)
    return pieces.reshape(stripe, 2, piece_rows)


def image_from_pieces(piece_sum, band_count, group_count):
    stripe = piece_sum.shape[0]
    piece_rows = piece_sum.shape[2]
    piece_cols = stripe // group_count
    image_width = piece_rows * group_count
    rows_dev = image_width // (band_count * group_count)
    spread = lax.all_to_all(
        piece_sum.reshape(stripe, 2, 1, piece_rows), "vis", split_axis=0, concat_axis=2, tiled=True
    )
    spread = spread.reshape(piece_cols, 2, image_width)
    col_real, col_imag = dft_last(spread[:, 0], spread[:, 1], 1.0)
    stacked = jnp.transpose(jnp.stack([col_real, col_imag]), (0, 2, 1))
    shaped = stacked.reshape(2, band_count, group_count, rows_dev, 1, 1, piece_cols)
    moved = lax.all_to_all(
        lax.all_to_all(shaped, "band", split_axis=1, concat_axis=4, tiled=True),
        "vis",
        split_axis=2,
        concat_axis=5,
        tiled=True,
    )
    moved = moved.reshape(2, rows_dev, image_width)
    out_real, out_imag = dft_last(moved[0], moved[1], 1.0)
    return out_real


def cols_down(field):
    image_width = field.shape[1]
    extended = jnp.concatenate([field, field[:, :6]], axis=1)
    low_part = 0.0
    high_part = 0.0
    for offset in range(8):
        taken = extended[:, offset : offset + image_width : 2]
        low_part = low_part + low_taps[offset] * taken
        high_part = high_part + high_taps[offset] * taken
    return (low_part, high_part)


def cols_up(low_part, high_part):
    halves = []
    for parity in range(2):
        summed = 0.0
        for delay in range(4):
            summed = summed + low_taps[parity + 2 * delay] * jnp.roll(low_part, delay, axis=1)
            summed = summed + high_taps[parity + 2 * delay] * jnp.roll(high_part, delay, axis=1)
        halves.append(summed)
    return jnp.stack(halves, axis=2).reshape(low_part.shape[0], 2 * low_part.shape[1])


def rows_up(low_ext, high_ext, half_rows):
    halves = []
    for parity in range(2):
        summed = 0.0
        for delay in range(4):
            begin = 3 - delay
            summed = summed + low_taps[parity + 2 * delay] * low_ext[begin : begin + half_rows]
            summed = summed + high_taps[parity + 2 * delay] * high_ext[begin : begin + half_rows]
        halves.append(summed)
    return jnp.stack(halves, axis=1).reshape(2 * half_rows, low_ext.shape[1])


def analysis(extrap):
    rows_dev = extrap.shape[0]
    taken_rows = min(6, rows_dev)
    parts_list = [extrap]
    parts_list.append(shifted(extrap[:taken_rows], ("band", "vis"), -1))
    extended = jnp.concatenate(parts_list, axis=0)
    half_rows = rows_dev // 2
    rows_low = 0.0
    rows_high = 0.0
    for offset in range(8):
        taken = extended[offset : offset + 2 * half_rows : 2]
        rows_low = rows_low + low_taps[offset] * taken
        rows_high = rows_high + high_taps[offset] * taken
    low_low, low_high = cols_down(rows_low)
    high_low, high_high = cols_down(rows_high)
    return jnp.stack([low_low, low_high, high_low, high_high])


def synthesis(coef_dual):
    half_rows = coef_dual.shape[1]
    taken_rows = min(3, half_rows)
    parts_list = [shifted(coef_dual[:, half_rows - taken_rows :, :], ("band", "vis"), 1)]
    joined = jnp.concatenate(parts_list[::-1] + [coef_dual], axis=1)
    cols_low = rows_up(joined[0], joined[2], half_rows)
    cols_high = rows_up(joined[1], joined[3], half_rows)
    return cols_up(cols_low, cols_high)


def degrid(kernel_here, tiles):
    kernel_real = kernel_here[:, :, 0]
    kernel_imag = kernel_here[:, :, 1]
    tile_real = tiles[:, :, 0]
    tile_imag = tiles[:, :, 1]
    out_real = jnp.einsum(
        "qsat,qst->qsa", kernel_real, tile_real, preferred_element_type=jnp.float32
    ) - jnp.einsum("qsat,qst->qsa", kernel_imag, tile_imag, preferred_element_type=jnp.float32)
    out_imag = jnp.einsum(
        "qsat,qst->qsa", kernel_real, tile_imag, preferred_element_type=jnp.float32
    ) + jnp.einsum("qsat,qst->qsa", kernel_imag, tile_real, preferred_element_type=jnp.float32)
    return jnp.stack([out_real, out_imag], axis=2)


def grid_back(kernel_here, weights):
    kernel_real = kernel_here[:, :, 0]
    kernel_imag = kernel_here[:, :, 1]
    weight_real = weights[:, :, 0]
    weight_imag = weights[:, :, 1]
    grid_real = jnp.einsum(
        "qsat,qsa->qst", kernel_real, weight_real, preferred_element_type=jnp.float32
    ) + jnp.einsum("qsat,qsa->qst", kernel_imag, weight_imag, preferred_element_type=jnp.float32)
    grid_imag = jnp.einsum(
        "qsat,qsa->qst", kernel_real, weight_imag, preferred_element_type=jnp.float32
    ) - jnp.einsum("qsat,qsa->qst", kernel_imag, weight_real, preferred_element_type=jnp.float32)
    return jnp.stack([grid_real, grid_imag], axis=2)


def local(sky_image, coef_dual, vis_dual, visibilities, kernel_blocks, tile_rows, tile_counts):
    band_count = lax.axis_size("band")
    group_count = lax.axis_size("vis")
    kernel_here = kernel_blocks[0, 0]
    rows_here = tile_rows[0, 0]
    slot_count = rows_here.shape[1]
    live_slots = (
        jnp.arange(slot_count, dtype=jnp.int32)[None, :] < tile_counts[0, 0][:, None]
    ).astype(jnp.float32)[:, :, None, None]
    vis_data = visibilities[0, 0]
    vis_state = vis_dual[0, 0]
    image_width = sky_image.shape[1]
    stripe = image_width // band_count
    piece_rows = image_width // group_count
    incoming_rows = lax.all_to_all(rows_here, "vis", split_axis=0, concat_axis=0, tiled=True)
    data_part = jnp.sum(live_slots * vis_data * vis_data)
    weights = (live_slots * vis_state).astype(jnp.bfloat16)
    contrib = grid_back(kernel_here, weights)
    arrived = lax.all_to_all(contrib, "vis", split_axis=0, concat_axis=0, tiled=True)
    piece_sum = jax.ops.segment_sum(
        arrived.reshape(-1, 2, piece_rows), incoming_rows.reshape(-1), num_segments=stripe
    )
    adjoint_part = image_from_pieces(piece_sum, band_count, group_count)
    smooth = synthesis(coef_dual)
    new_image = jnp.maximum(sky_image - smooth - adjoint_part, 0.0)
    extrap = 2.0 * new_image - sky_image
    coeffs = analysis(extrap)
    abs_total = jnp.sum(jnp.abs(coeffs))
    coef_total = lax.psum(abs_total, ("band", "vis"))
    threshold = 0.5 * coef_total / (IMG * IMG)
    coef_dual = jnp.clip(coef_dual + coeffs, -threshold, threshold)
    piece_grid = pieces_from_image(extrap, band_count, group_count)
    tiles = lax.all_to_all(
        piece_grid[incoming_rows], "vis", split_axis=0, concat_axis=0, tiled=True
    )
    predicted = degrid(kernel_here, tiles)
    residual = live_slots * (vis_state + predicted - vis_data)
    resid_square = jnp.sum(residual * residual)
    norm_square, data_square = lax.psum((resid_square, data_part), ("band", "vis"))
    radius = 0.5 * jnp.sqrt(data_square + 1e-06)
    size_value = jnp.sqrt(norm_square + 1e-06)
    vis_state = residual * (1.0 - jnp.minimum(1.0, radius / size_value))
    return (new_image, coef_dual, vis_state[None, None])


high = lax.Precision.HIGH
everywhere = ("band", "vis")


def wave_tables(length, digit_low):
    digit_high = length // digit_low
    low = np.arange(digit_low)
    wide = np.arange(digit_high)
    full = 2.0 * np.pi
    small = full * (low[:, None] * low[None, :] % digit_low) / digit_low
    twist = full * (low[:, None] * wide[None, :]) / length
    large = full * (wide[:, None] * wide[None, :] % digit_high) / digit_high
    return small, twist, large


def complex_matrix(angle, sign):
    c = np.cos(angle)
    s = sign * np.sin(angle)
    return np.stack([np.stack([c, -s], axis=1), np.stack([s, c], axis=1)])


def f32(values):
    return jnp.asarray(np.asarray(values, np.float32))


def bf16(values):
    return f32(values).astype(jnp.bfloat16)


def analysis_matrix(half):
    matrix = np.zeros((2, half, 2 * half + 6))
    for k in range(half):
        for j in range(8):
            matrix[0, k, 2 * k + j] = low_taps[j]
            matrix[1, k, 2 * k + j] = high_taps[j]
    return matrix.reshape(2 * half, 2 * half + 6)


def synthesis_matrix(half):
    matrix = np.zeros((2 * half, 2, half + 3))
    for n in range(2 * half):
        for delay in range(4):
            tap = n % 2 + 2 * delay
            matrix[n, 0, n // 2 - delay + 3] = low_taps[tap]
            matrix[n, 1, n // 2 - delay + 3] = high_taps[tap]
    return matrix


def fast_analysis(extrap, halo):
    rows_dev, width = extrap.shape
    extended = jnp.concatenate([extrap, halo], axis=0)
    by_rows = jnp.einsum("ij,jn->in", f32(analysis_matrix(rows_dev // 2)), extended, precision=high)
    size = 256
    blocks = by_rows.reshape(rows_dev, width // size, size)
    following = jnp.roll(blocks, -1, axis=1)[:, :, :6]
    matrix = analysis_matrix(size // 2)
    out = jnp.einsum("rbi,ji->rbj", blocks, f32(matrix[:, :size]), precision=high)
    out = out + jnp.einsum("rbi,ji->rbj", following, f32(matrix[:, size:]), precision=high)
    out = out.reshape(2, rows_dev // 2, width // size, 2, size // 2)
    return jnp.transpose(out, (0, 3, 1, 2, 4)).reshape(4, rows_dev // 2, width // 2)


def fast_synthesis(coef_dual):
    half_rows, half_width = coef_dual.shape[1:]
    halo = shifted(coef_dual[:, half_rows - 3 :, :], everywhere, 1)
    joined = jnp.concatenate([halo, coef_dual], axis=1)
    joined = joined.reshape(2, 2, half_rows + 3, half_width)
    by_rows = jnp.einsum("irj,rcjn->cin", f32(synthesis_matrix(half_rows)), joined, precision=high)
    size = 128
    blocks = by_rows.reshape(2, 2 * half_rows, half_width // size, size)
    before = jnp.roll(blocks, 1, axis=2)[:, :, :, size - 3 :]
    matrix = synthesis_matrix(size)
    out = jnp.einsum("cibk,nck->ibn", blocks, f32(matrix[:, :, 3:]), precision=high)
    out = out + jnp.einsum("cibk,nck->ibn", before, f32(matrix[:, :, :3]), precision=high)
    return out.reshape(2 * half_rows, 2 * half_width)


def cos_sums(values, size):
    half = size // 2
    if half < 2:
        return [values[0] + values[1], values[0] - values[1]]
    quarter = half // 2
    plus = [values[a] + values[half - a] for a in range(quarter)] + [values[quarter]]
    minus = [values[a] - values[half - a] for a in range(quarter)]
    out = [None] * (half + 1)
    out[0::2] = cos_sums(plus, half)
    for k in range(1, half, 2):
        total = minus[0]
        for a in range(1, quarter):
            total = total + minus[a] * math.cos(2 * math.pi * (a * k % size) / size)
        out[k] = total
    return out


def sin_sums(values, size):
    half = size // 2
    if half < 2:
        return [None] * (half + 1)
    quarter = half // 2
    plus = {a: values[a] + values[half - a] for a in range(1, quarter)}
    plus[quarter] = values[quarter]
    minus = [None] + [values[a] - values[half - a] for a in range(1, quarter)]
    out = [None] * (half + 1)
    out[0::2] = sin_sums(minus, half)
    for k in range(1, half, 2):
        total = None
        for a in range(1, quarter + 1):
            factor = math.sin(2 * math.pi * (a * k % size) / size)
            term = plus[a] if a * 4 == size and k % 4 == 1 else plus[a] * factor
            total = term if total is None else total + term
        out[k] = total
    return out


def even_odd(values):
    size = len(values)
    half = size // 2
    even = [values[0]] + [values[a] + values[size - a] for a in range(1, half)] + [values[half]]
    odd = [None] + [values[a] - values[size - a] for a in range(1, half)]
    return even, odd


def split(values):
    upper = values.astype(jnp.bfloat16)
    return upper, (values - upper.astype(jnp.float32)).astype(jnp.bfloat16)


def table_pair(values):
    upper = f32(values).astype(jnp.bfloat16)
    return upper, (f32(values) - upper.astype(jnp.float32)).astype(jnp.bfloat16)


def nt_dot(a, b):
    return lax.dot_general(a, b, (((1,), (1,)), ((), ())), preferred_element_type=jnp.float32)


def nn_dot(a, b):
    return lax.dot_general(a, b, (((1,), (0,)), ((), ())), preferred_element_type=jnp.float32)


LEVELS = 32000.0
MESH = pl.DeviceIdType.MESH
LANES = 128
whole = pl.BlockSpec(memory_space=pltpu.VMEM)


def place():
    band = lax.axis_index("band")
    vis = lax.axis_index("vis")
    groups = lax.axis_size("vis")
    z = vis // 4
    y = vis // 2 % 2
    core = vis % 2
    return band, z, y, core, groups


def gather_kernel(block_ref, cols_ref, out_ref, all_cols_ref, send_a, send_b, recv_a, recv_b):
    x, z, y, core, groups = place()
    levels = groups // 4

    def index(px, pz, py, pc):
        return px * groups + pz * 4 + py * 2 + pc

    def device(px, pz, py, pc):
        return (px, pz * 4 + py * 2 + pc)

    me = index(x, z, y, core)
    fx, fy = x * (1 - core) + (1 - x) * core, (1 - y) * (1 - core) + y * core
    sx, sy = (1 - x) * (1 - core) + x * core, y * (1 - core) + (1 - y) * core
    up, down, first, second, twin = 0, 1, 2, 3, 4
    targets = [
        device(x, z + 1, y, core),
        device(x, z - 1, y, core),
        device(fx, z, fy, core),
        device(sx, z, sy, core),
        device(x, z, y, 1 - core),
    ]
    has_up, has_down = z < levels - 1, z > 0
    barrier = pltpu.get_barrier_semaphore()

    def signal(way):
        pl.semaphore_signal(barrier, inc=1, device_id=targets[way], device_id_type=MESH)

    pl.when(has_up)(lambda: signal(up))
    pl.when(has_down)(lambda: signal(down))
    for way in (first, second, twin):
        signal(way)
    pl.semaphore_wait(barrier, 5 - (z + 1) // levels - (levels - z) // levels)

    def copies(block, way):
        own_a, own_b = out_ref.at[block], all_cols_ref.at[block]
        return [
            pltpu.make_async_remote_copy(
                src_ref=own_a,
                dst_ref=own_a,
                send_sem=send_a.at[way, block],
                recv_sem=recv_a.at[block],
                device_id=targets[way],
                device_id_type=MESH,
            ),
            pltpu.make_async_remote_copy(
                src_ref=own_b,
                dst_ref=own_b,
                send_sem=send_b.at[way, block],
                recv_sem=recv_b.at[block],
                device_id=targets[way],
                device_id_type=MESH,
            ),
        ]

    def start(block, way):
        for copy in copies(block, way):
            copy.start()

    def sent(block, way):
        for copy in copies(block, way):
            copy.wait_send()

    def got(block):
        for copy in copies(block, twin):
            copy.wait_recv()

    out_ref[me] = block_ref[...]
    all_cols_ref[me] = cols_ref[...]

    pl.when(has_up)(lambda: start(me, up))
    pl.when(has_down)(lambda: start(me, down))
    for way in (first, second, twin):
        start(me, way)

    def each_line(px, py, action):
        def at(j):
            if j == 0:
                action(index(px, z, py, core), 0)
                return
            pl.when(z >= j)(lambda: action(index(px, z - j, py, core), 1))
            pl.when(z + j < levels)(lambda: action(index(px, z + j, py, core), -1))

        return at

    def own_line(do):
        def action(block, heading):
            if heading == 0:
                return
            do(block, heading)

        return action

    def take_own(block, heading):
        got(block)
        if heading > 0:
            pl.when(has_up)(lambda: start(block, up))
        else:
            pl.when(has_down)(lambda: start(block, down))
        for way in (first, second, twin):
            start(block, way)

    def take_first(block, heading):
        got(block)
        for way in (second, twin):
            start(block, way)

    def take_second(block, heading):
        got(block)
        start(block, twin)

    dx, dy = 1 - x, 1 - y
    lines = [
        each_line(x, y, own_line(take_own)),
        each_line(fx, fy, take_first),
        each_line(sx, sy, take_second),
        each_line(dx, dy, take_second),
    ]
    for j in range(levels):
        for at in lines:
            at(j)

    for i in range(groups):
        bx, rest = i // (groups // 2), i % (groups // 2)
        got(bx * groups + rest * 2 + 1 - core)

    def end_own(block, heading):
        if heading == 0:
            pl.when(has_up)(lambda: sent(block, up))
            pl.when(has_down)(lambda: sent(block, down))
        elif heading > 0:
            pl.when(has_up)(lambda: sent(block, up))
        else:
            pl.when(has_down)(lambda: sent(block, down))
        for way in (first, second, twin):
            sent(block, way)

    def end_first(block, heading):
        for way in (second, twin):
            sent(block, way)

    def end_second(block, heading):
        sent(block, twin)

    lines = [
        each_line(x, y, end_own),
        each_line(fx, fy, end_first),
        each_line(sx, sy, end_second),
        each_line(dx, dy, end_second),
    ]
    for j in range(levels):
        for at in lines:
            at(j)


def gather_all(block, cols, devices):
    return pl.pallas_call(
        gather_kernel,
        out_shape=(
            jax.ShapeDtypeStruct((devices,) + block.shape, block.dtype),
            jax.ShapeDtypeStruct((devices,) + cols.shape, cols.dtype),
        ),
        in_specs=[whole] * 2,
        out_specs=(whole, whole),
        scratch_shapes=[
            pltpu.SemaphoreType.DMA((5, devices)),
            pltpu.SemaphoreType.DMA((5, devices)),
            pltpu.SemaphoreType.DMA((devices,)),
            pltpu.SemaphoreType.DMA((devices,)),
        ],
        compiler_params=pltpu.CompilerParams(collective_id=0, has_side_effects=True),
        name="gather_all",
    )(block, cols)


def level(values):
    return jnp.round(values).astype(jnp.int32)


def image_kernel(
    low,
    block_ref,
    cols_ref,
    turn_ref,
    phase_ref,
    inv_ref,
    tw_ref,
    fwd_ref,
    sky_ref,
    smooth_ref,
    image_ref,
    extrap_ref,
    picked_ref,
    unit_ref,
    fold_ref,
    grid_ref,
    hot_ref,
    half_ref,
    spec_ref,
    rest_ref,
):
    rows = sky_ref.shape[0]
    tiles = block_ref.shape[0]
    kept = low // 2 + 1
    wide = LANES
    lane = lax.broadcasted_iota(jnp.int32, (1, LANES), 1)
    for i in range(tiles // LANES):
        columns = jnp.where(lane < LANES // 2, cols_ref[2 * i], cols_ref[2 * i + 1])
        k1 = columns % low
        k2 = columns // low
        flip = k1 >= kept
        k1 = jnp.where(flip, low - k1, k1)
        k2 = jnp.where(flip, wide - 1 - k2, k2)
        fold_ref[0, i : i + 1, :] = (k1 * wide + k2).astype(jnp.float32)
        fold_ref[1, i : i + 1, :] = jnp.where(flip, -1.0, 1.0)
    chunk = 512
    for j in range(tiles // chunk):
        both = nt_dot(turn_ref[...], block_ref[j * chunk : (j + 1) * chunk, :])
        for i in range(chunk // LANES):
            b = j * (chunk // LANES) + i
            real = both[:rows, i * LANES : (i + 1) * LANES]
            imag = both[rows:, i * LANES : (i + 1) * LANES]
            out_real = real * phase_ref[0] - imag * phase_ref[1]
            out_imag = (real * phase_ref[1] + imag * phase_ref[0]) * fold_ref[1, b : b + 1, :]
            grid_ref[:rows, b * LANES : (b + 1) * LANES] = out_real.astype(jnp.bfloat16)
            grid_ref[rows:, b * LANES : (b + 1) * LANES] = out_imag.astype(jnp.bfloat16)

    def scatter(p, carry):
        base = pl.multiple_of(p * 2 * wide, 2 * wide)
        row = (lax.broadcasted_iota(jnp.int32, (2 * wide, LANES), 0) + base).astype(jnp.float32)
        for i in range(tiles // LANES):
            hit = row == fold_ref[0, i : i + 1, :]
            hot_ref[pl.ds(base, 2 * wide), i * LANES : (i + 1) * LANES] = jnp.where(
                hit, 1.0, 0.0
            ).astype(jnp.bfloat16)
        folded = nt_dot(grid_ref[...], hot_ref[pl.ds(base, 2 * wide), :]).astype(jnp.bfloat16)
        for e in range(2):
            pair = jnp.concatenate(
                [folded[:rows, e * wide : (e + 1) * wide], folded[rows:, e * wide : (e + 1) * wide]],
                axis=1,
            )
            mid = nn_dot(pair, inv_ref[...])
            k1 = p * 2 + e
            tw_real, tw_imag = tw_ref[0, pl.ds(k1, 1), :], tw_ref[1, pl.ds(k1, 1), :]
            real, imag = mid[:, :wide], mid[:, wide:]
            half_ref[k1, :, :wide] = real * tw_real - imag * tw_imag
            half_ref[k1, :, wide:] = real * tw_imag + imag * tw_real
        return carry

    lax.fori_loop(0, (kept + 1) // 2, scatter, 0)

    def strip(i, carry):
        at = pl.ds(pl.multiple_of(i * 8, 8), 8)
        cos_part = cos_sums([half_ref[k, at, :wide] for k in range(kept)], low)
        sin_part = sin_sums([None] + [half_ref[k, at, wide:] for k in range(1, kept - 1)], low)
        extraps = []
        for a in range(low):
            k = min(a, low - a)
            if a == 0 or a == low // 2:
                adjoint = cos_part[k]
            elif a < low // 2:
                adjoint = cos_part[k] - sin_part[k]
            else:
                adjoint = cos_part[k] + sin_part[k]
            here = slice(a * wide, (a + 1) * wide)
            sky = sky_ref[at, here]
            image = jnp.maximum(sky - smooth_ref[at, here] - adjoint, 0.0)
            extrap = 2.0 * image - sky
            image_ref[at, here] = image
            extrap_ref[at, here] = extrap
            extraps.append(extrap)
        even, odd = even_odd(extraps)
        real_part = cos_sums(even, low)
        imag_part = sin_sums(odd, low)
        for k in range(kept):
            tw_real, tw_imag = tw_ref[0, k : k + 1, :], tw_ref[1, k : k + 1, :]
            real = real_part[k] * tw_real
            imag = -real_part[k] * tw_imag
            if 0 < k < kept - 1:
                real = real - imag_part[k] * tw_imag
                imag = imag - imag_part[k] * tw_real
            half_ref[k, at, :wide] = real
            half_ref[k, at, wide:] = imag
        return carry

    lax.fori_loop(0, rows // 8, strip, 0)

    for k in range(kept):
        upper, lower = split(half_ref[k])
        out = nn_dot(upper, fwd_ref[0]) + nn_dot(lower, fwd_ref[0]) + nn_dot(upper, fwd_ref[1])
        here = slice(k * wide, (k + 1) * wide)
        upper, lower = split(out)
        spec_ref[:rows, here] = upper[:, :wide]
        spec_ref[rows:, here] = upper[:, wide:]
        rest_ref[:rows, here] = lower[:, :wide]
        rest_ref[rows:, here] = lower[:, wide:]

    def pick(j, carry):
        at = pl.multiple_of(j * 2 * LANES, 2 * LANES)
        hot = hot_ref[: kept * wide, pl.ds(at, 2 * LANES)]
        got = nn_dot(spec_ref[...], hot) + nn_dot(rest_ref[...], hot)
        for h in range(2):
            sign = fold_ref[1, pl.ds(2 * j + h, 1), :]
            real = got[:rows, h * LANES : (h + 1) * LANES]
            imag = got[rows:, h * LANES : (h + 1) * LANES] * sign
            most = jnp.max(jnp.maximum(jnp.abs(real), jnp.abs(imag)), axis=0, keepdims=True)
            most = jnp.maximum(most, 1e-30)
            unit_ref[2 * j + h] = most * (1.0 / LEVELS)
            to_level = LEVELS / most
            packed = level(real * to_level) * 65536 + level(imag * to_level)
            to = pl.ds(pl.multiple_of(at + h * LANES, LANES), LANES)
            picked_ref[to, :] = packed.T
        return carry

    lax.fori_loop(0, tiles // (2 * LANES), pick, 0)


def image_step(blocks, cols, me, sky_image, smooth, groups, slots, piece):
    rows, width = sky_image.shape
    tiles = blocks.shape[0] * blocks.shape[1]
    low = width // LANES
    kept = low // 2 + 1
    turn = np.arange(piece)
    angle = (me * rows + jnp.arange(rows, dtype=jnp.int32))[:, None] * turn[None, :] % width
    angle = (2.0 * math.pi / width) * angle.astype(jnp.float32)
    cosine, sine = jnp.cos(angle), jnp.sin(angle)
    turn = jnp.concatenate(
        [jnp.concatenate([cosine, -sine], axis=1), jnp.concatenate([sine, cosine], axis=1)]
    ).astype(jnp.bfloat16)
    owner = np.arange(LANES) // slots % groups
    shift = 2 * np.pi * (np.arange(rows)[:, None] * owner[None, :] % groups) / groups
    phase = f32(np.stack([np.cos(shift), np.sin(shift)]))
    wide = np.arange(LANES)
    full = 2 * np.pi * (wide[:, None] * wide[None, :] % LANES) / LANES
    c, s = np.cos(full) / width, np.sin(full) / width
    inverse = bf16(np.block([[c, s], [-s, c]]))
    forward = jnp.stack(table_pair(np.block([[c, -s], [s, c]])))
    twist = 2 * np.pi * np.arange(kept + 1)[:, None] * wide[None, :] / width
    twist = f32(np.stack([np.cos(twist), np.sin(twist)]))
    return pl.pallas_call(
        lambda *refs: image_kernel(low, *refs),
        out_shape=(
            jax.ShapeDtypeStruct((rows, width), jnp.float32),
            jax.ShapeDtypeStruct((rows, width), jnp.float32),
            jax.ShapeDtypeStruct((tiles, rows), jnp.int32),
            jax.ShapeDtypeStruct((tiles // LANES, 1, LANES), jnp.float32),
        ),
        in_specs=[whole] * 9,
        out_specs=(whole,) * 4,
        scratch_shapes=[
            pltpu.VMEM((2, tiles // LANES, LANES), jnp.float32),
            pltpu.VMEM((2 * rows, tiles), jnp.bfloat16),
            pltpu.VMEM(((kept + 1) * LANES, tiles), jnp.bfloat16),
            pltpu.VMEM((kept + 1, rows, 2 * LANES), jnp.float32),
            pltpu.VMEM((2 * rows, kept * LANES), jnp.bfloat16),
            pltpu.VMEM((2 * rows, kept * LANES), jnp.bfloat16),
        ],
        compiler_params=pltpu.CompilerParams(vmem_limit_bytes=60 * 2**20),
        name="image_step",
    )(
        blocks.reshape(tiles, -1),
        cols,
        turn,
        phase,
        inverse,
        twist,
        forward,
        sky_image,
        smooth,
    )


def exchange_kernel(
    picked_ref, unit_ref, top_ref, got_ref, units_ref, below_ref, send_a, send_b, recv_a, recv_b, halo
):
    x, z, y, core, groups = place()
    devices = 2 * groups
    tiles = got_ref.shape[1]

    def flipped(value, bit):
        return value + (1 - 2 * (value // bit % 2)) * bit

    me = x * groups + z * 4 + y * 2 + core
    barrier = pltpu.get_barrier_semaphore()
    peers = []
    for code in sorted(range(1, devices), key=lambda code: -(code // 8 % 2)):
        vis = z * 4 + y * 2 + core
        for bit in (1, 2, 4, 8):
            if code & bit:
                vis = flipped(vis, bit)
        band = 1 - x if code & 16 else x
        peers.append((band, vis))
    for peer in peers:
        pl.semaphore_signal(barrier, inc=1, device_id=peer, device_id_type=MESH)
    before = (me + devices - 1) % devices
    pl.semaphore_wait(barrier, devices - 1)
    edge = pltpu.make_async_remote_copy(
        src_ref=top_ref,
        dst_ref=below_ref,
        send_sem=halo.at[0],
        recv_sem=halo.at[1],
        device_id=(before // groups, before % groups),
        device_id_type=MESH,
    )
    edge.start()
    copies = []
    for i, (band, vis) in enumerate(peers):
        to = band * groups + vis
        at = pl.ds(pl.multiple_of(to * tiles, tiles), tiles)
        copies.append(
            pltpu.make_async_remote_copy(
                src_ref=picked_ref.at[at, :],
                dst_ref=got_ref.at[me],
                send_sem=send_a.at[i],
                recv_sem=recv_a.at[i],
                device_id=(band, vis),
                device_id_type=MESH,
            )
        )
        copies.append(
            pltpu.make_async_remote_copy(
                src_ref=unit_ref.at[to // 2],
                dst_ref=units_ref.at[me],
                send_sem=send_b.at[i],
                recv_sem=recv_b.at[i],
                device_id=(band, vis),
                device_id_type=MESH,
            )
        )
    for copy in copies:
        copy.start()
    here = pl.ds(pl.multiple_of(me * tiles, tiles), tiles)
    got_ref[me] = picked_ref[here, :]
    units_ref[me] = unit_ref[me // 2]
    edge.wait()
    for copy in copies:
        copy.wait()


def exchange(picked, units, extrap, devices):
    tiles = picked.shape[0] // devices
    top = extrap[:8]
    return pl.pallas_call(
        exchange_kernel,
        out_shape=(
            jax.ShapeDtypeStruct((devices, tiles) + picked.shape[1:], picked.dtype),
            jax.ShapeDtypeStruct((devices,) + units.shape[1:], units.dtype),
            jax.ShapeDtypeStruct(top.shape, top.dtype),
        ),
        in_specs=[whole] * 3,
        out_specs=(whole,) * 3,
        scratch_shapes=[
            pltpu.SemaphoreType.DMA((devices - 1,)),
            pltpu.SemaphoreType.DMA((devices - 1,)),
            pltpu.SemaphoreType.DMA((devices - 1,)),
            pltpu.SemaphoreType.DMA((devices - 1,)),
            pltpu.SemaphoreType.DMA((2,)),
        ],
        compiler_params=pltpu.CompilerParams(collective_id=1, has_side_effects=True),
        name="exchange",
    )(picked, units, top)


def tile_kernel(
    devices, got_ref, units_ref, phase_ref, last_ref, order_ref, out_ref, mid_ref, unit_ref
):
    tiles, rows = phase_ref.shape[1:]
    group = LANES * 2 // 16
    units = jnp.concatenate([units_ref[d] for d in range(devices)], axis=0)
    units = jnp.concatenate([units] * (LANES // devices), axis=0).T
    unit_ref[...] = jnp.where(lax.axis_index("vis") % 2 == 0, units[:tiles], units[tiles:])

    def strip(i, carry):
        at = pl.multiple_of(i * 8, 8)
        here = pl.ds(at, 8)
        cosine, sine = phase_ref[0, here, :], phase_ref[1, here, :]
        reals, imags = [], []
        for d in range(devices):
            packed = got_ref[d, here, :]
            real = (packed + 32768) >> 16
            imag = packed - (real << 16)
            unit = unit_ref[here, d : d + 1]
            real = real.astype(jnp.float32) * unit
            imag = imag.astype(jnp.float32) * unit
            reals.append(real * cosine + imag * sine)
            imags.append(imag * cosine - real * sine)
        even, odd = even_odd(reals)
        cos_real, sin_real = cos_sums(even, devices), sin_sums(odd, devices)
        even, odd = even_odd(imags)
        cos_imag, sin_imag = cos_sums(even, devices), sin_sums(odd, devices)
        half = devices // 2
        for k in range(half + 1):
            if k == 0 or k == half:
                outs = [(k, cos_real[k], cos_imag[k])]
            else:
                outs = [
                    (k, cos_real[k] + sin_imag[k], cos_imag[k] - sin_real[k]),
                    (devices - k, cos_real[k] - sin_imag[k], cos_imag[k] + sin_real[k]),
                ]
            for t, real, imag in outs:
                mid_ref[t, here, :rows] = real
                mid_ref[t, here, rows:] = imag
        return carry

    lax.fori_loop(0, tiles // 8, strip, 0)
    lane = lax.broadcasted_iota(jnp.int32, (1, 2 * LANES), 1) // 16
    pieces = []
    for g in range(devices // group):
        total = None
        for e in range(group):
            upper, lower = split(mid_ref[g * group + e])
            out = nn_dot(upper, last_ref[0, g]) + nn_dot(lower, last_ref[0, g])
            out = out + nn_dot(upper, last_ref[1, g])
            out = jnp.where(lane == e, out, 0.0)
            total = out if total is None else total + out
        pieces.append(total.astype(jnp.bfloat16))
    tile = jnp.concatenate(pieces, axis=1)
    out_ref[...] = nn_dot(tile, order_ref[...])


def finish_tiles(got, units, devices, groups, slots, rows, piece):
    width = devices * rows
    tiles = groups * slots
    shift = np.arange(tiles)[:, None] // slots * np.arange(rows)[None, :] % groups
    shift = 2 * np.pi * shift / groups
    phase = f32(np.stack([np.cos(shift), np.sin(shift)]))
    each = piece // devices
    t = np.arange(devices)[:, None] + devices * np.arange(each)[None, :]
    angle = 2 * np.pi * (np.arange(rows)[:, None, None] * t[None] % width) / width
    c, s = np.cos(angle), np.sin(angle)
    table = np.stack([np.stack([c, -s], axis=2), np.stack([s, c], axis=2)])
    table = table.reshape(2 * rows, -1, 2 * LANES).transpose(1, 0, 2)
    last = jnp.stack(table_pair(table))
    order = np.zeros((2 * piece, 2 * piece))
    for a in range(devices):
        for part in range(2):
            for b in range(each):
                order[(a * 2 + part) * each + b, part * piece + a + devices * b] = 1.0
    return pl.pallas_call(
        lambda *refs: tile_kernel(devices, *refs),
        out_shape=jax.ShapeDtypeStruct((tiles, 2 * piece), jnp.float32),
        in_specs=[whole] * 5,
        out_specs=whole,
        scratch_shapes=[
            pltpu.VMEM((devices, tiles, 2 * rows), jnp.float32),
            pltpu.VMEM((tiles, LANES), jnp.float32),
        ],
        compiler_params=pltpu.CompilerParams(vmem_limit_bytes=40 * 2**20),
        name="finish_tiles",
    )(got, units, phase, last, bf16(order))


def to_all(values, devices):
    flat = jnp.broadcast_to(values.reshape(1, -1), (devices, values.size))
    return lax.all_to_all(flat, everywhere, split_axis=0, concat_axis=0, tiled=True)


def fast_local(sky_image, coef_dual, vis_dual, visibilities, kernel_blocks, tile_rows, tile_counts):
    bands = lax.axis_size("band")
    groups = lax.axis_size("vis")
    devices = bands * groups
    me = lax.axis_index(everywhere)
    kernel_here = kernel_blocks[0, 0]
    slots = tile_rows.shape[3]
    rows_dev, width = sky_image.shape
    piece = width // groups
    stripe = width // bands
    tiles = groups * slots
    live_slots = (
        jnp.arange(slots, dtype=jnp.int32)[None, :] < tile_counts[0, 0][:, None]
    ).astype(jnp.float32)[:, :, None, None]
    vis_data = visibilities[0, 0]
    vis_state = vis_dual[0, 0]
    columns_here = (tile_rows[0, 0] + lax.axis_index("band") * stripe).reshape(1, tiles)
    columns_here = jnp.concatenate([columns_here, columns_here], axis=1)
    weights = (live_slots * vis_state).astype(jnp.bfloat16)
    contrib = grid_back(kernel_here, weights).astype(jnp.bfloat16).reshape(tiles, 2 * piece)
    blocks, cols = gather_all(contrib, columns_here, devices)
    smooth = fast_synthesis(coef_dual)
    new_image, extrap, picked, units = image_step(
        blocks, cols, me, sky_image, smooth, groups, slots, piece
    )
    got, units, below = exchange(picked, units, extrap, devices)
    tile = finish_tiles(got, units, devices, groups, slots, rows_dev, piece)
    tile = tile.astype(jnp.bfloat16).reshape(groups, slots, 2, piece)
    coeffs = fast_analysis(extrap, below[:6])
    predicted = degrid(kernel_here, tile)
    residual = live_slots * (vis_state + predicted - vis_data)
    sums = jnp.stack(
        [
            jnp.sum(jnp.abs(coeffs)),
            jnp.sum(residual * residual),
            jnp.sum(live_slots * vis_data * vis_data),
        ]
    )
    sums = jnp.sum(to_all(sums, devices), axis=0)
    threshold = 0.5 * sums[0] / (width * width)
    coef_dual = jnp.clip(coef_dual + coeffs, -threshold, threshold)
    radius = 0.5 * jnp.sqrt(sums[2] + 1e-06)
    size_value = jnp.sqrt(sums[1] + 1e-06)
    vis_state = residual * (1.0 - jnp.minimum(1.0, radius / size_value))
    return (new_image, coef_dual, vis_state[None, None])


def body_for(mesh):
    devices = mesh.shape["band"] * mesh.shape["vis"]
    relayed = mesh.shape["band"] == 2 and mesh.shape["vis"] % 4 == 0 and devices == 32

    def body(sky_image, *rest):
        rows, width = sky_image.shape
        piece = width // mesh.shape["vis"]
        tiles = rest[4].shape[2] * rest[4].shape[3]
        if relayed and rows == LANES and piece == 2 * LANES and 2 * tiles == LANES:
            return fast_local(sky_image, *rest)
        return local(sky_image, *rest)

    return body


def solution(mesh):
    return jax.shard_map(
        body_for(mesh),
        mesh=mesh,
        in_specs=(
            P(("band", "vis"), None),
            P(None, ("band", "vis"), None),
            P("band", "vis", None, None, None, None),
            P("band", "vis", None, None, None, None),
            P("band", "vis", None, None, None, None, None),
            P("band", "vis", None, None),
            P("band", "vis", None),
        ),
        out_specs=(
            P(("band", "vis"), None),
            P(None, ("band", "vis"), None),
            P("band", "vis", None, None, None, None),
        ),
        check_vma=False,
    )
```

profile of v0, /device:TPU:0, one launch (start us, length us, event | category | flops | bytes accessed | tf_op | source)
XLA Modules:
  0.0 162.0 jit_solution(5379145879117377531)
XLA Ops:
  0.6 1.1 slice.64
  2.3 0.7 fusion.41
  3.0 0.9 fusion.27
  4.0 1.5 fusion.3
  5.5 1.5 fusion.8
  9.7 36.7 %gather_all.1 = (bf16[32,64,512]{2,1,0:T(8,128)(2,1)}, s32[32,1,128]{2,1,0:T(1,128)}) custom-call(bf16[64,512]{1,0:T(8,128)(2,1)} %bitcast.150, s32[1,128]{1,0:T(1,128)} %pad_add_fusion.cols_ref), custom_call_target="tpu_custom_call" | custom-call | tf_op jit(solution)/shard_map/gather_all/pallas_call | solution.py:580
  48.0 3.5 %fusion.46 = f32[2,2048,128,1]{2,1,0,3:T(8,128)S(1)} fusion(f32[2,2,67,2048]{3,2,1,0:T(8,128)S(1)} %bitcast.140, f32[128,2,67,1]{0,2,3,1:T(8,128)S(1)} %copy-done.13), kind=kOutput, calls=%fused_computation.80 | convolution fusion | flops 421527552 | bytes 4361216 | tf_op jit(solution)/shard_map/irj,rcjn->cin/dot_general | solution.py:336
  51.6 1.8 %fusion.47 = f32[128,16,256,1]{2,0,1,3:T(8,128)S(1)} fusion(f32[2,128,16,128]{1,3,2,0:T(8,128)S(1)} %bitcast.142, f32[256,2,128,1]{2,0,3,1:T(8,128)S(1)} %copy-done.10), kind=kOutput, calls=%fused_computation.81 | convolution fusion | flops 805306368 | bytes 4456448 | tf_op jit(solution)/shard_map/cibk,nck->ibn/dot_general | solution.py:341
  53.5 1.1 fusion
  54.5 1.5 copy.116
  56.1 23.5 %image_step.1 = (f32[128,4096]{1,0:T(8,128)}, f32[128,4096]{1,0:T(8,128)}, s32[2048,128]{1,0:T(8,128)}, f32[16,1,128]{2,1,0:T(1,128)}) custom-call(bf16[2048,512]{1,0:T(8,128)(2,1)} %bitcast.145, s32[32,1,128]{2,1,0:T(1,128)} %get-tuple-element.13.refs_1_, bf16[256,512]{1,0:T(8,128)(2,1)} %maximum_maximum_fusion.refs_2_, ...), custom_call_target="tpu_custom_call" | custom-call | tf_op jit(solution)/shard_map/image_step/pallas_call | solution.py:763
  79.5 1.6 slice.68.top_ref
  81.1 31.6 %exchange.1 = (s32[32,64,128]{2,1,0:T(8,128)}, f32[32,1,128]{2,1,0:T(1,128)}, f32[8,4096]{1,0:T(8,128)}) custom-call(s32[2048,128]{1,0:T(8,128)} %get-tuple-element.16.picked_ref, f32[16,1,128]{2,1,0:T(1,128)} %get-tuple-element.17.unit_ref, f32[8,4096]{1,0:T(8,128)} %slice.68.top_ref), custom_call_target="tpu_custom_call" | custom-call | tf_op jit(solution)/shard_map/exchange/pallas_call | solution.py:866
  112.7 1.2 copy-done
  114.6 4.3 %finish_tiles.1 = f32[64,512]{1,0:T(8,128)S(1)} custom-call(s32[32,64,128]{2,1,0:T(8,128)S(1)} %copy-done, f32[32,1,128]{2,1,0:T(1,128)S(1)} %copy-done.4, f32[2,64,128]{2,1,0:T(8,128)S(1)} %copy-done.3, bf16[2,2,256,256]{3,2,1,0:T(8,128)(2,1)S(1)} %copy-done.2, bf16[512,512]{1,0:T(8,128)(2,1)S(1)} %copy-done.1), custom_call_target="tpu_custom_call" | custom-call | tf_op jit(solution)/shard_map/finish_tiles/pallas_call | solution.py:962
  119.2 1.8 %fusion.5 = f32[16,4,1,32]{3,2,1,0:T(1,128)S(1)} fusion(bf16[16,4,2,32,256]{4,3,2,1,0:T(8,128)(2,1)} %bitcast.163, bf16[16,4,256,1]{2,0,1,3:T(8,128)(2,1)S(1)} %bitcast.156), kind=kOutput, calls=%fused_computation.13 | convolution fusion | flops 1048576 | bytes 1089536 | tf_op jit(solution)/shard_map/qsat,qst->qsa/dot_general | solution.py:206
  120.9 1.8 %fusion.2 = f32[16,4,1,32]{3,2,1,0:T(1,128)S(1)} fusion(bf16[16,4,2,32,256]{4,3,2,1,0:T(8,128)(2,1)} %bitcast.164, bf16[16,4,256,1]{2,0,1,3:T(8,128)(2,1)S(1)} %bitcast.157), kind=kOutput, calls=%fused_computation.10 | convolution fusion | flops 1048576 | bytes 1089536 | tf_op jit(solution)/shard_map/qsat,qst->qsa/dot_general | solution.py:201
  122.7 1.6 fusion.1
  124.8 1.8 %fusion.48 = f32[4096,128]{1,0:T(8,128)S(1)} fusion(f32[128,4096]{1,0:T(8,128)S(1)} %copy-done.7, f32[128,128]{1,0:T(8,128)S(1)} %copy-done.15), kind=kOutput, calls=%fused_computation.82 | convolution fusion | flops 402653184 | bytes 4259840 | tf_op jit(solution)/shard_map/ij,jn->in/dot_general | solution.py:320
  126.6 1.8 %convolution_add_fusion = f32[4096,128]{1,0:T(8,128)S(1)} fusion(f32[4096,128]{1,0:T(8,128)S(1)} %fusion.48, f32[128,6]{1,0:T(8,128)S(1)} %copy-done.14, f32[8,4096]{1,0:T(8,128)S(1)} %copy-done.12), kind=kOutput, calls=%fused_computation | convolution fusion | flops 19398656 | bytes 4328448 | tf_op jit(solution)/shard_map/ij,jn->in/dot_general | solution.py:320
  128.6 0.8 copy-done.9
  129.4 1.9 %fusion.49 = f32[128,16,256]{2,0,1:T(8,128)S(1)} fusion(f32[128,16,256]{0,2,1:T(8,128)S(1)} %bitcast.139, f32[256,256,1]{1,0,2:T(8,128)S(1)} %copy-done.9), kind=kOutput, calls=%fused_computation.83 | convolution fusion | flops 805306368 | bytes 4456448 | tf_op jit(solution)/shard_map/rbi,ji->rbj/dot_general | solution.py:325
  131.3 2.4 %convolution_add_fusion.1 = f32[128,16,256]{2,0,1:T(8,128)} fusion(f32[128,16,256]{2,0,1:T(8,128)S(1)} %fusion.49, f32[256,6,1]{0,1,2:T(8,128)S(1)} %copy-done.16, f32[128,1,256]{0,2,1:T(8,128)S(1)} %slice.87, f32[128,15,256]{0,2,1:T(8,128)S(1)} %slice.86), kind=kOutput, calls=%fused_computation.6 | convolution fusion | flops 19410944 | bytes 6297600 | tf_op jit(solution)/shard_map/rbi,ji->rbj/dot_general | solution.py:326
  133.6 2.3 %reshape.102 = f32[2,64,16,2,128]{4,3,1,0,2:T(2,128)S(1)} reshape(f32[128,16,256]{2,0,1:T(8,128)} %convolution_add_fusion.1) | data formatting | bytes 4194304 | tf_op jit(solution)/shard_map/reshape | solution.py:327
  136.0 2.8 %abs_reduce_fusion = f32[]{:T(128)} fusion(f32[2,64,16,2,128]{4,3,1,0,2:T(2,128)S(1)} %reshape.102), kind=kLoop, calls=%fused_computation.5 | loop fusion | flops 1048575 | bytes 2097156 | tf_op jit(solution)/shard_map/reduce_sum | solution.py:1014
  139.5 2.0 %pad_maximum_fusion.6 = f32[3]{0:T(128)S(1)} fusion(f32[1]{0:T(128)} %bitcast.53, f32[1]{0:T(128)} %bitcast.52, f32[1]{0:T(128)} %bitcast.36), kind=kLoop, calls=%fused_computation.74 | loop fusion | flops 6 | bytes 24 | tf_op jit(solution)/shard_map/stack | solution.py:1012
  142.1 5.9 %all-to-all-start = ((f32[32,1,3]{2,1,0:T(1,128)}), f32[32,1,3]{2,1,0:T(1,128)S(1)}, u32[]{:S(2)}, u32[]{:S(2)}) async-start(f32[32,1,3]{2,1,0:T(1,128)} %broadcast_in_dim.2), calls=%async_computation | async-start | bytes 32768 | tf_op jit(solution)/shard_map/all_to_all | solution.py:978
  148.0 2.5 %copy.89 = f32[2,2,64,16,128]{4,3,2,1,0:T(8,128)} copy(f32[2,2,64,16,128]{4,1,2,0,3:T(2,128)S(1)} %bitcast.136) | data formatting | bytes 4194304 | tf_op jit(solution)/shard_map/transpose | solution.py:328
  150.6 2.9 %reshape.104 = f32[4,64,2048]{2,1,0:T(8,128)} reshape(f32[2,2,64,16,128]{4,3,2,1,0:T(8,128)} %copy.89) | data formatting | bytes 4194304 | tf_op jit(solution)/shard_map/reshape | solution.py:328
  153.5 1.7 %all-to-all-done = f32[32,1,3]{2,1,0:T(1,128)S(1)} async-done(((f32[32,1,3]{2,1,0:T(1,128)}), f32[32,1,3]{2,1,0:T(1,128)S(1)}, u32[]{:S(2)}, u32[]{:S(2)}) %all-to-all-start) | async-done | bytes 416 | tf_op jit(solution)/shard_map/all_to_all | solution.py:978
  157.8 3.4 %maximum_minimum_fusion = f32[4,64,2048]{2,1,0:T(8,128)} fusion(f32[4,64,2048]{2,1,0:T(8,128)S(1)} %copy-done.6, f32[4,64,2048]{2,1,0:T(8,128)} %reshape.104, f32[]{:T(128)S(6)} %neg.7, f32[]{:T(128)} %bitcast.54), kind=kLoop, calls=%fused_computation.4 | loop fusion | flops 1572864 | bytes 6291464 | tf_op jit(solution)/shard_map/jit(clip)/min | solution.py:1021
  161.2 0.8 fusion.24
  (72 shorter events, 8.3 us)
Async XLA Ops:
  0.6 6.4 %copy-start.19 = (bf16[1,1,16,4,2,32,256]{6,5,4,3,2,1,0:T(8,128)(2,1)S(1)}, bf16[1,1,16,4,2,32,256]{6,5,4,3,2,1,0:T(8,128)(2,1)}, u32[]{:S(2)}) copy-start(bf16[1,1,16,4,2,32,256]{6,5,4,3,2,1,0:T(8,128)(2,1)} %param.27) | copy-start | bytes 6291460
  1.8 45.4 %collective-permute-start = (f32[4,3,2048]{2,1,0:T(4,128)S(1)}, f32[4,3,2048]{2,1,0:T(4,128)S(1)}, u32[]{:S(2)}, u32[]{:S(2)}) collective-permute-start(f32[4,3,2048]{2,1,0:T(4,128)S(1)} %slice.64), channel_id=1, source_target_pairs={{31,0},{0,1},{1,2},{2,3},{3,4},{4,5},{5,6},{6,7},{7,8},{8,9},{9,10... | collective-permute-start | bytes 294920 | tf_op jit(solution)/shard_map/ppermute | solution.py:31
  4.0 3.5 %copy-start.18 = (s32[1,1,16,4]{2,3,1,0:T(4,128)S(1)}, s32[1,1,16,4]{2,3,1,0:T(4,128)}, u32[]{:S(2)}) copy-start(s32[1,1,16,4]{2,3,1,0:T(4,128)} %param.28) | copy-start | bytes 772
  7.0 40.2 %copy-start.5 = (f32[4,64,2048]{2,1,0:T(8,128)S(1)}, f32[4,64,2048]{2,1,0:T(8,128)}, u32[]{:S(2)}) copy-start(f32[4,64,2048]{2,1,0:T(8,128)} %param.24) | copy-start | bytes 6291460
  47.2 0.9 copy-start.13
  48.0 3.6 %copy-start.10 = (f32[256,2,128,1]{2,0,3,1:T(8,128)S(1)}, f32[256,2,128,1]{2,0,3,1:T(8,128)}, u32[]{:S(2)}) copy-start(f32[256,2,128,1]{2,0,3,1:T(8,128)} %constant.117) | copy-start | bytes 786436
  51.6 1.9 %copy-start.17 = (f32[256,2,3,1]{0,2,1,3:T(4,128)S(1)}, f32[256,2,3,1]{0,2,1,3:T(4,128)}, u32[]{:S(2)}) copy-start(f32[256,2,3,1]{0,2,1,3:T(4,128)} %constant.118) | copy-start | bytes 18436
  56.1 56.6 %copy-start.1 = (bf16[512,512]{1,0:T(8,128)(2,1)S(1)}, bf16[512,512]{1,0:T(8,128)(2,1)}, u32[]{:S(2)}) copy-start(bf16[512,512]{1,0:T(8,128)(2,1)} %constant.113.refs_4_) | copy-start | bytes 1572868
  56.1 56.6 %copy-start.2 = (bf16[2,2,256,256]{3,2,1,0:T(8,128)(2,1)S(1)}, bf16[2,2,256,256]{3,2,1,0:T(8,128)(2,1)}, u32[]{:S(2)}) copy-start(bf16[2,2,256,256]{3,2,1,0:T(8,128)(2,1)} %constant.112.refs_3_) | copy-start | bytes 1572868
  56.1 56.6 %copy-start.3 = (f32[2,64,128]{2,1,0:T(8,128)S(1)}, f32[2,64,128]{2,1,0:T(8,128)}, u32[]{:S(2)}) copy-start(f32[2,64,128]{2,1,0:T(8,128)} %constant.84.clone.refs_2_) | copy-start | bytes 196612
  112.7 1.2 copy-start
  113.9 0.7 copy-start.4
  119.2 5.2 %copy-start.20 = (bf16[1,1,16,4,2,32,256]{6,5,4,3,2,1,0:T(8,128)(2,1)S(1)}, bf16[1,1,16,4,2,32,256]{6,5,4,3,2,1,0:T(8,128)(2,1)}, u32[]{:S(2)}) copy-start(bf16[1,1,16,4,2,32,256]{6,5,4,3,2,1,0:T(8,128)(2,1)} %param.27) | copy-start | bytes 6291460
  120.9 3.8 %copy-start.7 = (f32[128,4096]{1,0:T(8,128)S(1)}, f32[128,4096]{1,0:T(8,128)}, u32[]{:S(2)}) copy-start(f32[128,4096]{1,0:T(8,128)} %get-tuple-element.15) | copy-start | bytes 6291460
  120.9 3.8 %copy-start.15 = (f32[128,128]{1,0:T(8,128)S(1)}, f32[128,128]{1,0:T(8,128)}, u32[]{:S(2)}) copy-start(f32[128,128]{1,0:T(8,128)} %constant.104) | copy-start | bytes 196612
  124.7 1.8 %copy-start.12 = (f32[8,4096]{1,0:T(8,128)S(1)}, f32[8,4096]{1,0:T(8,128)}, u32[]{:S(2)}) copy-start(f32[8,4096]{1,0:T(8,128)} %get-tuple-element.18) | copy-start | bytes 393220
  124.7 1.8 %copy-start.14 = (f32[128,6]{1,0:T(8,128)S(1)}, f32[128,6]{1,0:T(8,128)}, u32[]{:S(2)}) copy-start(f32[128,6]{1,0:T(8,128)} %constant.105) | copy-start | bytes 9220
  128.4 1.0 copy-start.9
  129.4 1.9 %copy-start.16 = (f32[256,6,1]{0,1,2:T(8,128)S(1)}, f32[256,6,1]{0,1,2:T(8,128)}, u32[]{:S(2)}) copy-start(f32[256,6,1]{0,1,2:T(8,128)} %constant.120) | copy-start | bytes 18436
  135.9 2.8 %copy-start.8 = (f32[1,1,16,4,2,32]{5,4,3,2,1,0:T(2,128)S(1)}, f32[1,1,16,4,2,32]{5,4,3,2,1,0:T(2,128)}, u32[]{:S(2)}) copy-start(f32[1,1,16,4,2,32]{5,4,3,2,1,0:T(2,128)} %param.25) | copy-start | bytes 49156
  136.0 2.8 %copy-start.11 = (f32[1,1,16,4,2,32]{5,4,3,2,1,0:T(2,128)S(1)}, f32[1,1,16,4,2,32]{5,4,3,2,1,0:T(2,128)}, u32[]{:S(2)}) copy-start(f32[1,1,16,4,2,32]{5,4,3,2,1,0:T(2,128)} %param.26) | copy-start | bytes 49156
  142.1 13.0 %all-to-all-start = ((f32[32,1,3]{2,1,0:T(1,128)}), f32[32,1,3]{2,1,0:T(1,128)S(1)}, u32[]{:S(2)}, u32[]{:S(2)}) async-start(f32[32,1,3]{2,1,0:T(1,128)} %broadcast_in_dim.2), calls=%async_computation | async-start | bytes 32768 | tf_op jit(solution)/shard_map/all_to_all | solution.py:978
  150.6 7.2 %copy-start.6 = (f32[4,64,2048]{2,1,0:T(8,128)S(1)}, f32[4,64,2048]{2,1,0:T(8,128)}, u32[]{:S(2)}) copy-start(f32[4,64,2048]{2,1,0:T(8,128)} %param.24) | copy-start | bytes 6291460
where the time goes:
time: 163 us; the launch traced here: 162 us
  Pallas kernels  96.1 us (59%)
  matrix products  23.3 us (14%)
  local copies, waits for them, and re-layouts  17.7 us (11%)
  other arithmetic  13.6 us (8%)
  starting transfers between devices  6.47 us (4%)
  between operations  3.07 us (2%)
  waiting for transfers between devices  1.7 us (1%)
    pallas_call x1, Pallas kernels, gather_all(): pl.pallas_call(gather_kernel, out_shape=(jax.ShapeDtypeStruct((devices,)...  36.7 us
    pallas_call x1, Pallas kernels, exchange(): pl.pallas_call(exchange_kernel, out_shape=(jax.ShapeDtypeStruct((devices,...  31.6 us
    pallas_call x1, Pallas kernels, image_step(): pl.pallas_call(lambda *refs: image_kernel(low, *refs), out_shape=(jax.Sha...  23.5 us
    all_to_all x1, starting transfers between devices, to_all(): lax.all_to_all(flat, everywhere, split_axis=0, concat_axis=0, tiled=True)  5.92 us
    pallas_call x1, Pallas kernels, finish_tiles(): pl.pallas_call(lambda *refs: tile_kernel(devices, *refs), out_shape=jax.S...  4.35 us
    unnamed x46, local copies, waits for them, and re-layouts  4.08 us
    dot_general x2, matrix products, fast_analysis(): jnp.einsum('ij,jn->in', f32(analysis_matrix(rows_dev // 2)), extended, pr...  3.63 us
    dot_general x1, matrix products, fast_synthesis(): jnp.einsum('irj,rcjn->cin', f32(synthesis_matrix(half_rows)), joined, pre...  3.53 us
  transfers between devices with their start and end apart: 2, of which 1 were waited for; matrix products, arithmetic and copies ran while one was open for 8% of the time, Pallas kernels for 23%

commit v1 on v0

--- a/solution.py
+++ b/solution.py
@@ -422,9 +422,35 @@
     return band, z, y, core, groups
 
 
-def gather_kernel(block_ref, cols_ref, out_ref, all_cols_ref, send_a, send_b, recv_a, recv_b):
+def taps_dot(values, tables):
+    upper, lower = split(values)
+    return nn_dot(upper, tables[0]) + nn_dot(lower, tables[0]) + nn_dot(upper, tables[1])
+
+
+def gather_kernel(
+    kernels_ref,
+    weights_ref,
+    cols_ref,
+    coef_ref,
+    up_ref,
+    edge_ref,
+    out_ref,
+    all_cols_ref,
+    smooth_ref,
+    tail_ref,
+    halo_ref,
+    joined_ref,
+    tall_ref,
+    send_a,
+    send_b,
+    recv_a,
+    recv_b,
+    halo_sem,
+):
     x, z, y, core, groups = place()
     levels = groups // 4
+    devices = 2 * groups
+    half_rows, half_width = coef_ref.shape[1:]
 
     def index(px, pz, py, pc):
         return px * groups + pz * 4 + py * 2 + pc
@@ -433,167 +459,178 @@
         return (px, pz * 4 + py * 2 + pc)
 
     me = index(x, z, y, core)
-    fx, fy = x * (1 - core) + (1 - x) * core, (1 - y) * (1 - core) + y * core
-    sx, sy = (1 - x) * (1 - core) + x * core, y * (1 - core) + (1 - y) * core
-    up, down, first, second, twin = 0, 1, 2, 3, 4
-    targets = [
-        device(x, z + 1, y, core),
-        device(x, z - 1, y, core),
-        device(fx, z, fy, core),
-        device(sx, z, sy, core),
-        device(x, z, y, 1 - core),
-    ]
-    has_up, has_down = z < levels - 1, z > 0
+    after, before = (me + 1) % devices, (me + devices - 1) % devices
+    twin = device(x, z, y, 1 - core)
+    line = [device(x, (z + k) % levels, y, core) for k in range(1, levels)]
+    corners = [(1 - x, y), (x, 1 - y), (1 - x, 1 - y)]
+    plane = [device(px, z, py, core) for px, py in corners]
+    follower = (after // groups, after % groups)
+    leader = (before // groups, before % groups)
     barrier = pltpu.get_barrier_semaphore()
-
-    def signal(way):
-        pl.semaphore_signal(barrier, inc=1, device_id=targets[way], device_id_type=MESH)
-
-    pl.when(has_up)(lambda: signal(up))
-    pl.when(has_down)(lambda: signal(down))
-    for way in (first, second, twin):
-        signal(way)
-    pl.semaphore_wait(barrier, 5 - (z + 1) // levels - (levels - z) // levels)
-
-    def copies(block, way):
+    peers = line + plane + [twin, follower, leader]
+    for peer in peers:
+        pl.semaphore_signal(barrier, inc=1, device_id=peer, device_id_type=MESH)
+
+    for c in range(4):
+        tail_ref[3 * c : 3 * c + 3, :] = coef_ref[c, half_rows - 3 :, :]
+    count = 16
+    span = kernels_ref.shape[0] * count // out_ref.shape[1]
+    lane = lax.broadcasted_iota(jnp.int32, (count, span), 1) // (span // count)
+    mine = lane == lax.broadcasted_iota(jnp.int32, (count, span), 0)
+    for i in range(out_ref.shape[1] // count):
+        spread = [jnp.where(mine, weights_ref[part, i : i + 1, :], 0.0) for part in range(2)]
+        spread = jnp.concatenate(spread, axis=0).astype(jnp.bfloat16)
+        both = nn_dot(spread, kernels_ref[i * span : (i + 1) * span, :])
+        both = jnp.concatenate([both[:count], both[count:]], axis=1)
+        out_ref[me, i * count : (i + 1) * count, :] = both.astype(jnp.bfloat16)
+    all_cols_ref[me] = cols_ref[...]
+    pl.semaphore_wait(barrier, len(peers))
+
+    started = []
+
+    def start(block, target, slot):
         own_a, own_b = out_ref.at[block], all_cols_ref.at[block]
-        return [
+        for own, send, recv in ((own_a, send_a, recv_a), (own_b, send_b, recv_b)):
+            copy = pltpu.make_async_remote_copy(
+                src_ref=own,
+                dst_ref=own,
+                send_sem=send.at[slot],
+                recv_sem=recv.at[block],
+                device_id=target,
+                device_id_type=MESH,
+            )
+            copy.start()
+            started.append(copy)
+
+    def got(block):
+        for ref, send, recv in ((out_ref, send_a, recv_a), (all_cols_ref, send_b, recv_b)):
             pltpu.make_async_remote_copy(
-                src_ref=own_a,
-                dst_ref=own_a,
-                send_sem=send_a.at[way, block],
-                recv_sem=recv_a.at[block],
-                device_id=targets[way],
+                src_ref=ref.at[block],
+                dst_ref=ref.at[block],
+                send_sem=send.at[0],
+                recv_sem=recv.at[block],
+                device_id=twin,
                 device_id_type=MESH,
-            ),
-            pltpu.make_async_remote_copy(
-                src_ref=own_b,
-                dst_ref=own_b,
-                send_sem=send_b.at[way, block],
-                recv_sem=recv_b.at[block],
-                device_id=targets[way],
-                device_id_type=MESH,
-            ),
-        ]
-
-    def start(block, way):
-        for copy in copies(block, way):
-            copy.start()
-
-    def sent(block, way):
-        for copy in copies(block, way):
-            copy.wait_send()
-
-    def got(block):
-        for copy in copies(block, twin):
-            copy.wait_recv()
-
-    out_ref[me] = block_ref[...]
-    all_cols_ref[me] = cols_ref[...]
-
-    pl.when(has_up)(lambda: start(me, up))
-    pl.when(has_down)(lambda: start(me, down))
-    for way in (first, second, twin):
-        start(me, way)
-
-    def each_line(px, py, action):
-        def at(j):
-            if j == 0:
-                action(index(px, z, py, core), 0)
-                return
-            pl.when(z >= j)(lambda: action(index(px, z - j, py, core), 1))
-            pl.when(z + j < levels)(lambda: action(index(px, z + j, py, core), -1))
-
-        return at
-
-    def own_line(do):
-        def action(block, heading):
-            if heading == 0:
-                return
-            do(block, heading)
-
-        return action
-
-    def take_own(block, heading):
+            ).wait_recv()
+
+    slots = iter(range(send_a.shape[0]))
+    far = sorted(range(1, levels), key=lambda k: abs(k - levels / 2))
+    for k in far:
+        start(me, line[k - 1], next(slots))
+    for target in plane:
+        start(me, target, next(slots))
+    edge = pltpu.make_async_remote_copy(
+        src_ref=tail_ref,
+        dst_ref=halo_ref,
+        send_sem=halo_sem.at[0],
+        recv_sem=halo_sem.at[1],
+        device_id=follower,
+        device_id_type=MESH,
+    )
+    edge.start()
+    start(me, twin, next(slots))
+
+    for c in range(4):
+        joined_ref[c, 8:, :] = coef_ref[c]
+    edge.wait()
+    for c in range(4):
+        joined_ref[c, 5:8, :] = halo_ref[3 * c : 3 * c + 3, :]
+
+    line_blocks = [index(x, (z + levels - k) % levels, y, core) for k in range(1, levels)]
+    for block in line_blocks:
         got(block)
-        if heading > 0:
-            pl.when(has_up)(lambda: start(block, up))
-        else:
-            pl.when(has_down)(lambda: start(block, down))
-        for way in (first, second, twin):
-            start(block, way)
-
-    def take_first(block, heading):
+        for target in plane:
+            start(block, target, next(slots))
+        start(block, twin, next(slots))
+
+    def tall(i, carry):
+        here = pl.ds(pl.multiple_of(i * LANES, LANES), LANES)
+        for c in range(2):
+            for k in range(half_rows // 8):
+                low = [joined_ref[c, 8 + 8 * k - d : 16 + 8 * k - d, here] for d in range(4)]
+                high = [joined_ref[c + 2, 8 + 8 * k - d : 16 + 8 * k - d, here] for d in range(4)]
+                for parity in range(2):
+                    total = 0.0
+                    for d in range(4):
+                        total = total + low_taps[parity + 2 * d] * low[d]
+                        total = total + high_taps[parity + 2 * d] * high[d]
+                    tall_ref[c, i, pl.ds(16 * k + parity, 8, stride=2), :] = total
+        return carry
+
+    lax.fori_loop(0, half_width // LANES, tall, 0)
+
+    for px, py in corners:
+        block = index(px, z, py, core)
         got(block)
-        for way in (second, twin):
-            start(block, way)
-
-    def take_second(block, heading):
-        got(block)
-        start(block, twin)
-
-    dx, dy = 1 - x, 1 - y
-    lines = [
-        each_line(x, y, own_line(take_own)),
-        each_line(fx, fy, take_first),
-        each_line(sx, sy, take_second),
-        each_line(dx, dy, take_second),
-    ]
-    for j in range(levels):
-        for at in lines:
-            at(j)
+        start(block, twin, next(slots))
+    for k in range(1, levels):
+        for px, py in corners:
+            block = index(px, (z + levels - k) % levels, py, core)
+            got(block)
+            start(block, twin, next(slots))
+
+    blocks = half_width // LANES
+
+    def broad(i, carry):
+        there = (i + blocks - 1) % blocks
+        near = jnp.concatenate([tall_ref[0, i], tall_ref[1, i]], axis=1)
+        last = jnp.concatenate([tall_ref[0, there], tall_ref[1, there]], axis=1)
+        out = taps_dot(near, up_ref)
+        first = taps_dot(last, edge_ref)
+        at = pl.multiple_of(i * 2 * LANES, 2 * LANES)
+        smooth_ref[:, pl.ds(at, LANES)] = out[:, :LANES] + first
+        smooth_ref[:, pl.ds(pl.multiple_of(at + LANES, LANES), LANES)] = out[:, LANES:]
+        return carry
+
+    lax.fori_loop(0, blocks, broad, 0)
 
     for i in range(groups):
         bx, rest = i // (groups // 2), i % (groups // 2)
         got(bx * groups + rest * 2 + 1 - core)
-
-    def end_own(block, heading):
-        if heading == 0:
-            pl.when(has_up)(lambda: sent(block, up))
-            pl.when(has_down)(lambda: sent(block, down))
-        elif heading > 0:
-            pl.when(has_up)(lambda: sent(block, up))
-        else:
-            pl.when(has_down)(lambda: sent(block, down))
-        for way in (first, second, twin):
-            sent(block, way)
-
-    def end_first(block, heading):
-        for way in (second, twin):
-            sent(block, way)
-
-    def end_second(block, heading):
-        sent(block, twin)
-
-    lines = [
-        each_line(x, y, end_own),
-        each_line(fx, fy, end_first),
-        each_line(sx, sy, end_second),
-        each_line(dx, dy, end_second),
-    ]
-    for j in range(levels):
-        for at in lines:
-            at(j)
-
-
-def gather_all(block, cols, devices):
+    for copy in started:
+        copy.wait_send()
+
+
+def gather_all(kernels, weights, cols, coef, devices):
+    tiles = weights.shape[1] * 16
+    half_rows, half_width = coef.shape[1:]
+    matrix = synthesis_matrix(LANES)
+    near = matrix[:, :, 3:].transpose(1, 2, 0).reshape(2 * LANES, 2 * LANES)
+    edge = np.zeros((2, LANES, LANES))
+    edge[:, LANES - 3 :, :] = matrix[:LANES, :, :3].transpose(1, 2, 0)
+    copies = 3 * 4 + 7 + 12
     return pl.pallas_call(
         gather_kernel,
         out_shape=(
-            jax.ShapeDtypeStruct((devices,) + block.shape, block.dtype),
+            jax.ShapeDtypeStruct((devices, tiles, 2 * kernels.shape[1]), jnp.bfloat16),
             jax.ShapeDtypeStruct((devices,) + cols.shape, cols.dtype),
+            jax.ShapeDtypeStruct((2 * half_rows, 2 * half_width), jnp.float32),
         ),
-        in_specs=[whole] * 2,
-        out_specs=(whole, whole),
+        in_specs=[whole] * 6,
+        out_specs=(whole,) * 3,
         scratch_shapes=[
-            pltpu.SemaphoreType.DMA((5, devices)),
-            pltpu.SemaphoreType.DMA((5, devices)),
+            pltpu.VMEM((16, half_width), jnp.float32),
+            pltpu.VMEM((16, half_width), jnp.float32),
+            pltpu.VMEM((4, half_rows + 8, half_width), jnp.float32),
+            pltpu.VMEM((2, half_width // LANES, 2 * half_rows, LANES), jnp.float32),
+            pltpu.SemaphoreType.DMA((copies,)),
+            pltpu.SemaphoreType.DMA((copies,)),
             pltpu.SemaphoreType.DMA((devices,)),
             pltpu.SemaphoreType.DMA((devices,)),
+            pltpu.SemaphoreType.DMA((2,)),
         ],
-        compiler_params=pltpu.CompilerParams(collective_id=0, has_side_effects=True),
+        compiler_params=pltpu.CompilerParams(
+            collective_id=0, has_side_effects=True, vmem_limit_bytes=40 * 2**20
+        ),
         name="gather_all",
-    )(block, cols)
+    )(
+        kernels,
+        weights,
+        cols,
+        coef,
+        jnp.stack(table_pair(near)),
+        jnp.stack(table_pair(edge.reshape(2 * LANES, LANES))),
+    )
 
 
 def level(values):
@@ -996,10 +1033,11 @@
     vis_state = vis_dual[0, 0]
     columns_here = (tile_rows[0, 0] + lax.axis_index("band") * stripe).reshape(1, tiles)
     columns_here = jnp.concatenate([columns_here, columns_here], axis=1)
-    weights = (live_slots * vis_state).astype(jnp.bfloat16)
-    contrib = grid_back(kernel_here, weights).astype(jnp.bfloat16).reshape(tiles, 2 * piece)
-    blocks, cols = gather_all(contrib, columns_here, devices)
-    smooth = fast_synthesis(coef_dual)
+    weights = live_slots * vis_state
+    weights = jnp.stack([weights, jnp.stack([weights[:, :, 1], -weights[:, :, 0]], axis=2)])
+    weights = weights.reshape(2, tiles // 16, -1)
+    kernels = kernel_here.reshape(-1, piece)
+    blocks, cols, smooth = gather_all(kernels, weights, columns_here, coef_dual, devices)
     new_image, extrap, picked, units = image_step(
         blocks, cols, me, sky_image, smooth, groups, slots, piece
     )

time: 163 us -> 143 us (0.88)
  matrix products: 23.3 us -> 9.37 us
  Pallas kernels: 96.1 us -> 85.9 us
  local copies, waits for them, and re-layouts: 17.7 us -> 23.8 us
    dot_general x7 -> x0, matrix products: 9.89 us -> none  [the longest x1 3.53 us: fast_synthesis(): jnp.einsum('irj,rcjn->cin', f32(synthesis_matrix(half_rows)), joined, pre...]
    pallas_call x1, Pallas kernels: 36.7 us -> 28.4 us  [gather_all(): pl.pallas_call(gather_kernel, out_shape=(jax.ShapeDtypeStruct((devices, t...]
    unnamed x46 -> x44, local copies, waits for them, and re-layouts: 4.08 us -> 11.4 us
    pallas_call x1, Pallas kernels: 31.6 us -> 29.8 us  [exchange(): pl.pallas_call(exchange_kernel, out_shape=(jax.ShapeDtypeStruct((devices,...]
  transfers between devices with their start and end apart: 2 -> 1, of which waited for: 1 -> 1; matrix products, arithmetic and copies ran while one was open for 8% -> 4% of each run, Pallas kernels for 23% -> 0%
where the time goes in v1:
time: 143 us; the launch traced here: 142 us
  Pallas kernels  85.9 us (60%)
  local copies, waits for them, and re-layouts  23.8 us (17%)
  other arithmetic  13.4 us (9%)
  matrix products  9.37 us (7%)
  starting transfers between devices  5.06 us (4%)
  between operations  2.97 us (2%)
  waiting for transfers between devices  1.7 us (1%)
    pallas_call x1, Pallas kernels, exchange(): pl.pallas_call(exchange_kernel, out_shape=(jax.ShapeDtypeStruct((devices,...  29.8 us
    pallas_call x1, Pallas kernels, gather_all(): pl.pallas_call(gather_kernel, out_shape=(jax.ShapeDtypeStruct((devices, t...  28.4 us
    pallas_call x1, Pallas kernels, image_step(): pl.pallas_call(lambda *refs: image_kernel(low, *refs), out_shape=(jax.Sha...  23.2 us
    unnamed x44, local copies, waits for them, and re-layouts  11.4 us
    all_to_all x1, starting transfers between devices, to_all(): lax.all_to_all(flat, everywhere, split_axis=0, concat_axis=0, tiled=True)  5.06 us
    pallas_call x1, Pallas kernels, finish_tiles(): pl.pallas_call(lambda *refs: tile_kernel(devices, *refs), out_shape=jax.S...  4.5 us
    dot_general x2, matrix products, fast_analysis(): jnp.einsum('ij,jn->in', f32(analysis_matrix(rows_dev // 2)), extended, pr...  3.62 us
    min x1, other arithmetic, fast_local(): coef_dual = jnp.clip(coef_dual + coeffs, -threshold, threshold)  3.26 us
  transfers between devices with their start and end apart: 1, of which 1 were waited for; matrix products, arithmetic and copies ran while one was open for 4% of the time, Pallas kernels for 0%

profile of v1, /device:TPU:0, one launch (start us, length us, event | category | flops | bytes accessed | tf_op | source)
XLA Modules:
  0.0 142.2 jit_solution(3309141452166950917)
XLA Ops:
  1.6 0.7 fusion.26
  2.3 1.0 squeeze.28
  3.3 0.9 bitcast_multiply_fusion
  5.4 0.7 maximum_maximum_fusion.refs_2_
  6.1 1.6 %copy-done = f32[4,64,2048]{2,1,0:T(8,128)S(1)} copy-done((f32[4,64,2048]{2,1,0:T(8,128)S(1)}, f32[4,64,2048]{2,1,0:T(8,128)}, u32[]{:S(2)}) %copy-start) | copy-done | bytes 2097176
  7.7 1.6 %copy-done.2 = bf16[1,1,16,4,2,32,256]{6,5,4,3,2,1,0:T(8,128)(2,1)S(1)} copy-done((bf16[1,1,16,4,2,32,256]{6,5,4,3,2,1,0:T(8,128)(2,1)S(1)}, bf16[1,1,16,4,2,32,256]{6,5,4,3,2,1,0:T(8,128)(2,1)}, u32[]{:S(2)}) %copy-start.2) | copy-done | bytes 2097176
  9.3 0.9 copy-done.9
  10.2 0.9 copy-done.10
  11.1 28.4 %gather_all.1 = (bf16[32,64,512]{2,1,0:T(8,128)(2,1)S(1)}, s32[32,1,128]{2,1,0:T(1,128)S(1)}, f32[128,4096]{1,0:T(8,128)S(1)}) custom-call(bf16[4096,256]{1,0:T(8,128)(2,1)S(1)} %bitcast.66, f32[2,4,1024]{2,1,0:T(4,128)S(1)} %pad_maximum_fusion.3.weights_ref, s32[1,128]{1,0:T(1,128)S(1)} %pad_add_fusion.cols_ref, f32[4,64,2048]{2,1,0:T(8,128)S(1)} %copy-done, ...), custom_call_target="tpu_custom_call" | custom-call | tf_op jit(solution)/shard_map/gather_all/pallas_call | solution.py:602
  39.5 1.3 copy-done.4
  40.8 1.3 copy-done.5
  42.8 23.2 %image_step.1 = (f32[128,4096]{1,0:T(8,128)}, f32[128,4096]{1,0:T(8,128)}, s32[2048,128]{1,0:T(8,128)}, f32[16,1,128]{2,1,0:T(1,128)}) custom-call(bf16[2048,512]{1,0:T(8,128)(2,1)} %bitcast.71, s32[32,1,128]{2,1,0:T(1,128)} %copy-done.12, bf16[256,512]{1,0:T(8,128)(2,1)} %maximum_maximum_fusion.refs_2_, f32[2,128,128]{2,1,0:T(8,128)} %constant.75.clone.refs_3_, ...), custom_call_target="tpu_custom_call" | custom-call | tf_op jit(solution)/shard_map/image_step/pallas_call | solution.py:800
  66.0 1.6 %slice.46.top_ref = f32[8,4096]{1,0:T(8,128)} slice(f32[128,4096]{1,0:T(8,128)} %get-tuple-element.17), slice={[0:8], [0:4096]} | slice | bytes 262144 | tf_op jit(solution)/shard_map/slice | solution.py:902
  67.6 29.8 %exchange.1 = (s32[32,64,128]{2,1,0:T(8,128)}, f32[32,1,128]{2,1,0:T(1,128)}, f32[8,4096]{1,0:T(8,128)}) custom-call(s32[2048,128]{1,0:T(8,128)} %get-tuple-element.18.picked_ref, f32[16,1,128]{2,1,0:T(1,128)} %get-tuple-element.19.unit_ref, f32[8,4096]{1,0:T(8,128)} %slice.46.top_ref), custom_call_target="tpu_custom_call" | custom-call | tf_op jit(solution)/shard_map/exchange/pallas_call | solution.py:903
  97.4 1.2 copy-done.6
  98.6 0.7 copy-done.13
  99.3 4.5 %finish_tiles.1 = f32[64,512]{1,0:T(8,128)S(1)} custom-call(s32[32,64,128]{2,1,0:T(8,128)S(1)} %copy-done.6, f32[32,1,128]{2,1,0:T(1,128)S(1)} %copy-done.13, f32[2,64,128]{2,1,0:T(8,128)S(1)} %copy-done.11, bf16[2,2,256,256]{3,2,1,0:T(8,128)(2,1)S(1)} %copy-done.8, bf16[512,512]{1,0:T(8,128)(2,1)S(1)} %copy-done.7), custom_call_target="tpu_custom_call" | custom-call | tf_op jit(solution)/shard_map/finish_tiles/pallas_call | solution.py:999
  106.0 1.8 %fusion.31 = f32[4096,128]{1,0:T(8,128)S(1)} fusion(f32[128,4096]{1,0:T(8,128)S(1)} %copy-done.14, f32[128,128]{1,0:T(8,128)S(1)} %copy-done.20), kind=kOutput, calls=%fused_computation.59 | convolution fusion | flops 402653184 | bytes 4259840 | tf_op jit(solution)/shard_map/ij,jn->in/dot_general | solution.py:320
  107.8 1.8 %convolution_add_fusion = f32[4096,128]{1,0:T(8,128)S(1)} fusion(f32[4096,128]{1,0:T(8,128)S(1)} %fusion.31, f32[128,6]{1,0:T(8,128)S(1)} %copy-done.19, f32[8,4096]{1,0:T(8,128)S(1)} %copy-done.18), kind=kOutput, calls=%fused_computation | convolution fusion | flops 19398656 | bytes 4328448 | tf_op jit(solution)/shard_map/ij,jn->in/dot_general | solution.py:320
  109.9 0.7 copy-done.16
  110.6 1.8 %fusion.32 = f32[128,16,256]{2,0,1:T(8,128)S(1)} fusion(f32[128,16,256]{0,2,1:T(8,128)S(1)} %bitcast.75, f32[256,256,1]{1,0,2:T(8,128)S(1)} %copy-done.16), kind=kOutput, calls=%fused_computation.60 | convolution fusion | flops 805306368 | bytes 4456448 | tf_op jit(solution)/shard_map/rbi,ji->rbj/dot_general | solution.py:325
  112.5 2.4 %convolution_add_fusion.1 = f32[128,16,256]{2,0,1:T(8,128)} fusion(f32[128,16,256]{2,0,1:T(8,128)S(1)} %fusion.32, f32[256,6,1]{0,1,2:T(8,128)S(1)} %copy-done.21, f32[128,1,256]{0,2,1:T(8,128)S(1)} %slice.63, f32[128,15,256]{0,2,1:T(8,128)S(1)} %slice.62), kind=kOutput, calls=%fused_computation.3 | convolution fusion | flops 19410944 | bytes 6297600 | tf_op jit(solution)/shard_map/rbi,ji->rbj/dot_general | solution.py:326
  114.9 2.3 %reshape.111 = f32[2,64,16,2,128]{4,3,1,0,2:T(2,128)S(1)} reshape(f32[128,16,256]{2,0,1:T(8,128)} %convolution_add_fusion.1) | data formatting | bytes 4194304 | tf_op jit(solution)/shard_map/reshape | solution.py:327
  117.2 2.8 %abs_reduce_fusion = f32[]{:T(128)} fusion(f32[2,64,16,2,128]{4,3,1,0,2:T(2,128)S(1)} %reshape.111), kind=kLoop, calls=%fused_computation.2 | loop fusion | flops 1048575 | bytes 2097156 | tf_op jit(solution)/shard_map/reduce_sum | solution.py:1052
  120.0 0.7 fusion.21
  120.7 2.0 %pad_maximum_fusion.4 = f32[3]{0:T(128)S(1)} fusion(f32[1]{0:T(128)} %bitcast.30, f32[1]{0:T(128)} %bitcast.29, f32[1]{0:T(128)} %bitcast.10), kind=kLoop, calls=%fused_computation.53 | loop fusion | flops 6 | bytes 24 | tf_op jit(solution)/shard_map/stack | solution.py:1050
  123.3 5.1 %all-to-all-start = ((f32[32,1,3]{2,1,0:T(1,128)}), f32[32,1,3]{2,1,0:T(1,128)S(1)}, u32[]{:S(2)}, u32[]{:S(2)}) async-start(f32[32,1,3]{2,1,0:T(1,128)} %broadcast_in_dim.2), calls=%async_computation | async-start | bytes 32768 | tf_op jit(solution)/shard_map/all_to_all | solution.py:1015
  128.4 2.5 %copy.75 = f32[2,2,64,16,128]{4,3,2,1,0:T(8,128)} copy(f32[2,2,64,16,128]{4,1,2,0,3:T(2,128)S(1)} %bitcast.72) | data formatting | bytes 4194304 | tf_op jit(solution)/shard_map/transpose | solution.py:328
  130.9 2.9 %reshape.113 = f32[4,64,2048]{2,1,0:T(8,128)} reshape(f32[2,2,64,16,128]{4,3,2,1,0:T(8,128)} %copy.75) | data formatting | bytes 4194304 | tf_op jit(solution)/shard_map/reshape | solution.py:328
  133.8 1.7 %all-to-all-done = f32[32,1,3]{2,1,0:T(1,128)S(1)} async-done(((f32[32,1,3]{2,1,0:T(1,128)}), f32[32,1,3]{2,1,0:T(1,128)S(1)}, u32[]{:S(2)}, u32[]{:S(2)}) %all-to-all-start) | async-done | bytes 416 | tf_op jit(solution)/shard_map/all_to_all | solution.py:1015
  138.2 3.3 %maximum_minimum_fusion = f32[4,64,2048]{2,1,0:T(8,128)} fusion(f32[4,64,2048]{2,1,0:T(8,128)S(1)} %copy-done.1, f32[4,64,2048]{2,1,0:T(8,128)} %reshape.113, f32[]{:T(128)S(6)} %neg.12, f32[]{:T(128)} %bitcast.31), kind=kLoop, calls=%fused_computation.1 | loop fusion | flops 1572864 | bytes 6291464 | tf_op jit(solution)/shard_map/jit(clip)/min | solution.py:1059
  141.4 0.8 fusion.18
  (64 shorter events, 6.3 us)
Async XLA Ops:
  6.1 1.6 %copy-start = (f32[4,64,2048]{2,1,0:T(8,128)S(1)}, f32[4,64,2048]{2,1,0:T(8,128)}, u32[]{:S(2)}) copy-start(f32[4,64,2048]{2,1,0:T(8,128)} %coef_ref.1) | copy-start | bytes 6291460
  7.7 1.6 %copy-start.2 = (bf16[1,1,16,4,2,32,256]{6,5,4,3,2,1,0:T(8,128)(2,1)S(1)}, bf16[1,1,16,4,2,32,256]{6,5,4,3,2,1,0:T(8,128)(2,1)}, u32[]{:S(2)}) copy-start(bf16[1,1,16,4,2,32,256]{6,5,4,3,2,1,0:T(8,128)(2,1)} %param.28) | copy-start | bytes 6291460
  9.3 0.9 copy-start.9
  10.2 0.9 copy-start.10
  39.5 1.3 copy-start.4
  40.8 1.3 copy-start.5
  42.2 0.6 copy-start.12
  42.8 54.6 %copy-start.7 = (bf16[512,512]{1,0:T(8,128)(2,1)S(1)}, bf16[512,512]{1,0:T(8,128)(2,1)}, u32[]{:S(2)}) copy-start(bf16[512,512]{1,0:T(8,128)(2,1)} %constant.121.refs_4_) | copy-start | bytes 1572868
  42.8 54.6 %copy-start.8 = (bf16[2,2,256,256]{3,2,1,0:T(8,128)(2,1)S(1)}, bf16[2,2,256,256]{3,2,1,0:T(8,128)(2,1)}, u32[]{:S(2)}) copy-start(bf16[2,2,256,256]{3,2,1,0:T(8,128)(2,1)} %constant.120.refs_3_) | copy-start | bytes 1572868
  42.8 54.6 %copy-start.11 = (f32[2,64,128]{2,1,0:T(8,128)S(1)}, f32[2,64,128]{2,1,0:T(8,128)}, u32[]{:S(2)}) copy-start(f32[2,64,128]{2,1,0:T(8,128)} %constant.79.clone.refs_2_) | copy-start | bytes 196612
  67.6 36.4 %copy-start.3 = (bf16[1,1,16,4,2,32,256]{6,5,4,3,2,1,0:T(8,128)(2,1)S(1)}, bf16[1,1,16,4,2,32,256]{6,5,4,3,2,1,0:T(8,128)(2,1)}, u32[]{:S(2)}) copy-start(bf16[1,1,16,4,2,32,256]{6,5,4,3,2,1,0:T(8,128)(2,1)} %param.28) | copy-start | bytes 6291460
  97.4 1.2 copy-start.6
  98.6 0.7 copy-start.13
  104.4 1.6 %copy-start.14 = (f32[128,4096]{1,0:T(8,128)S(1)}, f32[128,4096]{1,0:T(8,128)}, u32[]{:S(2)}) copy-start(f32[128,4096]{1,0:T(8,128)} %get-tuple-element.17) | copy-start | bytes 6291460
  104.4 1.6 %copy-start.20 = (f32[128,128]{1,0:T(8,128)S(1)}, f32[128,128]{1,0:T(8,128)}, u32[]{:S(2)}) copy-start(f32[128,128]{1,0:T(8,128)} %constant.112) | copy-start | bytes 196612
  106.0 1.8 %copy-start.18 = (f32[8,4096]{1,0:T(8,128)S(1)}, f32[8,4096]{1,0:T(8,128)}, u32[]{:S(2)}) copy-start(f32[8,4096]{1,0:T(8,128)} %get-tuple-element.20) | copy-start | bytes 393220
  106.0 1.8 %copy-start.19 = (f32[128,6]{1,0:T(8,128)S(1)}, f32[128,6]{1,0:T(8,128)}, u32[]{:S(2)}) copy-start(f32[128,6]{1,0:T(8,128)} %constant.113) | copy-start | bytes 9220
  109.7 1.0 copy-start.16
  110.6 1.8 %copy-start.21 = (f32[256,6,1]{0,1,2:T(8,128)S(1)}, f32[256,6,1]{0,1,2:T(8,128)}, u32[]{:S(2)}) copy-start(f32[256,6,1]{0,1,2:T(8,128)} %constant.125) | copy-start | bytes 18436
  117.2 2.8 %copy-start.15 = (f32[1,1,16,4,2,32]{5,4,3,2,1,0:T(2,128)S(1)}, f32[1,1,16,4,2,32]{5,4,3,2,1,0:T(2,128)}, u32[]{:S(2)}) copy-start(f32[1,1,16,4,2,32]{5,4,3,2,1,0:T(2,128)} %param.26) | copy-start | bytes 49156
  117.2 2.8 %copy-start.17 = (f32[1,1,16,4,2,32]{5,4,3,2,1,0:T(2,128)S(1)}, f32[1,1,16,4,2,32]{5,4,3,2,1,0:T(2,128)}, u32[]{:S(2)}) copy-start(f32[1,1,16,4,2,32]{5,4,3,2,1,0:T(2,128)} %param.27) | copy-start | bytes 49156
  123.3 12.2 %all-to-all-start = ((f32[32,1,3]{2,1,0:T(1,128)}), f32[32,1,3]{2,1,0:T(1,128)S(1)}, u32[]{:S(2)}, u32[]{:S(2)}) async-start(f32[32,1,3]{2,1,0:T(1,128)} %broadcast_in_dim.2), calls=%async_computation | async-start | bytes 32768 | tf_op jit(solution)/shard_map/all_to_all | solution.py:1015
  130.9 7.2 %copy-start.1 = (f32[4,64,2048]{2,1,0:T(8,128)S(1)}, f32[4,64,2048]{2,1,0:T(8,128)}, u32[]{:S(2)}) copy-start(f32[4,64,2048]{2,1,0:T(8,128)} %coef_ref.1) | copy-start | bytes 6291460

commit v2 on v1

--- a/solution.py
+++ b/solution.py
@@ -314,35 +314,6 @@
     return matrix
 
 
-def fast_analysis(extrap, halo):
-    rows_dev, width = extrap.shape
-    extended = jnp.concatenate([extrap, halo], axis=0)
-    by_rows = jnp.einsum("ij,jn->in", f32(analysis_matrix(rows_dev // 2)), extended, precision=high)
-    size = 256
-    blocks = by_rows.reshape(rows_dev, width // size, size)
-    following = jnp.roll(blocks, -1, axis=1)[:, :, :6]
-    matrix = analysis_matrix(size // 2)
-    out = jnp.einsum("rbi,ji->rbj", blocks, f32(matrix[:, :size]), precision=high)
-    out = out + jnp.einsum("rbi,ji->rbj", following, f32(matrix[:, size:]), precision=high)
-    out = out.reshape(2, rows_dev // 2, width // size, 2, size // 2)
-    return jnp.transpose(out, (0, 3, 1, 2, 4)).reshape(4, rows_dev // 2, width // 2)
-
-
-def fast_synthesis(coef_dual):
-    half_rows, half_width = coef_dual.shape[1:]
-    halo = shifted(coef_dual[:, half_rows - 3 :, :], everywhere, 1)
-    joined = jnp.concatenate([halo, coef_dual], axis=1)
-    joined = joined.reshape(2, 2, half_rows + 3, half_width)
-    by_rows = jnp.einsum("irj,rcjn->cin", f32(synthesis_matrix(half_rows)), joined, precision=high)
-    size = 128
-    blocks = by_rows.reshape(2, 2 * half_rows, half_width // size, size)
-    before = jnp.roll(blocks, 1, axis=2)[:, :, :, size - 3 :]
-    matrix = synthesis_matrix(size)
-    out = jnp.einsum("cibk,nck->ibn", blocks, f32(matrix[:, :, 3:]), precision=high)
-    out = out + jnp.einsum("cibk,nck->ibn", before, f32(matrix[:, :, :3]), precision=high)
-    return out.reshape(2 * half_rows, 2 * half_width)
-
-
 def cos_sums(values, size):
     half = size // 2
     if half < 2:
@@ -427,36 +398,106 @@
     return nn_dot(upper, tables[0]) + nn_dot(lower, tables[0]) + nn_dot(upper, tables[1])
 
 
-def gather_kernel(
-    kernels_ref,
+def level(values):
+    return jnp.round(values).astype(jnp.int32)
+
+
+def step_kernel(
+    low,
+    kernels_hbm,
+    coef_hbm,
+    sky_hbm,
+    up_hbm,
+    edge_hbm,
+    turn_hbm,
+    inv_hbm,
+    fwd_hbm,
+    near_hbm,
+    next_hbm,
+    last_hbm,
+    order_hbm,
     weights_ref,
     cols_ref,
-    coef_ref,
+    vis_ref,
+    phase_ref,
+    shift_ref,
+    tw_ref,
+    image_hbm,
+    merged_ref,
+    residual_ref,
+    sums_ref,
+    kernels_ref,
+    joined_ref,
+    sky_ref,
     up_ref,
     edge_ref,
-    out_ref,
-    all_cols_ref,
-    smooth_ref,
+    turn_ref,
+    inv_ref,
+    fwd_ref,
+    near_ref,
+    next_ref,
+    last_ref,
+    order_ref,
+    load_sem,
     tail_ref,
     halo_ref,
-    joined_ref,
+    block_ref,
+    all_cols_ref,
     tall_ref,
+    smooth_ref,
+    fold_ref,
+    grid_ref,
+    hot_ref,
+    half_ref,
+    spec_ref,
+    rest_ref,
+    extrap_ref,
+    picked_ref,
+    unit_ref,
+    got_ref,
+    units_ref,
+    mid_ref,
+    column_ref,
+    all_sums_ref,
     send_a,
     send_b,
     recv_a,
     recv_b,
+    send_p,
+    send_u,
+    recv_p,
+    recv_u,
+    send_s,
+    recv_s,
     halo_sem,
 ):
     x, z, y, core, groups = place()
     levels = groups // 4
     devices = 2 * groups
-    half_rows, half_width = coef_ref.shape[1:]
+    half_rows, half_width = coef_hbm.shape[1:]
+    rows = 2 * half_rows
+    tiles = block_ref.shape[1]
+    kept = low // 2 + 1
+    wide = LANES
 
     def index(px, pz, py, pc):
         return px * groups + pz * 4 + py * 2 + pc
 
     def device(px, pz, py, pc):
         return (px, pz * 4 + py * 2 + pc)
+
+    def ident(number):
+        return (number // groups, number % groups)
+
+    def remote(src, dst, send, recv, target):
+        return pltpu.make_async_remote_copy(
+            src_ref=src,
+            dst_ref=dst,
+            send_sem=send,
+            recv_sem=recv,
+            device_id=target,
+            device_id_type=MESH,
+        )
 
     me = index(x, z, y, core)
     after, before = (me + 1) % devices, (me + devices - 1) % devices
@@ -464,54 +505,60 @@
     line = [device(x, (z + k) % levels, y, core) for k in range(1, levels)]
     corners = [(1 - x, y), (x, 1 - y), (1 - x, 1 - y)]
     plane = [device(px, z, py, core) for px, py in corners]
-    follower = (after // groups, after % groups)
-    leader = (before // groups, before % groups)
     barrier = pltpu.get_barrier_semaphore()
-    peers = line + plane + [twin, follower, leader]
+    peers = line + plane + [twin, ident(after), ident(before)]
     for peer in peers:
         pl.semaphore_signal(barrier, inc=1, device_id=peer, device_id_type=MESH)
 
-    for c in range(4):
-        tail_ref[3 * c : 3 * c + 3, :] = coef_ref[c, half_rows - 3 :, :]
+    sources = [
+        (kernels_hbm, kernels_ref),
+        (coef_hbm, joined_ref.at[:, pl.ds(8, half_rows), :]),
+        (up_hbm, up_ref),
+        (edge_hbm, edge_ref),
+        (turn_hbm, turn_ref),
+        (inv_hbm, inv_ref),
+        (sky_hbm, sky_ref),
+        (fwd_hbm, fwd_ref),
+        (near_hbm, near_ref),
+        (next_hbm, next_ref),
+        (last_hbm, last_ref),
+        (order_hbm, order_ref),
+    ]
+    loads = [
+        pltpu.make_async_copy(src, dst, load_sem.at[i]) for i, (src, dst) in enumerate(sources)
+    ]
+    for load in loads:
+        load.start()
+    loads[0].wait()
     count = 16
-    span = kernels_ref.shape[0] * count // out_ref.shape[1]
+    span = kernels_ref.shape[0] * count // tiles
     lane = lax.broadcasted_iota(jnp.int32, (count, span), 1) // (span // count)
     mine = lane == lax.broadcasted_iota(jnp.int32, (count, span), 0)
-    for i in range(out_ref.shape[1] // count):
+    for i in range(tiles // count):
         spread = [jnp.where(mine, weights_ref[part, i : i + 1, :], 0.0) for part in range(2)]
         spread = jnp.concatenate(spread, axis=0).astype(jnp.bfloat16)
         both = nn_dot(spread, kernels_ref[i * span : (i + 1) * span, :])
         both = jnp.concatenate([both[:count], both[count:]], axis=1)
-        out_ref[me, i * count : (i + 1) * count, :] = both.astype(jnp.bfloat16)
+        block_ref[me, i * count : (i + 1) * count, :] = both.astype(jnp.bfloat16)
     all_cols_ref[me] = cols_ref[...]
+    loads[1].wait()
+    for c in range(4):
+        tail_ref[3 * c : 3 * c + 3, :] = joined_ref[c, half_rows + 5 :, :]
     pl.semaphore_wait(barrier, len(peers))
 
     started = []
 
     def start(block, target, slot):
-        own_a, own_b = out_ref.at[block], all_cols_ref.at[block]
+        own_a, own_b = block_ref.at[block], all_cols_ref.at[block]
         for own, send, recv in ((own_a, send_a, recv_a), (own_b, send_b, recv_b)):
-            copy = pltpu.make_async_remote_copy(
-                src_ref=own,
-                dst_ref=own,
-                send_sem=send.at[slot],
-                recv_sem=recv.at[block],
-                device_id=target,
-                device_id_type=MESH,
-            )
+            copy = remote(own, own, send.at[slot], recv.at[block], target)
             copy.start()
             started.append(copy)
 
     def got(block):
-        for ref, send, recv in ((out_ref, send_a, recv_a), (all_cols_ref, send_b, recv_b)):
-            pltpu.make_async_remote_copy(
-                src_ref=ref.at[block],
-                dst_ref=ref.at[block],
-                send_sem=send.at[0],
-                recv_sem=recv.at[block],
-                device_id=twin,
-                device_id_type=MESH,
-            ).wait_recv()
+        for ref, send, recv in ((block_ref, send_a, recv_a), (all_cols_ref, send_b, recv_b)):
+            own = ref.at[block]
+            remote(own, own, send.at[0], recv.at[block], twin).wait_recv()
 
     slots = iter(range(send_a.shape[0]))
     far = sorted(range(1, levels), key=lambda k: abs(k - levels / 2))
@@ -519,19 +566,9 @@
         start(me, line[k - 1], next(slots))
     for target in plane:
         start(me, target, next(slots))
-    edge = pltpu.make_async_remote_copy(
-        src_ref=tail_ref,
-        dst_ref=halo_ref,
-        send_sem=halo_sem.at[0],
-        recv_sem=halo_sem.at[1],
-        device_id=follower,
-        device_id_type=MESH,
-    )
+    edge = remote(tail_ref, halo_ref, halo_sem.at[0], halo_sem.at[1], ident(after))
     edge.start()
     start(me, twin, next(slots))
-
-    for c in range(4):
-        joined_ref[c, 8:, :] = coef_ref[c]
     edge.wait()
     for c in range(4):
         joined_ref[c, 5:8, :] = halo_ref[3 * c : 3 * c + 3, :]
@@ -542,22 +579,23 @@
         for target in plane:
             start(block, target, next(slots))
         start(block, twin, next(slots))
+    strips = half_width // LANES
 
     def tall(i, carry):
         here = pl.ds(pl.multiple_of(i * LANES, LANES), LANES)
         for c in range(2):
             for k in range(half_rows // 8):
-                low = [joined_ref[c, 8 + 8 * k - d : 16 + 8 * k - d, here] for d in range(4)]
-                high = [joined_ref[c + 2, 8 + 8 * k - d : 16 + 8 * k - d, here] for d in range(4)]
+                lows = [joined_ref[c, 8 + 8 * k - d : 16 + 8 * k - d, here] for d in range(4)]
+                highs = [joined_ref[c + 2, 8 + 8 * k - d : 16 + 8 * k - d, here] for d in range(4)]
                 for parity in range(2):
                     total = 0.0
                     for d in range(4):
-                        total = total + low_taps[parity + 2 * d] * low[d]
-                        total = total + high_taps[parity + 2 * d] * high[d]
-                    tall_ref[c, i, pl.ds(16 * k + parity, 8, stride=2), :] = total
+                        total = total + low_taps[parity + 2 * d] * lows[d]
+                        total = total + high_taps[parity + 2 * d] * highs[d]
+                    tall_ref[c * strips + i, pl.ds(16 * k + parity, 8, stride=2), :] = total
         return carry
 
-    lax.fori_loop(0, half_width // LANES, tall, 0)
+    lax.fori_loop(0, strips, tall, 0)
 
     for px, py in corners:
         block = index(px, z, py, core)
@@ -568,104 +606,31 @@
             block = index(px, (z + levels - k) % levels, py, core)
             got(block)
             start(block, twin, next(slots))
-
-    blocks = half_width // LANES
+    loads[2].wait()
+    loads[3].wait()
 
     def broad(i, carry):
-        there = (i + blocks - 1) % blocks
-        near = jnp.concatenate([tall_ref[0, i], tall_ref[1, i]], axis=1)
-        last = jnp.concatenate([tall_ref[0, there], tall_ref[1, there]], axis=1)
+        there = (i + strips - 1) % strips
+        near = jnp.concatenate([tall_ref[i], tall_ref[strips + i]], axis=1)
+        last = jnp.concatenate([tall_ref[there], tall_ref[strips + there]], axis=1)
         out = taps_dot(near, up_ref)
         first = taps_dot(last, edge_ref)
-        at = pl.multiple_of(i * 2 * LANES, 2 * LANES)
-        smooth_ref[:, pl.ds(at, LANES)] = out[:, :LANES] + first
-        smooth_ref[:, pl.ds(pl.multiple_of(at + LANES, LANES), LANES)] = out[:, LANES:]
+        smooth_ref[2 * i] = out[:, :LANES] + first
+        smooth_ref[2 * i + 1] = out[:, LANES:]
         return carry
 
-    lax.fori_loop(0, blocks, broad, 0)
+    lax.fori_loop(0, strips, broad, 0)
+    loads[4].wait()
+    loads[5].wait()
 
     for i in range(groups):
         bx, rest = i // (groups // 2), i % (groups // 2)
         got(bx * groups + rest * 2 + 1 - core)
-    for copy in started:
-        copy.wait_send()
-
-
-def gather_all(kernels, weights, cols, coef, devices):
-    tiles = weights.shape[1] * 16
-    half_rows, half_width = coef.shape[1:]
-    matrix = synthesis_matrix(LANES)
-    near = matrix[:, :, 3:].transpose(1, 2, 0).reshape(2 * LANES, 2 * LANES)
-    edge = np.zeros((2, LANES, LANES))
-    edge[:, LANES - 3 :, :] = matrix[:LANES, :, :3].transpose(1, 2, 0)
-    copies = 3 * 4 + 7 + 12
-    return pl.pallas_call(
-        gather_kernel,
-        out_shape=(
-            jax.ShapeDtypeStruct((devices, tiles, 2 * kernels.shape[1]), jnp.bfloat16),
-            jax.ShapeDtypeStruct((devices,) + cols.shape, cols.dtype),
-            jax.ShapeDtypeStruct((2 * half_rows, 2 * half_width), jnp.float32),
-        ),
-        in_specs=[whole] * 6,
-        out_specs=(whole,) * 3,
-        scratch_shapes=[
-            pltpu.VMEM((16, half_width), jnp.float32),
-            pltpu.VMEM((16, half_width), jnp.float32),
-            pltpu.VMEM((4, half_rows + 8, half_width), jnp.float32),
-            pltpu.VMEM((2, half_width // LANES, 2 * half_rows, LANES), jnp.float32),
-            pltpu.SemaphoreType.DMA((copies,)),
-            pltpu.SemaphoreType.DMA((copies,)),
-            pltpu.SemaphoreType.DMA((devices,)),
-            pltpu.SemaphoreType.DMA((devices,)),
-            pltpu.SemaphoreType.DMA((2,)),
-        ],
-        compiler_params=pltpu.CompilerParams(
-            collective_id=0, has_side_effects=True, vmem_limit_bytes=40 * 2**20
-        ),
-        name="gather_all",
-    )(
-        kernels,
-        weights,
-        cols,
-        coef,
-        jnp.stack(table_pair(near)),
-        jnp.stack(table_pair(edge.reshape(2 * LANES, LANES))),
-    )
-
-
-def level(values):
-    return jnp.round(values).astype(jnp.int32)
-
-
-def image_kernel(
-    low,
-    block_ref,
-    cols_ref,
-    turn_ref,
-    phase_ref,
-    inv_ref,
-    tw_ref,
-    fwd_ref,
-    sky_ref,
-    smooth_ref,
-    image_ref,
-    extrap_ref,
-    picked_ref,
-    unit_ref,
-    fold_ref,
-    grid_ref,
-    hot_ref,
-    half_ref,
-    spec_ref,
-    rest_ref,
-):
-    rows = sky_ref.shape[0]
-    tiles = block_ref.shape[0]
-    kept = low // 2 + 1
-    wide = LANES
+
+    total_tiles = devices * tiles
     lane = lax.broadcasted_iota(jnp.int32, (1, LANES), 1)
-    for i in range(tiles // LANES):
-        columns = jnp.where(lane < LANES // 2, cols_ref[2 * i], cols_ref[2 * i + 1])
+    for i in range(devices // 2):
+        columns = jnp.where(lane < tiles, all_cols_ref[2 * i], all_cols_ref[2 * i + 1])
         k1 = columns % low
         k2 = columns // low
         flip = k1 >= kept
@@ -674,8 +639,9 @@
         fold_ref[0, i : i + 1, :] = (k1 * wide + k2).astype(jnp.float32)
         fold_ref[1, i : i + 1, :] = jnp.where(flip, -1.0, 1.0)
     chunk = 512
-    for j in range(tiles // chunk):
-        both = nt_dot(turn_ref[...], block_ref[j * chunk : (j + 1) * chunk, :])
+    for j in range(total_tiles // chunk):
+        some = block_ref[j * chunk // tiles : (j + 1) * chunk // tiles]
+        both = nt_dot(turn_ref[...], some.reshape(chunk, -1))
         for i in range(chunk // LANES):
             b = j * (chunk // LANES) + i
             real = both[:rows, i * LANES : (i + 1) * LANES]
@@ -688,17 +654,15 @@
     def scatter(p, carry):
         base = pl.multiple_of(p * 2 * wide, 2 * wide)
         row = (lax.broadcasted_iota(jnp.int32, (2 * wide, LANES), 0) + base).astype(jnp.float32)
-        for i in range(tiles // LANES):
+        for i in range(total_tiles // LANES):
             hit = row == fold_ref[0, i : i + 1, :]
             hot_ref[pl.ds(base, 2 * wide), i * LANES : (i + 1) * LANES] = jnp.where(
                 hit, 1.0, 0.0
             ).astype(jnp.bfloat16)
         folded = nt_dot(grid_ref[...], hot_ref[pl.ds(base, 2 * wide), :]).astype(jnp.bfloat16)
         for e in range(2):
-            pair = jnp.concatenate(
-                [folded[:rows, e * wide : (e + 1) * wide], folded[rows:, e * wide : (e + 1) * wide]],
-                axis=1,
-            )
+            here = slice(e * wide, (e + 1) * wide)
+            pair = jnp.concatenate([folded[:rows, here], folded[rows:, here]], axis=1)
             mid = nn_dot(pair, inv_ref[...])
             k1 = p * 2 + e
             tw_real, tw_imag = tw_ref[0, pl.ds(k1, 1), :], tw_ref[1, pl.ds(k1, 1), :]
@@ -708,6 +672,7 @@
         return carry
 
     lax.fori_loop(0, (kept + 1) // 2, scatter, 0)
+    loads[6].wait()
 
     def strip(i, carry):
         at = pl.ds(pl.multiple_of(i * 8, 8), 8)
@@ -724,10 +689,10 @@
                 adjoint = cos_part[k] + sin_part[k]
             here = slice(a * wide, (a + 1) * wide)
             sky = sky_ref[at, here]
-            image = jnp.maximum(sky - smooth_ref[at, here] - adjoint, 0.0)
+            image = jnp.maximum(sky - smooth_ref[a, at, :] - adjoint, 0.0)
             extrap = 2.0 * image - sky
-            image_ref[at, here] = image
-            extrap_ref[at, here] = extrap
+            sky_ref[at, here] = image
+            extrap_ref[a, at, :] = extrap
             extraps.append(extrap)
         even, odd = even_odd(extraps)
         real_part = cos_sums(even, low)
@@ -744,25 +709,57 @@
         return carry
 
     lax.fori_loop(0, rows // 8, strip, 0)
-
-    for k in range(kept):
-        upper, lower = split(half_ref[k])
-        out = nn_dot(upper, fwd_ref[0]) + nn_dot(lower, fwd_ref[0]) + nn_dot(upper, fwd_ref[1])
-        here = slice(k * wide, (k + 1) * wide)
+    store = pltpu.make_async_copy(sky_ref, image_hbm, load_sem.at[len(loads)])
+    store.start()
+    top = remote(
+        extrap_ref.at[:, pl.ds(0, 8), :],
+        extrap_ref.at[:, pl.ds(rows, 8), :],
+        halo_sem.at[2],
+        halo_sem.at[3],
+        ident(before),
+    )
+    top.start()
+    loads[7].wait()
+
+    def spectrum(k, carry):
+        out = taps_dot(half_ref[k], fwd_ref)
+        here = pl.ds(pl.multiple_of(k * wide, wide), wide)
         upper, lower = split(out)
         spec_ref[:rows, here] = upper[:, :wide]
         spec_ref[rows:, here] = upper[:, wide:]
         rest_ref[:rows, here] = lower[:, :wide]
         rest_ref[rows:, here] = lower[:, wide:]
-
-    def pick(j, carry):
+        return carry
+
+    lax.fori_loop(0, kept, spectrum, 0)
+
+    def sends(to):
+        at = pl.ds(pl.multiple_of(to * tiles, tiles), tiles)
+        return [
+            remote(picked_ref.at[at, :], got_ref.at[me], send_p.at[to], recv_p.at[me], ident(to)),
+            remote(unit_ref.at[to // 2], units_ref.at[me], send_u.at[to], recv_u.at[me], ident(to)),
+        ]
+
+    def arrivals(origin):
+        at = pl.ds(0, tiles)
+        return [
+            remote(
+                picked_ref.at[at, :], got_ref.at[origin], send_p.at[0], recv_p.at[origin], twin
+            ),
+            remote(unit_ref.at[0], units_ref.at[origin], send_u.at[0], recv_u.at[origin], twin),
+        ]
+
+    def pick(s, carry):
+        half = levels // 2
+        to_z = (z // half + 1 + s // levels) % 2 * half + s // 2 % half
+        j = (x + 1 + s) % 2 * levels + to_z
         at = pl.multiple_of(j * 2 * LANES, 2 * LANES)
         hot = hot_ref[: kept * wide, pl.ds(at, 2 * LANES)]
-        got = nn_dot(spec_ref[...], hot) + nn_dot(rest_ref[...], hot)
+        both = nn_dot(spec_ref[...], hot) + nn_dot(rest_ref[...], hot)
         for h in range(2):
             sign = fold_ref[1, pl.ds(2 * j + h, 1), :]
-            real = got[:rows, h * LANES : (h + 1) * LANES]
-            imag = got[rows:, h * LANES : (h + 1) * LANES] * sign
+            real = both[:rows, h * LANES : (h + 1) * LANES]
+            imag = both[rows:, h * LANES : (h + 1) * LANES] * sign
             most = jnp.max(jnp.maximum(jnp.abs(real), jnp.abs(imag)), axis=0, keepdims=True)
             most = jnp.maximum(most, 1e-30)
             unit_ref[2 * j + h] = most * (1.0 / LEVELS)
@@ -770,176 +767,72 @@
             packed = level(real * to_level) * 65536 + level(imag * to_level)
             to = pl.ds(pl.multiple_of(at + h * LANES, LANES), LANES)
             picked_ref[to, :] = packed.T
+        for i in range(4):
+            to = j * 4 + i
+
+            @pl.when(to != me)
+            def _():
+                for copy in sends(to):
+                    copy.start()
+
         return carry
 
-    lax.fori_loop(0, tiles // (2 * LANES), pick, 0)
-
-
-def image_step(blocks, cols, me, sky_image, smooth, groups, slots, piece):
-    rows, width = sky_image.shape
-    tiles = blocks.shape[0] * blocks.shape[1]
-    low = width // LANES
-    kept = low // 2 + 1
-    turn = np.arange(piece)
-    angle = (me * rows + jnp.arange(rows, dtype=jnp.int32))[:, None] * turn[None, :] % width
-    angle = (2.0 * math.pi / width) * angle.astype(jnp.float32)
-    cosine, sine = jnp.cos(angle), jnp.sin(angle)
-    turn = jnp.concatenate(
-        [jnp.concatenate([cosine, -sine], axis=1), jnp.concatenate([sine, cosine], axis=1)]
-    ).astype(jnp.bfloat16)
-    owner = np.arange(LANES) // slots % groups
-    shift = 2 * np.pi * (np.arange(rows)[:, None] * owner[None, :] % groups) / groups
-    phase = f32(np.stack([np.cos(shift), np.sin(shift)]))
-    wide = np.arange(LANES)
-    full = 2 * np.pi * (wide[:, None] * wide[None, :] % LANES) / LANES
-    c, s = np.cos(full) / width, np.sin(full) / width
-    inverse = bf16(np.block([[c, s], [-s, c]]))
-    forward = jnp.stack(table_pair(np.block([[c, -s], [s, c]])))
-    twist = 2 * np.pi * np.arange(kept + 1)[:, None] * wide[None, :] / width
-    twist = f32(np.stack([np.cos(twist), np.sin(twist)]))
-    return pl.pallas_call(
-        lambda *refs: image_kernel(low, *refs),
-        out_shape=(
-            jax.ShapeDtypeStruct((rows, width), jnp.float32),
-            jax.ShapeDtypeStruct((rows, width), jnp.float32),
-            jax.ShapeDtypeStruct((tiles, rows), jnp.int32),
-            jax.ShapeDtypeStruct((tiles // LANES, 1, LANES), jnp.float32),
-        ),
-        in_specs=[whole] * 9,
-        out_specs=(whole,) * 4,
-        scratch_shapes=[
-            pltpu.VMEM((2, tiles // LANES, LANES), jnp.float32),
-            pltpu.VMEM((2 * rows, tiles), jnp.bfloat16),
-            pltpu.VMEM(((kept + 1) * LANES, tiles), jnp.bfloat16),
-            pltpu.VMEM((kept + 1, rows, 2 * LANES), jnp.float32),
-            pltpu.VMEM((2 * rows, kept * LANES), jnp.bfloat16),
-            pltpu.VMEM((2 * rows, kept * LANES), jnp.bfloat16),
-        ],
-        compiler_params=pltpu.CompilerParams(vmem_limit_bytes=60 * 2**20),
-        name="image_step",
-    )(
-        blocks.reshape(tiles, -1),
-        cols,
-        turn,
-        phase,
-        inverse,
-        twist,
-        forward,
-        sky_image,
-        smooth,
-    )
-
-
-def exchange_kernel(
-    picked_ref, unit_ref, top_ref, got_ref, units_ref, below_ref, send_a, send_b, recv_a, recv_b, halo
-):
-    x, z, y, core, groups = place()
-    devices = 2 * groups
-    tiles = got_ref.shape[1]
-
-    def flipped(value, bit):
-        return value + (1 - 2 * (value // bit % 2)) * bit
-
-    me = x * groups + z * 4 + y * 2 + core
-    barrier = pltpu.get_barrier_semaphore()
-    peers = []
-    for code in sorted(range(1, devices), key=lambda code: -(code // 8 % 2)):
-        vis = z * 4 + y * 2 + core
-        for bit in (1, 2, 4, 8):
-            if code & bit:
-                vis = flipped(vis, bit)
-        band = 1 - x if code & 16 else x
-        peers.append((band, vis))
-    for peer in peers:
-        pl.semaphore_signal(barrier, inc=1, device_id=peer, device_id_type=MESH)
-    before = (me + devices - 1) % devices
-    pl.semaphore_wait(barrier, devices - 1)
-    edge = pltpu.make_async_remote_copy(
-        src_ref=top_ref,
-        dst_ref=below_ref,
-        send_sem=halo.at[0],
-        recv_sem=halo.at[1],
-        device_id=(before // groups, before % groups),
-        device_id_type=MESH,
-    )
-    edge.start()
-    copies = []
-    for i, (band, vis) in enumerate(peers):
-        to = band * groups + vis
-        at = pl.ds(pl.multiple_of(to * tiles, tiles), tiles)
-        copies.append(
-            pltpu.make_async_remote_copy(
-                src_ref=picked_ref.at[at, :],
-                dst_ref=got_ref.at[me],
-                send_sem=send_a.at[i],
-                recv_sem=recv_a.at[i],
-                device_id=(band, vis),
-                device_id_type=MESH,
-            )
-        )
-        copies.append(
-            pltpu.make_async_remote_copy(
-                src_ref=unit_ref.at[to // 2],
-                dst_ref=units_ref.at[me],
-                send_sem=send_b.at[i],
-                recv_sem=recv_b.at[i],
-                device_id=(band, vis),
-                device_id_type=MESH,
-            )
-        )
-    for copy in copies:
-        copy.start()
-    here = pl.ds(pl.multiple_of(me * tiles, tiles), tiles)
-    got_ref[me] = picked_ref[here, :]
+    lax.fori_loop(0, devices // 4, pick, 0)
+    got_ref[me] = picked_ref[pl.ds(pl.multiple_of(me * tiles, tiles), tiles), :]
     units_ref[me] = unit_ref[me // 2]
-    edge.wait()
-    for copy in copies:
-        copy.wait()
-
-
-def exchange(picked, units, extrap, devices):
-    tiles = picked.shape[0] // devices
-    top = extrap[:8]
-    return pl.pallas_call(
-        exchange_kernel,
-        out_shape=(
-            jax.ShapeDtypeStruct((devices, tiles) + picked.shape[1:], picked.dtype),
-            jax.ShapeDtypeStruct((devices,) + units.shape[1:], units.dtype),
-            jax.ShapeDtypeStruct(top.shape, top.dtype),
-        ),
-        in_specs=[whole] * 3,
-        out_specs=(whole,) * 3,
-        scratch_shapes=[
-            pltpu.SemaphoreType.DMA((devices - 1,)),
-            pltpu.SemaphoreType.DMA((devices - 1,)),
-            pltpu.SemaphoreType.DMA((devices - 1,)),
-            pltpu.SemaphoreType.DMA((devices - 1,)),
-            pltpu.SemaphoreType.DMA((2,)),
-        ],
-        compiler_params=pltpu.CompilerParams(collective_id=1, has_side_effects=True),
-        name="exchange",
-    )(picked, units, top)
-
-
-def tile_kernel(
-    devices, got_ref, units_ref, phase_ref, last_ref, order_ref, out_ref, mid_ref, unit_ref
-):
-    tiles, rows = phase_ref.shape[1:]
-    group = LANES * 2 // 16
+    top.wait()
+    loads[8].wait()
+    loads[9].wait()
+
+    def rows_down(i, carry):
+        for k in range(half_rows // 8):
+            lows, highs = 0.0, 0.0
+            for tap in range(8):
+                taken = extrap_ref[i, pl.ds(16 * k + tap, 8, stride=2), :]
+                lows = lows + low_taps[tap] * taken
+                highs = highs + high_taps[tap] * taken
+            tall_ref[i, 8 * k : 8 * k + 8, :] = lows
+            tall_ref[i, half_rows + 8 * k : half_rows + 8 * k + 8, :] = highs
+        return carry
+
+    lax.fori_loop(0, low, rows_down, 0)
+
+    def cols_down(b, absolute):
+        here = jnp.concatenate([tall_ref[2 * b], tall_ref[2 * b + 1]], axis=1)
+        out = taps_dot(here, near_ref) + taps_dot(tall_ref[(2 * b + 2) % low], next_ref)
+        at = pl.ds(pl.multiple_of(b * LANES, LANES), LANES)
+        for c in range(4):
+            top_row, left = c // 2 * half_rows, c % 2 * LANES
+            part = out[top_row : top_row + half_rows, left : left + LANES]
+            absolute = absolute + jnp.abs(part)
+            merged_ref[c, :, at] = joined_ref[c, 8:, at] + part
+        return absolute
+
+    absolute = lax.fori_loop(0, low // 2, cols_down, jnp.zeros((half_rows, LANES), jnp.float32))
+    abs_total = jnp.sum(jnp.sum(absolute, axis=0, keepdims=True), axis=1, keepdims=True)
+    loads[10].wait()
+    loads[11].wait()
+
+    def landed(k, carry):
+        for copy in arrivals((me + k) % devices):
+            copy.wait_recv()
+        return carry
+
+    lax.fori_loop(1, devices, landed, 0)
+
     units = jnp.concatenate([units_ref[d] for d in range(devices)], axis=0)
     units = jnp.concatenate([units] * (LANES // devices), axis=0).T
-    unit_ref[...] = jnp.where(lax.axis_index("vis") % 2 == 0, units[:tiles], units[tiles:])
-
-    def strip(i, carry):
-        at = pl.multiple_of(i * 8, 8)
-        here = pl.ds(at, 8)
-        cosine, sine = phase_ref[0, here, :], phase_ref[1, here, :]
+    column_ref[...] = jnp.where(core == 0, units[:tiles], units[tiles:])
+
+    def finish(i, carry):
+        here = pl.ds(pl.multiple_of(i * 8, 8), 8)
+        cosine, sine = shift_ref[0, here, :], shift_ref[1, here, :]
         reals, imags = [], []
         for d in range(devices):
             packed = got_ref[d, here, :]
             real = (packed + 32768) >> 16
             imag = packed - (real << 16)
-            unit = unit_ref[here, d : d + 1]
+            unit = column_ref[here, d : d + 1]
             real = real.astype(jnp.float32) * unit
             imag = imag.astype(jnp.float32) * unit
             reals.append(real * cosine + imag * sine)
@@ -962,7 +855,8 @@
                 mid_ref[t, here, rows:] = imag
         return carry
 
-    lax.fori_loop(0, tiles // 8, strip, 0)
+    lax.fori_loop(0, tiles // 8, finish, 0)
+    group = 2 * LANES // 16
     lane = lax.broadcasted_iota(jnp.int32, (1, 2 * LANES), 1) // 16
     pieces = []
     for g in range(devices // group):
@@ -974,45 +868,179 @@
             out = jnp.where(lane == e, out, 0.0)
             total = out if total is None else total + out
         pieces.append(total.astype(jnp.bfloat16))
-    tile = jnp.concatenate(pieces, axis=1)
-    out_ref[...] = nn_dot(tile, order_ref[...])
-
-
-def finish_tiles(got, units, devices, groups, slots, rows, piece):
-    width = devices * rows
+    tile = nn_dot(jnp.concatenate(pieces, axis=1), order_ref[...]).astype(jnp.bfloat16)
+    piece = kernels_ref.shape[1]
+    first, second = [], []
+    for i in range(tiles // count):
+        here = tile[i * count : (i + 1) * count]
+        pair = jnp.concatenate([here[:, :piece], here[:, piece:]], axis=0)
+        out = nt_dot(pair, kernels_ref[i * span : (i + 1) * span, :])
+        first.append(jnp.sum(jnp.where(mine, out[:count], 0.0), axis=0, keepdims=True))
+        second.append(jnp.sum(jnp.where(mine, out[count:], 0.0), axis=0, keepdims=True))
+    first = jnp.concatenate(first, axis=0)
+    second = jnp.concatenate(second, axis=0)
+    visits = span // count // 2
+    lane = lax.broadcasted_iota(jnp.int32, first.shape, 1) // visits % 2
+    crossed = jnp.where(
+        lane == 0, -pltpu.roll(second, span - visits, 1), pltpu.roll(second, visits, 1)
+    )
+    live = vis_ref[2]
+    residual = live * (vis_ref[0] + first + crossed - vis_ref[1])
+    residual_ref[...] = residual
+    norms = []
+    for values in (residual, vis_ref[1] * live):
+        norms.append(jnp.sum(jnp.sum(values * values, axis=0, keepdims=True), axis=1, keepdims=True))
+    lane = lax.broadcasted_iota(jnp.int32, (1, LANES), 1)
+    row = jnp.where(lane == 0, abs_total, jnp.where(lane == 1, norms[0], norms[1]))
+    all_sums_ref[me] = row
+
+    def share(k, carry):
+        to = (me + k) % devices
+        own = all_sums_ref.at[me]
+        remote(own, own, send_s.at[to], recv_s.at[me], ident(to)).start()
+        return carry
+
+    lax.fori_loop(1, devices, share, 0)
+    for copy in started:
+        copy.wait_send()
+    store.wait()
+
+    def shared(k, total):
+        other = (me + k) % devices
+        own = all_sums_ref.at[other]
+        remote(own, own, send_s.at[other], recv_s.at[other], twin).wait_recv()
+        return total
+
+    lax.fori_loop(1, devices, shared, 0)
+    total = all_sums_ref[0]
+    for d in range(1, devices):
+        total = total + all_sums_ref[d]
+    sums_ref[...] = total
+
+    def sent(k, carry):
+        to = (me + k) % devices
+        for copy in sends(to):
+            copy.wait_send()
+        own = all_sums_ref.at[me]
+        remote(own, own, send_s.at[to], recv_s.at[me], ident(to)).wait_send()
+        return carry
+
+    lax.fori_loop(1, devices, sent, 0)
+
+
+def step(kernels, coef, sky, weights, cols, vis, me, groups, slots, devices):
+    rows, width = sky.shape
+    piece = kernels.shape[1]
     tiles = groups * slots
-    shift = np.arange(tiles)[:, None] // slots * np.arange(rows)[None, :] % groups
-    shift = 2 * np.pi * shift / groups
-    phase = f32(np.stack([np.cos(shift), np.sin(shift)]))
+    half_rows, half_width = coef.shape[1:]
+    low = width // LANES
+    kept = low // 2 + 1
+    wide = np.arange(LANES)
+    matrix = synthesis_matrix(LANES)
+    up = matrix[:, :, 3:].transpose(1, 2, 0).reshape(2 * LANES, 2 * LANES)
+    edge = np.zeros((2, LANES, LANES))
+    edge[:, LANES - 3 :, :] = matrix[:LANES, :, :3].transpose(1, 2, 0)
+    matrix = analysis_matrix(LANES).T
+    following = np.zeros((LANES, 2 * LANES))
+    following[:6] = matrix[2 * LANES :]
+    turn = np.arange(piece)
+    angle = (me * rows + jnp.arange(rows, dtype=jnp.int32))[:, None] * turn[None, :] % width
+    angle = (2.0 * math.pi / width) * angle.astype(jnp.float32)
+    cosine, sine = jnp.cos(angle), jnp.sin(angle)
+    turn = jnp.concatenate(
+        [jnp.concatenate([cosine, -sine], axis=1), jnp.concatenate([sine, cosine], axis=1)]
+    ).astype(jnp.bfloat16)
+    owner = wide // slots % groups
+    shift = 2 * np.pi * (np.arange(rows)[:, None] * owner[None, :] % groups) / groups
+    phase = np.stack([np.cos(shift), np.sin(shift)])
+    full = 2 * np.pi * (wide[:, None] * wide[None, :] % LANES) / LANES
+    c, s = np.cos(full) / width, np.sin(full) / width
+    inverse = np.block([[c, s], [-s, c]])
+    forward = np.block([[c, -s], [s, c]])
+    twist = 2 * np.pi * np.arange(kept + 1)[:, None] * wide[None, :] / width
     each = piece // devices
     t = np.arange(devices)[:, None] + devices * np.arange(each)[None, :]
     angle = 2 * np.pi * (np.arange(rows)[:, None, None] * t[None] % width) / width
     c, s = np.cos(angle), np.sin(angle)
-    table = np.stack([np.stack([c, -s], axis=2), np.stack([s, c], axis=2)])
-    table = table.reshape(2 * rows, -1, 2 * LANES).transpose(1, 0, 2)
-    last = jnp.stack(table_pair(table))
+    last = np.stack([np.stack([c, -s], axis=2), np.stack([s, c], axis=2)])
+    last = last.reshape(2 * rows, -1, 2 * LANES).transpose(1, 0, 2)
     order = np.zeros((2 * piece, 2 * piece))
     for a in range(devices):
         for part in range(2):
             for b in range(each):
                 order[(a * 2 + part) * each + b, part * piece + a + devices * b] = 1.0
+    loaded = [
+        kernels,
+        coef,
+        sky,
+        jnp.stack(table_pair(up)),
+        jnp.stack(table_pair(edge.reshape(2 * LANES, LANES))),
+        turn,
+        bf16(inverse),
+        jnp.stack(table_pair(forward)),
+        jnp.stack(table_pair(matrix[: 2 * LANES])),
+        jnp.stack(table_pair(following)),
+        jnp.stack(table_pair(last)),
+        bf16(order),
+    ]
+    held = [
+        weights,
+        cols,
+        vis,
+        f32(phase),
+        f32(phase[:, :, :tiles].transpose(0, 2, 1)),
+        f32(np.stack([np.cos(twist), np.sin(twist)])),
+    ]
+    buffers = [pltpu.VMEM(value.shape, value.dtype) for value in loaded]
+    buffers[1] = pltpu.VMEM((4, half_rows + 8, half_width), jnp.float32)
+    copies = 3 * 4 + 7 + 12
+    dma = pltpu.SemaphoreType.DMA
+    anywhere = pl.BlockSpec(memory_space=pl.ANY)
     return pl.pallas_call(
-        lambda *refs: tile_kernel(devices, *refs),
-        out_shape=jax.ShapeDtypeStruct((tiles, 2 * piece), jnp.float32),
-        in_specs=[whole] * 5,
-        out_specs=whole,
-        scratch_shapes=[
+        lambda *refs: step_kernel(low, *refs),
+        out_shape=(
+            jax.ShapeDtypeStruct((rows, width), jnp.float32),
+            jax.ShapeDtypeStruct(coef.shape, jnp.float32),
+            jax.ShapeDtypeStruct(vis.shape[1:], jnp.float32),
+            jax.ShapeDtypeStruct((1, LANES), jnp.float32),
+        ),
+        in_specs=[anywhere] * len(loaded) + [whole] * len(held),
+        out_specs=(anywhere, whole, whole, whole),
+        scratch_shapes=buffers[:1]
+        + [buffers[1]]
+        + buffers[2:]
+        + [
+            dma((len(loaded) + 1,)),
+            pltpu.VMEM((16, half_width), jnp.float32),
+            pltpu.VMEM((16, half_width), jnp.float32),
+            pltpu.VMEM((devices, tiles, 2 * piece), jnp.bfloat16),
+            pltpu.VMEM((devices,) + cols.shape, jnp.int32),
+            pltpu.VMEM((low, rows, LANES), jnp.float32),
+            pltpu.VMEM((low, rows, LANES), jnp.float32),
+            pltpu.VMEM((2, devices // 2, LANES), jnp.float32),
+            pltpu.VMEM((2 * rows, devices * tiles), jnp.bfloat16),
+            pltpu.VMEM(((kept + 1) * LANES, devices * tiles), jnp.bfloat16),
+            pltpu.VMEM((kept + 1, rows, 2 * LANES), jnp.float32),
+            pltpu.VMEM((2 * rows, kept * LANES), jnp.bfloat16),
+            pltpu.VMEM((2 * rows, kept * LANES), jnp.bfloat16),
+            pltpu.VMEM((low, rows + 8, LANES), jnp.float32),
+            pltpu.VMEM((devices * tiles, rows), jnp.int32),
+            pltpu.VMEM((devices // 2, 1, LANES), jnp.float32),
+            pltpu.VMEM((devices, tiles, rows), jnp.int32),
+            pltpu.VMEM((devices, 1, LANES), jnp.float32),
             pltpu.VMEM((devices, tiles, 2 * rows), jnp.float32),
             pltpu.VMEM((tiles, LANES), jnp.float32),
-        ],
-        compiler_params=pltpu.CompilerParams(vmem_limit_bytes=40 * 2**20),
-        name="finish_tiles",
-    )(got, units, phase, last, bf16(order))
-
-
-def to_all(values, devices):
-    flat = jnp.broadcast_to(values.reshape(1, -1), (devices, values.size))
-    return lax.all_to_all(flat, everywhere, split_axis=0, concat_axis=0, tiled=True)
+            pltpu.VMEM((devices, 1, LANES), jnp.float32),
+            dma((copies,)),
+            dma((copies,)),
+        ]
+        + [dma((devices,))] * 8
+        + [dma((4,))],
+        compiler_params=pltpu.CompilerParams(
+            collective_id=0, has_side_effects=True, vmem_limit_bytes=58 * 2**20
+        ),
+        name="step",
+    )(*loaded, *held)
 
 
 def fast_local(sky_image, coef_dual, vis_dual, visibilities, kernel_blocks, tile_rows, tile_counts):
@@ -1037,30 +1065,18 @@
     weights = jnp.stack([weights, jnp.stack([weights[:, :, 1], -weights[:, :, 0]], axis=2)])
     weights = weights.reshape(2, tiles // 16, -1)
     kernels = kernel_here.reshape(-1, piece)
-    blocks, cols, smooth = gather_all(kernels, weights, columns_here, coef_dual, devices)
-    new_image, extrap, picked, units = image_step(
-        blocks, cols, me, sky_image, smooth, groups, slots, piece
+    vis_rows = (tiles // 16, kernels.shape[0] * 16 // tiles)
+    live = jnp.broadcast_to(live_slots, vis_state.shape)
+    vis = jnp.stack([vis_state, vis_data, live]).reshape((3,) + vis_rows)
+    new_image, merged, residual, sums = step(
+        kernels, coef_dual, sky_image, weights, columns_here, vis, me, groups, slots, devices
     )
-    got, units, below = exchange(picked, units, extrap, devices)
-    tile = finish_tiles(got, units, devices, groups, slots, rows_dev, piece)
-    tile = tile.astype(jnp.bfloat16).reshape(groups, slots, 2, piece)
-    coeffs = fast_analysis(extrap, below[:6])
-    predicted = degrid(kernel_here, tile)
-    residual = live_slots * (vis_state + predicted - vis_data)
-    sums = jnp.stack(
-        [
-            jnp.sum(jnp.abs(coeffs)),
-            jnp.sum(residual * residual),
-            jnp.sum(live_slots * vis_data * vis_data),
-        ]
-    )
-    sums = jnp.sum(to_all(sums, devices), axis=0)
-    threshold = 0.5 * sums[0] / (width * width)
-    coef_dual = jnp.clip(coef_dual + coeffs, -threshold, threshold)
-    radius = 0.5 * jnp.sqrt(sums[2] + 1e-06)
-    size_value = jnp.sqrt(sums[1] + 1e-06)
+    threshold = 0.5 * sums[0, 0] / (width * width)
+    coef_dual = jnp.clip(merged, -threshold, threshold)
+    radius = 0.5 * jnp.sqrt(sums[0, 2] + 1e-06)
+    size_value = jnp.sqrt(sums[0, 1] + 1e-06)
     vis_state = residual * (1.0 - jnp.minimum(1.0, radius / size_value))
-    return (new_image, coef_dual, vis_state[None, None])
+    return (new_image, coef_dual, vis_state.reshape(vis_dual.shape))
 
 
 def body_for(mesh):

time: 143 us -> 101 us (0.71)
  local copies, waits for them, and re-layouts: 23.8 us -> 5.9 us
  matrix products: 9.37 us -> 0 us
  starting transfers between devices: 5.06 us -> 0 us
  other arithmetic: 13.4 us -> 9.09 us
  Pallas kernels: 85.9 us -> 83.1 us
  waiting for transfers between devices: 1.7 us -> 0 us
    unnamed x44 -> x5, local copies, waits for them, and re-layouts: 11.4 us -> 1.33 us
    dot_general x8 -> x0, matrix products: 9.37 us -> none  [the longest x2 3.62 us: fast_analysis(): jnp.einsum('ij,jn->in', f32(analysis_matrix(rows_dev // 2)), extended, pr...]
    all_to_all x1 -> x0, starting transfers between devices: 5.06 us -> none  [to_all(): lax.all_to_all(flat, everywhere, split_axis=0, concat_axis=0, tiled=True)]
    reshape x3 -> x1, local copies, waits for them, and re-layouts: 5.18 us -> 0.75 us  [fast_local(): return (new_image, coef_dual, vis_state.reshape(vis_dual.shape))]
    reduce_sum x3 -> x0, other arithmetic: 3.53 us -> none  [the longest x1 2.77 us: fast_local(): jnp.sum(jnp.abs(coeffs))]
    pallas_call x4 -> x1, Pallas kernels: 85.9 us -> 83.1 us  [step(): pl.pallas_call(lambda *refs: step_kernel(low, *refs), out_shape=(jax.Shap...]
    transpose x1 -> x0, local copies, waits for them, and re-layouts: 2.54 us -> none  [fast_analysis(): jnp.transpose(out, (0, 3, 1, 2, 4)).reshape(4, rows_dev // 2, width // 2)]
    all_to_all x1 -> x0, waiting for transfers between devices: 1.7 us -> none  [to_all(): lax.all_to_all(flat, everywhere, split_axis=0, concat_axis=0, tiled=True)]
  transfers between devices with their start and end apart: 1 -> 0, of which waited for: 1 -> 0; matrix products, arithmetic and copies ran while one was open for 4% -> 0% of each run, Pallas kernels for 0% -> 0%
where the time goes in v2:
time: 101 us
  Pallas kernels  83.1 us (82%)
  other arithmetic  9.09 us (9%)
  local copies, waits for them, and re-layouts  5.9 us (6%)
  between operations  2.75 us (3%)
    pallas_call x1, Pallas kernels, step(): pl.pallas_call(lambda *refs: step_kernel(low, *refs), out_shape=(jax.Shap...  83.1 us
    min x1, other arithmetic, fast_local(): coef_dual = jnp.clip(merged, -threshold, threshold)  3.38 us

profile of v2, /device:TPU:0, one launch (start us, length us, event | category | flops | bytes accessed | tf_op | source)
XLA Modules:
  0.0 100.8 jit_solution(18188078367105157249)
XLA Ops:
  0.6 0.7 broadcast_add_fusion
  1.3 0.1 copy.29
  1.4 0.1 add.49
  1.5 0.6 pad_add_fusion.refs_13_
  2.1 0.7 fusion.8
  2.8 1.0 squeeze.4
  3.8 1.0 stack.91
  4.8 1.0 bitcast_multiply_fusion
  5.7 0.1 fusion.9
  5.8 0.1 pad_maximum_fusion
  5.9 0.1 stack.89
  6.0 0.1 mul.69
  6.1 0.1 mul.70
  6.3 0.6 pad_maximum_fusion.1.refs_14_
  6.9 0.6 pad_maximum_fusion.2.refs_12_
  7.5 0.6 negate_convert_fusion
  8.2 0.7 maximum_maximum_fusion.refs_5_
  8.9 83.1 %step.1 = (f32[128,4096]{1,0:T(8,128)}, f32[4,64,2048]{2,1,0:T(8,128)}, f32[4,1024]{1,0:T(4,128)}, f32[1,128]{1,0:T(1,128)}) custom-call(bf16[4096,256]{1,0:T(8,128)(2,1)} %bitcast.8, f32[4,64,2048]{2,1,0:T(8,128)} %refs_1_.1, f32[128,4096]{1,0:T(8,128)} %refs_2_.1, bf16[2,256,256]{2,1,0:T(8,128)(2,1)} %constant.93.refs_3_, ...), custom_call_target="tpu_custom_call" | custom-call | tf_op jit(solution)/shard_map/step/pallas_call | solution.py:999
  92.0 1.3 %fusion.10 = (f32[1,1]{1,0:T(1,128)}, f32[1,1]{1,0:T(1,128)}, f32[1,1]{1,0:T(1,128)}) fusion(f32[1,128]{1,0:T(1,128)} %get-tuple-element.8), kind=kLoop, calls=%fused_computation.28 | loop fusion | bytes 24 | tf_op jit(solution)/shard_map/slice | solution.py:1077
  95.3 0.0 copy-start.1
  95.3 0.0 copy-start
  95.3 3.4 %maximum_minimum_fusion = f32[4,64,2048]{2,1,0:T(8,128)} fusion(f32[4,64,2048]{2,1,0:T(8,128)} %get-tuple-element.9, f32[]{:T(128)S(6)} %neg.12, f32[]{:T(128)} %bitcast.3), kind=kLoop, calls=%fused_computation | loop fusion | flops 1048576 | bytes 4194312 | tf_op jit(solution)/shard_map/jit(clip)/min | solution.py:1075
  98.7 0.0 copy-done.1
  98.7 0.8 reshape.102
  99.5 0.0 copy-done
  99.5 1.3 %copy.31 = f32[128,4096]{1,0:T(8,128)} copy(f32[128,4096]{1,0:T(8,128)S(1)} %copy-done) | data formatting | bytes 4194304
  (3 shorter events, 0.0 us)
Async XLA Ops:
  95.3 3.4 %copy-start.1 = (f32[4,1024]{1,0:T(4,128)S(1)}, f32[4,1024]{1,0:T(4,128)}, u32[]{:S(2)}) copy-start(f32[4,1024]{1,0:T(4,128)} %get-tuple-element.10) | copy-start | bytes 49156
  95.3 4.2 %copy-start = (f32[128,4096]{1,0:T(8,128)S(1)}, f32[128,4096]{1,0:T(8,128)}, u32[]{:S(2)}) copy-start(f32[128,4096]{1,0:T(8,128)} %get-tuple-element.22) | copy-start | bytes 6291460

commit v3 on v2

--- a/solution.py
+++ b/solution.py
@@ -409,29 +409,30 @@
     sky_hbm,
     up_hbm,
     edge_hbm,
-    turn_hbm,
+    base_hbm,
+    spin_hbm,
     inv_hbm,
     fwd_hbm,
     near_hbm,
     next_hbm,
     last_hbm,
     order_hbm,
-    weights_ref,
-    cols_ref,
-    vis_ref,
+    state_ref,
+    data_ref,
+    rows_ref,
+    counts_ref,
     phase_ref,
     shift_ref,
     tw_ref,
-    image_hbm,
+    sky_ref,
     merged_ref,
-    residual_ref,
-    sums_ref,
+    vis_out_ref,
     kernels_ref,
     joined_ref,
-    sky_ref,
     up_ref,
     edge_ref,
-    turn_ref,
+    base_ref,
+    spin_ref,
     inv_ref,
     fwd_ref,
     near_ref,
@@ -443,6 +444,8 @@
     halo_ref,
     block_ref,
     all_cols_ref,
+    turn_ref,
+    total_ref,
     tall_ref,
     smooth_ref,
     fold_ref,
@@ -515,7 +518,8 @@
         (coef_hbm, joined_ref.at[:, pl.ds(8, half_rows), :]),
         (up_hbm, up_ref),
         (edge_hbm, edge_ref),
-        (turn_hbm, turn_ref),
+        (base_hbm, base_ref),
+        (spin_hbm, spin_ref),
         (inv_hbm, inv_ref),
         (sky_hbm, sky_ref),
         (fwd_hbm, fwd_ref),
@@ -532,15 +536,42 @@
     loads[0].wait()
     count = 16
     span = kernels_ref.shape[0] * count // tiles
-    lane = lax.broadcasted_iota(jnp.int32, (count, span), 1) // (span // count)
-    mine = lane == lax.broadcasted_iota(jnp.int32, (count, span), 0)
+    width = low * wide
+    stripe = width // 2
+    slots = rows_ref.shape[1]
+    lane = lax.broadcasted_iota(jnp.int32, (tiles, groups), 1)
+    tile_id = lax.broadcasted_iota(jnp.int32, (tiles, groups), 0)
+    counts = jnp.where(lane == tile_id // slots, counts_ref[...].astype(jnp.float32), 0.0)
+    counts = jnp.sum(counts, axis=1, keepdims=True)
+    tile_id = lax.broadcasted_iota(jnp.int32, (tiles, 1), 0)
+    live = jnp.where((tile_id % slots).astype(jnp.float32) < counts, 1.0, 0.0)
+    state = [state_ref[:, part, :] for part in range(2)]
+    data = [data_ref[:, part, :] for part in range(2)]
+    ours = [part * live for part in state]
+    turned = [ours[0], ours[1], ours[0], ours[1]], [ours[1], -ours[0], ours[1], -ours[0]]
+    turned = [jnp.concatenate(parts, axis=1) for parts in turned]
+    pair_lane = lax.broadcasted_iota(jnp.int32, (count, LANES), 1) // (LANES // 2)
+    pair_row = lax.broadcasted_iota(jnp.int32, (count, LANES), 0)
+    masks = [pair_lane + 2 * k == pair_row for k in range(count // 2)]
     for i in range(tiles // count):
-        spread = [jnp.where(mine, weights_ref[part, i : i + 1, :], 0.0) for part in range(2)]
+        spread = [
+            jnp.concatenate(
+                [jnp.where(mask, part[i * count : (i + 1) * count], 0.0) for mask in masks], axis=1
+            )
+            for part in turned
+        ]
         spread = jnp.concatenate(spread, axis=0).astype(jnp.bfloat16)
         both = nn_dot(spread, kernels_ref[i * span : (i + 1) * span, :])
         both = jnp.concatenate([both[:count], both[count:]], axis=1)
         block_ref[me, i * count : (i + 1) * count, :] = both.astype(jnp.bfloat16)
-    all_cols_ref[me] = cols_ref[...]
+    lane = lax.broadcasted_iota(jnp.int32, (groups, LANES), 1) % tiles
+    owner = lax.broadcasted_iota(jnp.int32, (groups, LANES), 0)
+    columns = 0.0
+    for slot in range(slots):
+        here = rows_ref[:, slot : slot + 1].astype(jnp.float32)
+        columns = columns + jnp.where(lane == owner * slots + slot, here, 0.0)
+    columns = jnp.sum(columns, axis=0, keepdims=True).astype(jnp.int32)
+    all_cols_ref[me] = columns + x * stripe
     loads[1].wait()
     for c in range(4):
         tail_ref[3 * c : 3 * c + 3, :] = joined_ref[c, half_rows + 5 :, :]
@@ -560,25 +591,24 @@
             own = ref.at[block]
             remote(own, own, send.at[0], recv.at[block], twin).wait_recv()
 
-    slots = iter(range(send_a.shape[0]))
+    slots_of = iter(range(send_a.shape[0]))
     far = sorted(range(1, levels), key=lambda k: abs(k - levels / 2))
     for k in far:
-        start(me, line[k - 1], next(slots))
+        start(me, line[k - 1], next(slots_of))
     for target in plane:
-        start(me, target, next(slots))
+        start(me, target, next(slots_of))
     edge = remote(tail_ref, halo_ref, halo_sem.at[0], halo_sem.at[1], ident(after))
     edge.start()
-    start(me, twin, next(slots))
+    start(me, twin, next(slots_of))
+    line_blocks = [index(x, (z + levels - k) % levels, y, core) for k in far]
+    for block in line_blocks:
+        got(block)
+        for target in plane:
+            start(block, target, next(slots_of))
+        start(block, twin, next(slots_of))
     edge.wait()
     for c in range(4):
         joined_ref[c, 5:8, :] = halo_ref[3 * c : 3 * c + 3, :]
-
-    line_blocks = [index(x, (z + levels - k) % levels, y, core) for k in range(1, levels)]
-    for block in line_blocks:
-        got(block)
-        for target in plane:
-            start(block, target, next(slots))
-        start(block, twin, next(slots))
     strips = half_width // LANES
 
     def tall(i, carry):
@@ -600,14 +630,9 @@
     for px, py in corners:
         block = index(px, z, py, core)
         got(block)
-        start(block, twin, next(slots))
-    for k in range(1, levels):
-        for px, py in corners:
-            block = index(px, (z + levels - k) % levels, py, core)
-            got(block)
-            start(block, twin, next(slots))
-    loads[2].wait()
-    loads[3].wait()
+        start(block, twin, next(slots_of))
+    for load in loads[2:8]:
+        load.wait()
 
     def broad(i, carry):
         there = (i + strips - 1) % strips
@@ -619,47 +644,81 @@
         smooth_ref[2 * i + 1] = out[:, LANES:]
         return carry
 
-    lax.fori_loop(0, strips, broad, 0)
-    loads[4].wait()
-    loads[5].wait()
-
-    for i in range(groups):
-        bx, rest = i // (groups // 2), i % (groups // 2)
-        got(bx * groups + rest * 2 + 1 - core)
+    lax.fori_loop(0, strips // 2, broad, 0)
+    spin_cos, spin_sin = spin_ref[0, pl.ds(me, 1), :], spin_ref[1, pl.ds(me, 1), :]
+    cosine = (base_ref[0] * spin_cos - base_ref[1] * spin_sin).astype(jnp.bfloat16)
+    sine = (base_ref[1] * spin_cos + base_ref[0] * spin_sin).astype(jnp.bfloat16)
+    piece = kernels_ref.shape[1]
+    turn_ref[:rows, :piece] = cosine
+    turn_ref[:rows, piece:] = -sine
+    turn_ref[rows:, :piece] = sine
+    turn_ref[rows:, piece:] = cosine
+    for n, k in enumerate(far):
+        for px, py in corners:
+            block = index(px, (z + levels - k) % levels, py, core)
+            got(block)
+            start(block, twin, next(slots_of))
+        if n == 0:
+            lax.fori_loop(strips // 2, strips, broad, 0)
 
     total_tiles = devices * tiles
+    class_tiles = groups * tiles
+    parts = class_tiles // LANES
     lane = lax.broadcasted_iota(jnp.int32, (1, LANES), 1)
-    for i in range(devices // 2):
-        columns = jnp.where(lane < tiles, all_cols_ref[2 * i], all_cols_ref[2 * i + 1])
-        k1 = columns % low
-        k2 = columns // low
-        flip = k1 >= kept
-        k1 = jnp.where(flip, low - k1, k1)
-        k2 = jnp.where(flip, wide - 1 - k2, k2)
-        fold_ref[0, i : i + 1, :] = (k1 * wide + k2).astype(jnp.float32)
-        fold_ref[1, i : i + 1, :] = jnp.where(flip, -1.0, 1.0)
-    chunk = 512
-    for j in range(total_tiles // chunk):
-        some = block_ref[j * chunk // tiles : (j + 1) * chunk // tiles]
-        both = nt_dot(turn_ref[...], some.reshape(chunk, -1))
-        for i in range(chunk // LANES):
-            b = j * (chunk // LANES) + i
-            real = both[:rows, i * LANES : (i + 1) * LANES]
-            imag = both[rows:, i * LANES : (i + 1) * LANES]
-            out_real = real * phase_ref[0] - imag * phase_ref[1]
-            out_imag = (real * phase_ref[1] + imag * phase_ref[0]) * fold_ref[1, b : b + 1, :]
-            grid_ref[:rows, b * LANES : (b + 1) * LANES] = out_real.astype(jnp.bfloat16)
-            grid_ref[rows:, b * LANES : (b + 1) * LANES] = out_imag.astype(jnp.bfloat16)
-
-    def scatter(p, carry):
+
+    def spread_class(c):
+        for i in range(parts):
+            columns = jnp.where(
+                lane < tiles, all_cols_ref[4 * i + c], all_cols_ref[4 * i + 2 + c]
+            )
+            k1 = columns % low
+            k2 = columns // low
+            flip = k1 >= kept
+            k1 = jnp.where(flip, low - k1, k1)
+            k2 = jnp.where(flip, wide - 1 - k2, k2)
+            fold_ref[0, pl.ds(c * parts + i, 1), :] = (k1 * wide + k2).astype(jnp.float32)
+            fold_ref[1, pl.ds(c * parts + i, 1), :] = jnp.where(flip, -1.0, 1.0)
+        chunk = 4 * LANES
+        for j in range(class_tiles // chunk):
+            n = chunk // tiles
+            some = [block_ref[2 * (j * n + i) + c] for i in range(n)]
+            both = nt_dot(turn_ref[...], jnp.concatenate(some, axis=0))
+            for i in range(chunk // LANES):
+                b = c * parts + j * (chunk // LANES) + i
+                at = pl.ds(pl.multiple_of(b * LANES, LANES), LANES)
+                real = both[:rows, i * LANES : (i + 1) * LANES]
+                imag = both[rows:, i * LANES : (i + 1) * LANES]
+                sign = fold_ref[1, pl.ds(b, 1), :]
+                out_real = real * phase_ref[0] - imag * phase_ref[1]
+                out_imag = (real * phase_ref[1] + imag * phase_ref[0]) * sign
+                grid_ref[:rows, at] = out_real.astype(jnp.bfloat16)
+                grid_ref[rows:, at] = out_imag.astype(jnp.bfloat16)
+
+    def folded_class(c, p):
         base = pl.multiple_of(p * 2 * wide, 2 * wide)
         row = (lax.broadcasted_iota(jnp.int32, (2 * wide, LANES), 0) + base).astype(jnp.float32)
-        for i in range(total_tiles // LANES):
-            hit = row == fold_ref[0, i : i + 1, :]
-            hot_ref[pl.ds(base, 2 * wide), i * LANES : (i + 1) * LANES] = jnp.where(
-                hit, 1.0, 0.0
-            ).astype(jnp.bfloat16)
-        folded = nt_dot(grid_ref[...], hot_ref[pl.ds(base, 2 * wide), :]).astype(jnp.bfloat16)
+        hots = []
+        for i in range(parts):
+            hit = row == fold_ref[0, pl.ds(c * parts + i, 1), :]
+            hots.append(jnp.where(hit, 1.0, 0.0).astype(jnp.bfloat16))
+        hot = jnp.concatenate(hots, axis=1)
+        at = pl.ds(pl.multiple_of(c * class_tiles, class_tiles), class_tiles)
+        hot_ref[pl.ds(base, 2 * wide), at] = hot
+        return nt_dot(grid_ref[:, at], hot)
+
+    spread_class(core)
+
+    def scatter_own(p, carry):
+        total_ref[p] = folded_class(core, p)
+        return carry
+
+    lax.fori_loop(0, (kept + 1) // 2, scatter_own, 0)
+    for i in range(groups):
+        got(2 * i + 1 - core)
+    spread_class(1 - core)
+
+    def scatter(p, carry):
+        folded = (total_ref[p] + folded_class(1 - core, p)).astype(jnp.bfloat16)
         for e in range(2):
             here = slice(e * wide, (e + 1) * wide)
             pair = jnp.concatenate([folded[:rows, here], folded[rows:, here]], axis=1)
@@ -672,7 +731,6 @@
         return carry
 
     lax.fori_loop(0, (kept + 1) // 2, scatter, 0)
-    loads[6].wait()
 
     def strip(i, carry):
         at = pl.ds(pl.multiple_of(i * 8, 8), 8)
@@ -709,8 +767,6 @@
         return carry
 
     lax.fori_loop(0, rows // 8, strip, 0)
-    store = pltpu.make_async_copy(sky_ref, image_hbm, load_sem.at[len(loads)])
-    store.start()
     top = remote(
         extrap_ref.at[:, pl.ds(0, 8), :],
         extrap_ref.at[:, pl.ds(rows, 8), :],
@@ -719,7 +775,7 @@
         ident(before),
     )
     top.start()
-    loads[7].wait()
+    loads[8].wait()
 
     def spectrum(k, carry):
         out = taps_dot(half_ref[k], fwd_ref)
@@ -734,10 +790,12 @@
     lax.fori_loop(0, kept, spectrum, 0)
 
     def sends(to):
-        at = pl.ds(pl.multiple_of(to * tiles, tiles), tiles)
+        order = to % 2 * groups + to // 2
+        at = pl.ds(pl.multiple_of(order * tiles, tiles), tiles)
+        unit = unit_ref.at[order // 2]
         return [
             remote(picked_ref.at[at, :], got_ref.at[me], send_p.at[to], recv_p.at[me], ident(to)),
-            remote(unit_ref.at[to // 2], units_ref.at[me], send_u.at[to], recv_u.at[me], ident(to)),
+            remote(unit, units_ref.at[me], send_u.at[to], recv_u.at[me], ident(to)),
         ]
 
     def arrivals(origin):
@@ -751,8 +809,9 @@
 
     def pick(s, carry):
         half = levels // 2
-        to_z = (z // half + 1 + s // levels) % 2 * half + s // 2 % half
-        j = (x + 1 + s) % 2 * levels + to_z
+        to_class, to_x = (core + s) % 2, (x + 1 + s // 2) % 2
+        spot = to_x * 2 + (z // half + 1 + s // 4) % 2
+        j = to_class * 4 + spot
         at = pl.multiple_of(j * 2 * LANES, 2 * LANES)
         hot = hot_ref[: kept * wide, pl.ds(at, 2 * LANES)]
         both = nn_dot(spec_ref[...], hot) + nn_dot(rest_ref[...], hot)
@@ -768,7 +827,7 @@
             to = pl.ds(pl.multiple_of(at + h * LANES, LANES), LANES)
             picked_ref[to, :] = packed.T
         for i in range(4):
-            to = j * 4 + i
+            to = (spot * 4 + i) * 2 + to_class
 
             @pl.when(to != me)
             def _():
@@ -778,11 +837,12 @@
         return carry
 
     lax.fori_loop(0, devices // 4, pick, 0)
-    got_ref[me] = picked_ref[pl.ds(pl.multiple_of(me * tiles, tiles), tiles), :]
-    units_ref[me] = unit_ref[me // 2]
+    order = core * groups + me // 2
+    got_ref[me] = picked_ref[pl.ds(pl.multiple_of(order * tiles, tiles), tiles), :]
+    units_ref[me] = unit_ref[order // 2]
     top.wait()
-    loads[8].wait()
     loads[9].wait()
+    loads[10].wait()
 
     def rows_down(i, carry):
         for k in range(half_rows // 8):
@@ -810,8 +870,8 @@
 
     absolute = lax.fori_loop(0, low // 2, cols_down, jnp.zeros((half_rows, LANES), jnp.float32))
     abs_total = jnp.sum(jnp.sum(absolute, axis=0, keepdims=True), axis=1, keepdims=True)
-    loads[10].wait()
     loads[11].wait()
+    loads[12].wait()
 
     def landed(k, carry):
         for copy in arrivals((me + k) % devices):
@@ -822,7 +882,7 @@
 
     units = jnp.concatenate([units_ref[d] for d in range(devices)], axis=0)
     units = jnp.concatenate([units] * (LANES // devices), axis=0).T
-    column_ref[...] = jnp.where(core == 0, units[:tiles], units[tiles:])
+    column_ref[...] = jnp.where(y == 0, units[:tiles], units[tiles:])
 
     def finish(i, carry):
         here = pl.ds(pl.multiple_of(i * 8, 8), 8)
@@ -869,26 +929,34 @@
             total = out if total is None else total + out
         pieces.append(total.astype(jnp.bfloat16))
     tile = nn_dot(jnp.concatenate(pieces, axis=1), order_ref[...]).astype(jnp.bfloat16)
-    piece = kernels_ref.shape[1]
     first, second = [], []
+    near_row = pair_row % 2 == 0
     for i in range(tiles // count):
         here = tile[i * count : (i + 1) * count]
         pair = jnp.concatenate([here[:, :piece], here[:, piece:]], axis=0)
         out = nt_dot(pair, kernels_ref[i * span : (i + 1) * span, :])
-        first.append(jnp.sum(jnp.where(mine, out[:count], 0.0), axis=0, keepdims=True))
-        second.append(jnp.sum(jnp.where(mine, out[count:], 0.0), axis=0, keepdims=True))
+        for found, half in ((first, out[:count]), (second, out[count:])):
+            total = 0.0
+            for k in range(count // 2):
+                total = total + jnp.where(
+                    pair_row // 2 == k, half[:, k * LANES : (k + 1) * LANES], 0.0
+                )
+            found.append(jnp.where(near_row, total, pltpu.roll(total, LANES // 2, 1)))
     first = jnp.concatenate(first, axis=0)
     second = jnp.concatenate(second, axis=0)
-    visits = span // count // 2
-    lane = lax.broadcasted_iota(jnp.int32, first.shape, 1) // visits % 2
+    visits = state_ref.shape[2]
+    lane = lax.broadcasted_iota(jnp.int32, first.shape, 1)
     crossed = jnp.where(
-        lane == 0, -pltpu.roll(second, span - visits, 1), pltpu.roll(second, visits, 1)
+        lane // visits % 2 == 0,
+        -pltpu.roll(second, LANES - visits, 1),
+        pltpu.roll(second, visits, 1),
     )
-    live = vis_ref[2]
-    residual = live * (vis_ref[0] + first + crossed - vis_ref[1])
-    residual_ref[...] = residual
+    keep = jnp.where(lane < 2 * visits, live, 0.0)
+    state_wide = jnp.concatenate(state + state, axis=1)
+    data_wide = jnp.concatenate(data + data, axis=1)
+    residual = keep * (state_wide + first + crossed - data_wide)
     norms = []
-    for values in (residual, vis_ref[1] * live):
+    for values in (residual, data_wide * keep):
         norms.append(jnp.sum(jnp.sum(values * values, axis=0, keepdims=True), axis=1, keepdims=True))
     lane = lax.broadcasted_iota(jnp.int32, (1, LANES), 1)
     row = jnp.where(lane == 0, abs_total, jnp.where(lane == 1, norms[0], norms[1]))
@@ -903,7 +971,6 @@
     lax.fori_loop(1, devices, share, 0)
     for copy in started:
         copy.wait_send()
-    store.wait()
 
     def shared(k, total):
         other = (me + k) % devices
@@ -915,7 +982,20 @@
     total = all_sums_ref[0]
     for d in range(1, devices):
         total = total + all_sums_ref[d]
-    sums_ref[...] = total
+    threshold = 0.5 * total[:, 0:1] / (width * width)
+    size = jnp.sqrt(total[:, 1:2] + 1e-06)
+    radius = 0.5 * jnp.sqrt(total[:, 2:3] + 1e-06)
+    residual = residual * (1.0 - jnp.minimum(1.0, radius / size))
+    vis_out_ref[:, 0, :] = residual[:, :visits]
+    vis_out_ref[:, 1, :] = residual[:, visits : 2 * visits]
+
+    def clip(i, carry):
+        at = pl.ds(pl.multiple_of(i * LANES, LANES), LANES)
+        for c in range(4):
+            merged_ref[c, :, at] = jnp.clip(merged_ref[c, :, at], -threshold, threshold)
+        return carry
+
+    lax.fori_loop(0, half_width // LANES, clip, 0)
 
     def sent(k, carry):
         to = (me + k) % devices
@@ -928,9 +1008,10 @@
     lax.fori_loop(1, devices, sent, 0)
 
 
-def step(kernels, coef, sky, weights, cols, vis, me, groups, slots, devices):
+def step(kernels, coef, sky, state, data, tile_rows, tile_counts, groups, devices):
     rows, width = sky.shape
     piece = kernels.shape[1]
+    slots = tile_rows.shape[1]
     tiles = groups * slots
     half_rows, half_width = coef.shape[1:]
     low = width // LANES
@@ -944,12 +1025,8 @@
     following = np.zeros((LANES, 2 * LANES))
     following[:6] = matrix[2 * LANES :]
     turn = np.arange(piece)
-    angle = (me * rows + jnp.arange(rows, dtype=jnp.int32))[:, None] * turn[None, :] % width
-    angle = (2.0 * math.pi / width) * angle.astype(jnp.float32)
-    cosine, sine = jnp.cos(angle), jnp.sin(angle)
-    turn = jnp.concatenate(
-        [jnp.concatenate([cosine, -sine], axis=1), jnp.concatenate([sine, cosine], axis=1)]
-    ).astype(jnp.bfloat16)
+    base = 2 * np.pi * np.arange(rows)[:, None] * turn[None, :] / width
+    spin = 2 * np.pi * (np.arange(devices)[:, None] * turn[None, :] % devices) / devices
     owner = wide // slots % groups
     shift = 2 * np.pi * (np.arange(rows)[:, None] * owner[None, :] % groups) / groups
     phase = np.stack([np.cos(shift), np.sin(shift)])
@@ -975,7 +1052,8 @@
         sky,
         jnp.stack(table_pair(up)),
         jnp.stack(table_pair(edge.reshape(2 * LANES, LANES))),
-        turn,
+        f32(np.stack([np.cos(base), np.sin(base)])),
+        f32(np.stack([np.cos(spin), np.sin(spin)])),
         bf16(inverse),
         jnp.stack(table_pair(forward)),
         jnp.stack(table_pair(matrix[: 2 * LANES])),
@@ -984,9 +1062,10 @@
         bf16(order),
     ]
     held = [
-        weights,
-        cols,
-        vis,
+        state,
+        data,
+        tile_rows,
+        tile_counts,
         f32(phase),
         f32(phase[:, :, :tiles].transpose(0, 2, 1)),
         f32(np.stack([np.cos(twist), np.sin(twist)])),
@@ -1001,20 +1080,20 @@
         out_shape=(
             jax.ShapeDtypeStruct((rows, width), jnp.float32),
             jax.ShapeDtypeStruct(coef.shape, jnp.float32),
-            jax.ShapeDtypeStruct(vis.shape[1:], jnp.float32),
-            jax.ShapeDtypeStruct((1, LANES), jnp.float32),
+            jax.ShapeDtypeStruct(state.shape, jnp.float32),
         ),
         in_specs=[anywhere] * len(loaded) + [whole] * len(held),
-        out_specs=(anywhere, whole, whole, whole),
-        scratch_shapes=buffers[:1]
-        + [buffers[1]]
-        + buffers[2:]
+        out_specs=(whole, whole, whole),
+        scratch_shapes=buffers[:2]
+        + buffers[3:]
         + [
-            dma((len(loaded) + 1,)),
+            dma((len(loaded),)),
             pltpu.VMEM((16, half_width), jnp.float32),
             pltpu.VMEM((16, half_width), jnp.float32),
             pltpu.VMEM((devices, tiles, 2 * piece), jnp.bfloat16),
-            pltpu.VMEM((devices,) + cols.shape, jnp.int32),
+            pltpu.VMEM((devices, 1, LANES), jnp.int32),
+            pltpu.VMEM((2 * rows, 2 * piece), jnp.bfloat16),
+            pltpu.VMEM(((kept + 1) // 2, 2 * rows, 2 * LANES), jnp.float32),
             pltpu.VMEM((low, rows, LANES), jnp.float32),
             pltpu.VMEM((low, rows, LANES), jnp.float32),
             pltpu.VMEM((2, devices // 2, LANES), jnp.float32),
@@ -1044,38 +1123,20 @@
 
 
 def fast_local(sky_image, coef_dual, vis_dual, visibilities, kernel_blocks, tile_rows, tile_counts):
-    bands = lax.axis_size("band")
     groups = lax.axis_size("vis")
-    devices = bands * groups
-    me = lax.axis_index(everywhere)
-    kernel_here = kernel_blocks[0, 0]
-    slots = tile_rows.shape[3]
-    rows_dev, width = sky_image.shape
-    piece = width // groups
-    stripe = width // bands
-    tiles = groups * slots
-    live_slots = (
-        jnp.arange(slots, dtype=jnp.int32)[None, :] < tile_counts[0, 0][:, None]
-    ).astype(jnp.float32)[:, :, None, None]
-    vis_data = visibilities[0, 0]
-    vis_state = vis_dual[0, 0]
-    columns_here = (tile_rows[0, 0] + lax.axis_index("band") * stripe).reshape(1, tiles)
-    columns_here = jnp.concatenate([columns_here, columns_here], axis=1)
-    weights = live_slots * vis_state
-    weights = jnp.stack([weights, jnp.stack([weights[:, :, 1], -weights[:, :, 0]], axis=2)])
-    weights = weights.reshape(2, tiles // 16, -1)
-    kernels = kernel_here.reshape(-1, piece)
-    vis_rows = (tiles // 16, kernels.shape[0] * 16 // tiles)
-    live = jnp.broadcast_to(live_slots, vis_state.shape)
-    vis = jnp.stack([vis_state, vis_data, live]).reshape((3,) + vis_rows)
-    new_image, merged, residual, sums = step(
-        kernels, coef_dual, sky_image, weights, columns_here, vis, me, groups, slots, devices
+    devices = lax.axis_size("band") * groups
+    taken = kernel_blocks.shape
+    new_image, coef_dual, vis_state = step(
+        kernel_blocks.reshape(-1, taken[-1]),
+        coef_dual,
+        sky_image,
+        vis_dual.reshape((-1,) + vis_dual.shape[4:]),
+        visibilities.reshape((-1,) + vis_dual.shape[4:]),
+        tile_rows[0, 0],
+        tile_counts[0],
+        groups,
+        devices,
     )
-    threshold = 0.5 * sums[0, 0] / (width * width)
-    coef_dual = jnp.clip(merged, -threshold, threshold)
-    radius = 0.5 * jnp.sqrt(sums[0, 2] + 1e-06)
-    size_value = jnp.sqrt(sums[0, 1] + 1e-06)
-    vis_state = residual * (1.0 - jnp.minimum(1.0, radius / size_value))
     return (new_image, coef_dual, vis_state.reshape(vis_dual.shape))
 
 

time: 101 us -> 87.5 us (0.87)
  other arithmetic: 9.09 us -> 0 us
  Pallas kernels: 83.1 us -> 80.1 us
  between operations: 2.75 us -> 0.65 us
    unnamed x5 -> x7, local copies, waits for them, and re-layouts: 1.33 us -> 5.22 us
    min x1 -> x0, other arithmetic: 3.38 us -> none  [fast_local(): coef_dual = jnp.clip(merged, -threshold, threshold)]
    pallas_call x1, Pallas kernels: 83.1 us -> 80.1 us  [step(): pl.pallas_call(lambda *refs: step_kernel(low, *refs), out_shape=(jax.Shap...]
    another operation x4 -> x0, other arithmetic: 1.94 us -> none  [the longest x1 0.64 us: fast_local(): vis = jnp.stack([vis_state, vis_data, live]).reshape((3,) + vis_rows)]
    slice x1 -> x0, local copies, waits for them, and re-layouts: 1.34 us -> none  [fast_local(): size_value = jnp.sqrt(sums[0, 1] + 1e-06)]
    concatenate x2 -> x0, other arithmetic: 1.32 us -> none  [the longest x1 0.72 us: step(): jnp.concatenate([jnp.concatenate([cosine, -sine], axis=1), jnp.concatenat...]
    another operation x2 -> x0, local copies, waits for them, and re-layouts: 1.09 us -> none  [the longest x1 0.97 us: fast_local(): vis = jnp.stack([vis_state, vis_data, live]).reshape((3,) + vis_rows)]
where the time goes in v3:
time: 87.5 us; the launch traced here: 87.3 us
  Pallas kernels  80.1 us (92%)
  local copies, waits for them, and re-layouts  6.57 us (8%)
    pallas_call x1, Pallas kernels, step(): pl.pallas_call(lambda *refs: step_kernel(low, *refs), out_shape=(jax.Shap...  80.1 us
    unnamed x7, local copies, waits for them, and re-layouts  5.22 us

profile of v3, /device:TPU:0, one launch (start us, length us, event | category | flops | bytes accessed | tf_op | source)
XLA Modules:
  0.0 87.3 jit_solution(13270201628505064492)
XLA Ops:
  0.6 1.4 %copy.29.refs_15_ = s32[16,4]{1,0:T(8,128)} copy(s32[16,4]{0,1:T(4,128)} %bitcast.10) | data formatting | bytes 512 | tf_op jit(solution)/shard_map/squeeze | solution.py:1135
  2.0 80.1 %step.1 = (f32[128,4096]{1,0:T(8,128)}, f32[4,64,2048]{2,1,0:T(8,128)}, f32[64,2,32]{2,1,0:T(2,128)}) custom-call(bf16[4096,256]{1,0:T(8,128)(2,1)} %bitcast.6, f32[4,64,2048]{2,1,0:T(8,128)} %refs_1_.1, f32[128,4096]{1,0:T(8,128)} %refs_2_.1, bf16[2,256,256]{2,1,0:T(8,128)(2,1)} %constant.50.refs_3_, bf16[2,256,128]{2,1,0:T(8,128)(2,1)} %constant.57.refs_4_, ...), custom_call_target="tpu_custom_call" | custom-call | tf_op jit(solution)/shard_map/step/pallas_call | solution.py:1078
  82.1 0.0 copy-start
  82.1 3.3 %copy.33 = f32[128,4096]{1,0:T(8,128)} copy(f32[128,4096]{1,0:T(8,128)} %get-tuple-element.12) | data formatting | bytes 4194304
  85.4 0.0 copy-done
  85.4 0.0 copy-start.1
  85.4 1.3 %copy.34 = f32[4,64,2048]{2,1,0:T(8,128)} copy(f32[4,64,2048]{2,1,0:T(8,128)S(1)} %copy-done) | data formatting | bytes 4194304
  86.7 0.0 copy-done.1
  86.7 0.6 copy.35
Async XLA Ops:
  82.1 3.3 %copy-start = (f32[4,64,2048]{2,1,0:T(8,128)S(1)}, f32[4,64,2048]{2,1,0:T(8,128)}, u32[]{:S(2)}) copy-start(f32[4,64,2048]{2,1,0:T(8,128)} %get-tuple-element.13) | copy-start | bytes 6291460
  85.4 1.3 %copy-start.1 = (f32[64,2,32]{2,1,0:T(2,128)S(1)}, f32[64,2,32]{2,1,0:T(2,128)}, u32[]{:S(2)}) copy-start(f32[64,2,32]{2,1,0:T(2,128)} %get-tuple-element.8) | copy-start | bytes 49156

commit v4 on v3

--- a/solution.py
+++ b/solution.py
@@ -424,11 +424,13 @@
     phase_ref,
     shift_ref,
     tw_ref,
-    sky_ref,
-    merged_ref,
+    image_hbm,
+    coef_out_hbm,
     vis_out_ref,
     kernels_ref,
     joined_ref,
+    sky_ref,
+    merged_ref,
     up_ref,
     edge_ref,
     base_ref,
@@ -461,6 +463,7 @@
     units_ref,
     mid_ref,
     column_ref,
+    all_abs_ref,
     all_sums_ref,
     send_a,
     send_b,
@@ -470,6 +473,8 @@
     send_u,
     recv_p,
     recv_u,
+    send_t,
+    recv_t,
     send_s,
     recv_s,
     halo_sem,
@@ -538,7 +543,7 @@
     span = kernels_ref.shape[0] * count // tiles
     width = low * wide
     stripe = width // 2
-    slots = rows_ref.shape[1]
+    slots = rows_ref.shape[0]
     lane = lax.broadcasted_iota(jnp.int32, (tiles, groups), 1)
     tile_id = lax.broadcasted_iota(jnp.int32, (tiles, groups), 0)
     counts = jnp.where(lane == tile_id // slots, counts_ref[...].astype(jnp.float32), 0.0)
@@ -567,8 +572,9 @@
     lane = lax.broadcasted_iota(jnp.int32, (groups, LANES), 1) % tiles
     owner = lax.broadcasted_iota(jnp.int32, (groups, LANES), 0)
     columns = 0.0
+    by_owner = rows_ref[...].astype(jnp.float32).T
     for slot in range(slots):
-        here = rows_ref[:, slot : slot + 1].astype(jnp.float32)
+        here = by_owner[:, slot : slot + 1]
         columns = columns + jnp.where(lane == owner * slots + slot, here, 0.0)
     columns = jnp.sum(columns, axis=0, keepdims=True).astype(jnp.int32)
     all_cols_ref[me] = columns + x * stripe
@@ -767,6 +773,8 @@
         return carry
 
     lax.fori_loop(0, rows // 8, strip, 0)
+    store = pltpu.make_async_copy(sky_ref, image_hbm, load_sem.at[len(loads)])
+    store.start()
     top = remote(
         extrap_ref.at[:, pl.ds(0, 8), :],
         extrap_ref.at[:, pl.ds(rows, 8), :],
@@ -794,18 +802,28 @@
         at = pl.ds(pl.multiple_of(order * tiles, tiles), tiles)
         unit = unit_ref.at[order // 2]
         return [
-            remote(picked_ref.at[at, :], got_ref.at[me], send_p.at[to], recv_p.at[me], ident(to)),
-            remote(unit, units_ref.at[me], send_u.at[to], recv_u.at[me], ident(to)),
+            remote(picked_ref.at[at, :], got_ref.at[me], send_p.at[0], recv_p.at[0], ident(to)),
+            remote(unit, units_ref.at[me], send_u.at[0], recv_u.at[0], ident(to)),
         ]
 
-    def arrivals(origin):
-        at = pl.ds(0, tiles)
-        return [
-            remote(
-                picked_ref.at[at, :], got_ref.at[origin], send_p.at[0], recv_p.at[origin], twin
-            ),
-            remote(unit_ref.at[0], units_ref.at[origin], send_u.at[0], recv_u.at[origin], twin),
-        ]
+    others = pl.ds(0, devices - 1)
+
+    def total_of(ref, send, recv):
+        return remote(ref.at[others], ref.at[others], send.at[0], recv.at[0], twin)
+
+    def share_row(ref, send, recv):
+        def one(k, carry):
+            to = (me + k) % devices
+            remote(ref.at[me], ref.at[me], send.at[0], recv.at[0], ident(to)).start()
+            return carry
+
+        lax.fori_loop(1, devices, one, 0)
+
+    def row_total(ref):
+        total = ref[0]
+        for d in range(1, devices):
+            total = total + ref[d]
+        return total
 
     def pick(s, carry):
         half = levels // 2
@@ -873,12 +891,11 @@
     loads[11].wait()
     loads[12].wait()
 
-    def landed(k, carry):
-        for copy in arrivals((me + k) % devices):
-            copy.wait_recv()
-        return carry
-
-    lax.fori_loop(1, devices, landed, 0)
+    lane = lax.broadcasted_iota(jnp.int32, (1, LANES), 1)
+    all_abs_ref[me] = jnp.where(lane == 0, abs_total, 0.0)
+    share_row(all_abs_ref, send_t, recv_t)
+    total_of(got_ref, send_p, recv_p).wait_recv()
+    total_of(units_ref, send_u, recv_u).wait_recv()
 
     units = jnp.concatenate([units_ref[d] for d in range(devices)], axis=0)
     units = jnp.concatenate([units] * (LANES // devices), axis=0).T
@@ -959,35 +976,10 @@
     for values in (residual, data_wide * keep):
         norms.append(jnp.sum(jnp.sum(values * values, axis=0, keepdims=True), axis=1, keepdims=True))
     lane = lax.broadcasted_iota(jnp.int32, (1, LANES), 1)
-    row = jnp.where(lane == 0, abs_total, jnp.where(lane == 1, norms[0], norms[1]))
-    all_sums_ref[me] = row
-
-    def share(k, carry):
-        to = (me + k) % devices
-        own = all_sums_ref.at[me]
-        remote(own, own, send_s.at[to], recv_s.at[me], ident(to)).start()
-        return carry
-
-    lax.fori_loop(1, devices, share, 0)
-    for copy in started:
-        copy.wait_send()
-
-    def shared(k, total):
-        other = (me + k) % devices
-        own = all_sums_ref.at[other]
-        remote(own, own, send_s.at[other], recv_s.at[other], twin).wait_recv()
-        return total
-
-    lax.fori_loop(1, devices, shared, 0)
-    total = all_sums_ref[0]
-    for d in range(1, devices):
-        total = total + all_sums_ref[d]
-    threshold = 0.5 * total[:, 0:1] / (width * width)
-    size = jnp.sqrt(total[:, 1:2] + 1e-06)
-    radius = 0.5 * jnp.sqrt(total[:, 2:3] + 1e-06)
-    residual = residual * (1.0 - jnp.minimum(1.0, radius / size))
-    vis_out_ref[:, 0, :] = residual[:, :visits]
-    vis_out_ref[:, 1, :] = residual[:, visits : 2 * visits]
+    all_sums_ref[me] = jnp.where(lane == 0, norms[0], norms[1])
+    share_row(all_sums_ref, send_s, recv_s)
+    total_of(all_abs_ref, send_t, recv_t).wait_recv()
+    threshold = 0.5 * row_total(all_abs_ref)[:, 0:1] / (width * width)
 
     def clip(i, carry):
         at = pl.ds(pl.multiple_of(i * LANES, LANES), LANES)
@@ -996,22 +988,28 @@
         return carry
 
     lax.fori_loop(0, half_width // LANES, clip, 0)
-
-    def sent(k, carry):
-        to = (me + k) % devices
-        for copy in sends(to):
-            copy.wait_send()
-        own = all_sums_ref.at[me]
-        remote(own, own, send_s.at[to], recv_s.at[me], ident(to)).wait_send()
-        return carry
-
-    lax.fori_loop(1, devices, sent, 0)
+    store_coef = pltpu.make_async_copy(merged_ref, coef_out_hbm, load_sem.at[len(loads) + 1])
+    store_coef.start()
+    for copy in started:
+        copy.wait_send()
+    total_of(got_ref, send_p, recv_p).wait_send()
+    total_of(units_ref, send_u, recv_u).wait_send()
+    total_of(all_abs_ref, send_t, recv_t).wait_send()
+    total_of(all_sums_ref, send_s, recv_s).wait()
+    total = row_total(all_sums_ref)
+    size = jnp.sqrt(total[:, 0:1] + 1e-06)
+    radius = 0.5 * jnp.sqrt(total[:, 1:2] + 1e-06)
+    residual = residual * (1.0 - jnp.minimum(1.0, radius / size))
+    vis_out_ref[:, 0, :] = residual[:, :visits]
+    vis_out_ref[:, 1, :] = residual[:, visits : 2 * visits]
+    store.wait()
+    store_coef.wait()
 
 
 def step(kernels, coef, sky, state, data, tile_rows, tile_counts, groups, devices):
     rows, width = sky.shape
     piece = kernels.shape[1]
-    slots = tile_rows.shape[1]
+    slots = tile_rows.shape[0]
     tiles = groups * slots
     half_rows, half_width = coef.shape[1:]
     low = width // LANES
@@ -1074,7 +1072,7 @@
     buffers[1] = pltpu.VMEM((4, half_rows + 8, half_width), jnp.float32)
     copies = 3 * 4 + 7 + 12
     dma = pltpu.SemaphoreType.DMA
-    anywhere = pl.BlockSpec(memory_space=pl.ANY)
+    anywhere = pl.BlockSpec(memory_space=pltpu.HBM)
     return pl.pallas_call(
         lambda *refs: step_kernel(low, *refs),
         out_shape=(
@@ -1083,11 +1081,12 @@
             jax.ShapeDtypeStruct(state.shape, jnp.float32),
         ),
         in_specs=[anywhere] * len(loaded) + [whole] * len(held),
-        out_specs=(whole, whole, whole),
-        scratch_shapes=buffers[:2]
+        out_specs=(anywhere, anywhere, whole),
+        scratch_shapes=buffers[:3]
+        + [pltpu.VMEM(coef.shape, jnp.float32)]
         + buffers[3:]
         + [
-            dma((len(loaded),)),
+            dma((len(loaded) + 2,)),
             pltpu.VMEM((16, half_width), jnp.float32),
             pltpu.VMEM((16, half_width), jnp.float32),
             pltpu.VMEM((devices, tiles, 2 * piece), jnp.bfloat16),
@@ -1110,13 +1109,15 @@
             pltpu.VMEM((devices, tiles, 2 * rows), jnp.float32),
             pltpu.VMEM((tiles, LANES), jnp.float32),
             pltpu.VMEM((devices, 1, LANES), jnp.float32),
+            pltpu.VMEM((devices, 1, LANES), jnp.float32),
             dma((copies,)),
             dma((copies,)),
         ]
-        + [dma((devices,))] * 8
+        + [dma((devices,))] * 2
+        + [dma((1,))] * 8
         + [dma((4,))],
         compiler_params=pltpu.CompilerParams(
-            collective_id=0, has_side_effects=True, vmem_limit_bytes=58 * 2**20
+            collective_id=0, has_side_effects=True, vmem_limit_bytes=60 * 2**20
         ),
         name="step",
     )(*loaded, *held)
@@ -1132,7 +1133,7 @@
         sky_image,
         vis_dual.reshape((-1,) + vis_dual.shape[4:]),
         visibilities.reshape((-1,) + vis_dual.shape[4:]),
-        tile_rows[0, 0],
+        tile_rows[0, 0].T,
         tile_counts[0],
         groups,
         devices,

time: 87.5 us -> 81.4 us (0.930)
  Pallas kernels: 80.1 us -> 75.4 us
  local copies, waits for them, and re-layouts: 6.57 us -> 5.22 us
    pallas_call x1, Pallas kernels: 80.1 us -> 75.4 us  [step(): pl.pallas_call(lambda *refs: step_kernel(low, *refs), out_shape=(jax.Shap...]
    squeeze x1 -> x0, local copies, waits for them, and re-layouts: 1.36 us -> none  [fast_local(): tile_rows[0, 0]]
where the time goes in v4:
time: 81.4 us; the launch traced here: 81.2 us
  Pallas kernels  75.4 us (93%)
  local copies, waits for them, and re-layouts  5.22 us (6%)
    pallas_call x1, Pallas kernels, step(): pl.pallas_call(lambda *refs: step_kernel(low, *refs), out_shape=(jax.Shap...  75.4 us
    unnamed x7, local copies, waits for them, and re-layouts  5.22 us

profile of v4, /device:TPU:0, one launch (start us, length us, event | category | flops | bytes accessed | tf_op | source)
XLA Modules:
  0.0 81.2 jit_solution(8378986518679528934)
XLA Ops:
  0.6 75.4 %step.1 = (f32[128,4096]{1,0:T(8,128)}, f32[4,64,2048]{2,1,0:T(8,128)}, f32[64,2,32]{2,1,0:T(2,128)}) custom-call(bf16[4096,256]{1,0:T(8,128)(2,1)} %bitcast.8, f32[4,64,2048]{2,1,0:T(8,128)} %refs_1_.1, f32[128,4096]{1,0:T(8,128)} %refs_2_.1, bf16[2,256,256]{2,1,0:T(8,128)(2,1)} %constant.50.refs_3_, bf16[2,256,128]{2,1,0:T(8,128)(2,1)} %constant.57.refs_4_, ...), custom_call_target="tpu_custom_call" | custom-call | tf_op jit(solution)/shard_map/step/pallas_call | solution.py:1076
  76.0 0.0 copy-start
  76.0 3.3 %copy.32 = f32[128,4096]{1,0:T(8,128)} copy(f32[128,4096]{1,0:T(8,128)} %get-tuple-element.12) | data formatting | bytes 4194304
  79.3 0.0 copy-done
  79.3 0.0 copy-start.1
  79.3 1.3 %copy.33 = f32[4,64,2048]{2,1,0:T(8,128)} copy(f32[4,64,2048]{2,1,0:T(8,128)S(1)} %copy-done) | data formatting | bytes 4194304
  80.6 0.0 copy-done.1
  80.6 0.6 copy.34
Async XLA Ops:
  76.0 3.3 %copy-start = (f32[4,64,2048]{2,1,0:T(8,128)S(1)}, f32[4,64,2048]{2,1,0:T(8,128)}, u32[]{:S(2)}) copy-start(f32[4,64,2048]{2,1,0:T(8,128)} %get-tuple-element.13) | copy-start | bytes 6291460
  79.3 1.3 %copy-start.1 = (f32[64,2,32]{2,1,0:T(2,128)S(1)}, f32[64,2,32]{2,1,0:T(2,128)}, u32[]{:S(2)}) copy-start(f32[64,2,32]{2,1,0:T(2,128)} %get-tuple-element.8) | copy-start | bytes 49156

commit v5 on v4

--- a/solution.py
+++ b/solution.py
@@ -415,7 +415,8 @@
     fwd_hbm,
     near_hbm,
     next_hbm,
-    last_hbm,
+    half_base_hbm,
+    half_spin_hbm,
     order_hbm,
     state_ref,
     data_ref,
@@ -439,7 +440,8 @@
     fwd_ref,
     near_ref,
     next_ref,
-    last_ref,
+    half_base_ref,
+    half_spin_ref,
     order_ref,
     load_sem,
     tail_ref,
@@ -461,8 +463,13 @@
     unit_ref,
     got_ref,
     units_ref,
-    mid_ref,
-    column_ref,
+    sum_table_ref,
+    terms_ref,
+    own_ref,
+    sums_out_ref,
+    sums_unit_ref,
+    sums_got_ref,
+    sums_units_ref,
     all_abs_ref,
     all_sums_ref,
     send_a,
@@ -473,6 +480,10 @@
     send_u,
     recv_p,
     recv_u,
+    send_z,
+    recv_z,
+    send_w,
+    recv_w,
     send_t,
     recv_t,
     send_s,
@@ -530,7 +541,8 @@
         (fwd_hbm, fwd_ref),
         (near_hbm, near_ref),
         (next_hbm, next_ref),
-        (last_hbm, last_ref),
+        (half_base_hbm, half_base_ref),
+        (half_spin_hbm, half_spin_ref),
         (order_hbm, order_ref),
     ]
     loads = [
@@ -659,6 +671,22 @@
     turn_ref[:rows, piece:] = -sine
     turn_ref[rows:, :piece] = sine
     turn_ref[rows:, piece:] = cosine
+    for load in loads[11:13]:
+        load.wait()
+    for n in range(4):
+        spin_cos, spin_sin = half_spin_ref[0, n : n + 1, :], half_spin_ref[1, n : n + 1, :]
+        cosine = half_base_ref[0] * spin_cos - half_base_ref[1] * spin_sin
+        sine = half_base_ref[1] * spin_cos + half_base_ref[0] * spin_sin
+        for p in range(2):
+            part = slice(p * LANES, (p + 1) * LANES)
+            c, d = split(cosine[:, part]), split(sine[:, part])
+            real_rows = slice(2 * n * rows, (2 * n + 1) * rows)
+            imag_rows = slice((2 * n + 1) * rows, (2 * n + 2) * rows)
+            for e in range(2):
+                sum_table_ref[e, p, real_rows, :LANES] = c[e]
+                sum_table_ref[e, p, real_rows, LANES:] = -d[e]
+                sum_table_ref[e, p, imag_rows, :LANES] = d[e]
+                sum_table_ref[e, p, imag_rows, LANES:] = c[e]
     for n, k in enumerate(far):
         for px, py in corners:
             block = index(px, (z + levels - k) % levels, py, core)
@@ -672,11 +700,13 @@
     parts = class_tiles // LANES
     lane = lax.broadcasted_iota(jnp.int32, (1, LANES), 1)
 
+    def block_of(u):
+        return u // 2 % 2 * groups + u // 4 * 4 + u % 2 * 2
+
     def spread_class(c):
         for i in range(parts):
-            columns = jnp.where(
-                lane < tiles, all_cols_ref[4 * i + c], all_cols_ref[4 * i + 2 + c]
-            )
+            first = block_of(2 * i) + c
+            columns = jnp.where(lane < tiles, all_cols_ref[first], all_cols_ref[first + 2])
             k1 = columns % low
             k2 = columns // low
             flip = k1 >= kept
@@ -687,7 +717,7 @@
         chunk = 4 * LANES
         for j in range(class_tiles // chunk):
             n = chunk // tiles
-            some = [block_ref[2 * (j * n + i) + c] for i in range(n)]
+            some = [block_ref[block_of(j * n + i) + c] for i in range(n)]
             both = nt_dot(turn_ref[...], jnp.concatenate(some, axis=0))
             for i in range(chunk // LANES):
                 b = c * parts + j * (chunk // LANES) + i
@@ -797,19 +827,21 @@
 
     lax.fori_loop(0, kept, spectrum, 0)
 
-    def sends(to):
-        order = to % 2 * groups + to // 2
-        at = pl.ds(pl.multiple_of(order * tiles, tiles), tiles)
-        unit = unit_ref.at[order // 2]
+    mate = x * 4 + y * 2 + core
+
+    def sends(to_z, to_x, to_y, to_class):
+        at = to_class * class_tiles + (to_z * 4 + to_x * 2 + to_y) * tiles
+        at = pl.ds(pl.multiple_of(at, tiles), tiles)
+        unit = unit_ref.at[to_class * parts + to_z * 2 + to_x]
+        spot, half, target = to_z * 8 + mate, to_z // 2, device(to_x, z, to_y, to_class)
         return [
-            remote(picked_ref.at[at, :], got_ref.at[me], send_p.at[0], recv_p.at[0], ident(to)),
-            remote(unit, units_ref.at[me], send_u.at[0], recv_u.at[0], ident(to)),
+            remote(picked_ref.at[at, :], got_ref.at[spot], send_p.at[0], recv_p.at[half], target),
+            remote(unit, units_ref.at[spot], send_u.at[0], recv_u.at[half], target),
         ]
 
-    others = pl.ds(0, devices - 1)
-
-    def total_of(ref, send, recv):
-        return remote(ref.at[others], ref.at[others], send.at[0], recv.at[0], twin)
+    def total_of(ref, send, recv, count=devices - 1, at=0):
+        some = ref.at[pl.ds(0, count)]
+        return remote(some, some, send.at[0], recv.at[at], twin)
 
     def share_row(ref, send, recv):
         def one(k, carry):
@@ -825,11 +857,13 @@
             total = total + ref[d]
         return total
 
+    def ordered(n):
+        return (z // 2 + 1 + n // 2) % 2 * 2 + (z + 1 + n) % 2
+
     def pick(s, carry):
-        half = levels // 2
-        to_class, to_x = (core + s) % 2, (x + 1 + s // 2) % 2
-        spot = to_x * 2 + (z // half + 1 + s // 4) % 2
-        j = to_class * 4 + spot
+        to_z = ordered(s // 2)
+        to_class = (core + 1 + s) % 2
+        j = to_class * 4 + to_z
         at = pl.multiple_of(j * 2 * LANES, 2 * LANES)
         hot = hot_ref[: kept * wide, pl.ds(at, 2 * LANES)]
         both = nn_dot(spec_ref[...], hot) + nn_dot(rest_ref[...], hot)
@@ -844,20 +878,22 @@
             packed = level(real * to_level) * 65536 + level(imag * to_level)
             to = pl.ds(pl.multiple_of(at + h * LANES, LANES), LANES)
             picked_ref[to, :] = packed.T
-        for i in range(4):
-            to = (spot * 4 + i) * 2 + to_class
-
-            @pl.when(to != me)
-            def _():
-                for copy in sends(to):
-                    copy.start()
+        for to_x in range(2):
+            for to_y in range(2):
+                away = (to_x - x) * (to_x - x) + (to_y - y) * (to_y - y)
+
+                @pl.when(away + (to_class - core) * (to_class - core) != 0)
+                def _():
+                    for copy in sends(to_z, to_x, to_y, to_class):
+                        copy.start()
 
         return carry
 
     lax.fori_loop(0, devices // 4, pick, 0)
-    order = core * groups + me // 2
-    got_ref[me] = picked_ref[pl.ds(pl.multiple_of(order * tiles, tiles), tiles), :]
-    units_ref[me] = unit_ref[order // 2]
+    for to_z in range(levels):
+        at = core * class_tiles + (to_z * 4 + x * 2 + y) * tiles
+        got_ref[to_z * 8 + mate] = picked_ref[pl.ds(pl.multiple_of(at, tiles), tiles), :]
+        units_ref[to_z * 8 + mate] = unit_ref[core * parts + to_z * 2 + x]
     top.wait()
     loads[9].wait()
     loads[10].wait()
@@ -886,66 +922,103 @@
             merged_ref[c, :, at] = joined_ref[c, 8:, at] + part
         return absolute
 
-    absolute = lax.fori_loop(0, low // 2, cols_down, jnp.zeros((half_rows, LANES), jnp.float32))
+    def plane_sums(n, absolute):
+        half = (z // 2 + 1 + n) % 2
+        total_of(got_ref, send_p, recv_p, 14, half).wait_recv()
+        total_of(units_ref, send_u, recv_u, 14, half).wait_recv()
+        rows_of = [units_ref[half * 16 + i] for i in range(16)]
+        units = jnp.concatenate(rows_of * (LANES // 16), axis=0).T
+        units = jnp.where(y == 0, units[:tiles], units[tiles:])
+        cosine, sine = shift_ref[0], shift_ref[1]
+        level_cos = half_spin_ref[0, pl.ds(4 * z, 1), :]
+        level_sin = half_spin_ref[1, pl.ds(4 * z, 1), :]
+        for e in range(2):
+            strip_rows = slice(e * tiles, (e + 1) * tiles)
+            for pair in range(4):
+                reals, imags = [], []
+                for side in range(2):
+                    m = side * 4 + pair
+                    packed = got_ref[half * 16 + e * 8 + m]
+                    real = (packed + 32768) >> 16
+                    imag = packed - (real << 16)
+                    unit = units[:, e * 8 + m : e * 8 + m + 1]
+                    real = real.astype(jnp.float32) * unit
+                    imag = imag.astype(jnp.float32) * unit
+                    reals.append(real * cosine + imag * sine)
+                    imags.append(imag * cosine - real * sine)
+                at = 2 * pair * LANES
+                for p, values in ((0, (reals[0] + reals[1], imags[0] + imags[1])),
+                                  (1, (reals[0] - reals[1], imags[0] - imags[1]))):
+                    for part in range(2):
+                        upper, lower = split(values[part])
+                        here = slice(at + part * LANES, at + (part + 1) * LANES)
+                        terms_ref[0, p, strip_rows, here] = upper
+                        terms_ref[1, p, strip_rows, here] = lower
+        reals, imags = [], []
+        for p in range(2):
+            out = nn_dot(terms_ref[0, p], sum_table_ref[0, p])
+            out = out + nn_dot(terms_ref[1, p], sum_table_ref[0, p])
+            out = out + nn_dot(terms_ref[0, p], sum_table_ref[1, p])
+            part = slice(p * LANES, (p + 1) * LANES)
+            turn_cos, turn_sin = level_cos[:, part], level_sin[:, part]
+            real, imag = out[:, :LANES], out[:, LANES:]
+            reals.append(real * turn_cos + imag * turn_sin)
+            imags.append(imag * turn_cos - real * turn_sin)
+        real = jnp.concatenate(reals, axis=1)
+        imag = jnp.concatenate(imags, axis=1)
+        most = jnp.max(jnp.maximum(jnp.abs(real), jnp.abs(imag)), axis=1, keepdims=True)
+        most = jnp.maximum(most, 1e-30)
+        to_level = LEVELS / most
+        packed = level(real * to_level) * 65536 + level(imag * to_level)
+        sums_unit_ref[half] = jnp.broadcast_to(most * (1.0 / LEVELS), (LANES, LANES)).T[:1]
+        for e in range(2):
+            strip_rows = slice(e * tiles, (e + 1) * tiles)
+            to_z = half * 2 + e
+            sums_out_ref[to_z] = packed[strip_rows]
+
+            @pl.when(to_z == z)
+            def _():
+                own_ref[:, : 2 * LANES] = real[strip_rows]
+                own_ref[:, 2 * LANES :] = imag[strip_rows]
+
+            @pl.when(to_z != z)
+            def _():
+                target = device(x, to_z, y, core)
+                remote(
+                    sums_out_ref.at[to_z], sums_got_ref.at[z], send_z.at[0], recv_z.at[0], target
+                ).start()
+                remote(
+                    sums_unit_ref.at[half],
+                    sums_units_ref.at[z],
+                    send_w.at[0],
+                    recv_w.at[0],
+                    target,
+                ).start()
+
+        return lax.fori_loop(n * (low // 4), (n + 1) * (low // 4), cols_down, absolute)
+
+    absolute = lax.fori_loop(0, 2, plane_sums, jnp.zeros((half_rows, LANES), jnp.float32))
     abs_total = jnp.sum(jnp.sum(absolute, axis=0, keepdims=True), axis=1, keepdims=True)
-    loads[11].wait()
-    loads[12].wait()
+    loads[13].wait()
 
     lane = lax.broadcasted_iota(jnp.int32, (1, LANES), 1)
     all_abs_ref[me] = jnp.where(lane == 0, abs_total, 0.0)
     share_row(all_abs_ref, send_t, recv_t)
-    total_of(got_ref, send_p, recv_p).wait_recv()
-    total_of(units_ref, send_u, recv_u).wait_recv()
-
-    units = jnp.concatenate([units_ref[d] for d in range(devices)], axis=0)
-    units = jnp.concatenate([units] * (LANES // devices), axis=0).T
-    column_ref[...] = jnp.where(y == 0, units[:tiles], units[tiles:])
-
-    def finish(i, carry):
-        here = pl.ds(pl.multiple_of(i * 8, 8), 8)
-        cosine, sine = shift_ref[0, here, :], shift_ref[1, here, :]
-        reals, imags = [], []
-        for d in range(devices):
-            packed = got_ref[d, here, :]
-            real = (packed + 32768) >> 16
-            imag = packed - (real << 16)
-            unit = column_ref[here, d : d + 1]
-            real = real.astype(jnp.float32) * unit
-            imag = imag.astype(jnp.float32) * unit
-            reals.append(real * cosine + imag * sine)
-            imags.append(imag * cosine - real * sine)
-        even, odd = even_odd(reals)
-        cos_real, sin_real = cos_sums(even, devices), sin_sums(odd, devices)
-        even, odd = even_odd(imags)
-        cos_imag, sin_imag = cos_sums(even, devices), sin_sums(odd, devices)
-        half = devices // 2
-        for k in range(half + 1):
-            if k == 0 or k == half:
-                outs = [(k, cos_real[k], cos_imag[k])]
-            else:
-                outs = [
-                    (k, cos_real[k] + sin_imag[k], cos_imag[k] - sin_real[k]),
-                    (devices - k, cos_real[k] - sin_imag[k], cos_imag[k] + sin_real[k]),
-                ]
-            for t, real, imag in outs:
-                mid_ref[t, here, :rows] = real
-                mid_ref[t, here, rows:] = imag
-        return carry
-
-    lax.fori_loop(0, tiles // 8, finish, 0)
-    group = 2 * LANES // 16
-    lane = lax.broadcasted_iota(jnp.int32, (1, 2 * LANES), 1) // 16
-    pieces = []
-    for g in range(devices // group):
-        total = None
-        for e in range(group):
-            upper, lower = split(mid_ref[g * group + e])
-            out = nn_dot(upper, last_ref[0, g]) + nn_dot(lower, last_ref[0, g])
-            out = out + nn_dot(upper, last_ref[1, g])
-            out = jnp.where(lane == e, out, 0.0)
-            total = out if total is None else total + out
-        pieces.append(total.astype(jnp.bfloat16))
-    tile = nn_dot(jnp.concatenate(pieces, axis=1), order_ref[...]).astype(jnp.bfloat16)
+    total_of(sums_got_ref, send_z, recv_z, levels - 1).wait_recv()
+    total_of(sums_units_ref, send_w, recv_w, levels - 1).wait_recv()
+    units = [sums_units_ref[(z + k) % levels] for k in range(1, levels)]
+    units = jnp.concatenate(units + [units[0]] * (LANES - levels + 1), axis=0).T
+    units = jnp.where(z % 2 == 0, units[:tiles], units[tiles:])
+    real, imag = own_ref[:, : 2 * LANES], own_ref[:, 2 * LANES :]
+    for k in range(1, levels):
+        packed = sums_got_ref[(z + k) % levels]
+        upper = (packed + 32768) >> 16
+        lower = packed - (upper << 16)
+        unit = units[:, k - 1 : k]
+        real = real + upper.astype(jnp.float32) * unit
+        imag = imag + lower.astype(jnp.float32) * unit
+    tile = jnp.concatenate([real, imag], axis=1).astype(jnp.bfloat16)
+    tile = nn_dot(tile, order_ref[...]).astype(jnp.bfloat16)
     first, second = [], []
     near_row = pair_row % 2 == 0
     for i in range(tiles // count):
@@ -992,8 +1065,10 @@
     store_coef.start()
     for copy in started:
         copy.wait_send()
-    total_of(got_ref, send_p, recv_p).wait_send()
-    total_of(units_ref, send_u, recv_u).wait_send()
+    total_of(got_ref, send_p, recv_p, 28).wait_send()
+    total_of(units_ref, send_u, recv_u, 28).wait_send()
+    total_of(sums_got_ref, send_z, recv_z, levels - 1).wait_send()
+    total_of(sums_units_ref, send_w, recv_w, levels - 1).wait_send()
     total_of(all_abs_ref, send_t, recv_t).wait_send()
     total_of(all_sums_ref, send_s, recv_s).wait()
     total = row_total(all_sums_ref)
@@ -1033,17 +1108,12 @@
     inverse = np.block([[c, s], [-s, c]])
     forward = np.block([[c, -s], [s, c]])
     twist = 2 * np.pi * np.arange(kept + 1)[:, None] * wide[None, :] / width
-    each = piece // devices
-    t = np.arange(devices)[:, None] + devices * np.arange(each)[None, :]
-    angle = 2 * np.pi * (np.arange(rows)[:, None, None] * t[None] % width) / width
-    c, s = np.cos(angle), np.sin(angle)
-    last = np.stack([np.stack([c, -s], axis=2), np.stack([s, c], axis=2)])
-    last = last.reshape(2 * rows, -1, 2 * LANES).transpose(1, 0, 2)
+    halves = np.concatenate([turn[0::2], turn[1::2]])
+    half_base = 2 * np.pi * np.arange(rows)[:, None] * halves[None, :] / width
+    half_spin = 2 * np.pi * (np.arange(devices)[:, None] * halves[None, :] % devices) / devices
     order = np.zeros((2 * piece, 2 * piece))
-    for a in range(devices):
-        for part in range(2):
-            for b in range(each):
-                order[(a * 2 + part) * each + b, part * piece + a + devices * b] = 1.0
+    for part in range(2):
+        order[part * piece + np.arange(piece), part * piece + halves] = 1.0
     loaded = [
         kernels,
         coef,
@@ -1056,7 +1126,8 @@
         jnp.stack(table_pair(forward)),
         jnp.stack(table_pair(matrix[: 2 * LANES])),
         jnp.stack(table_pair(following)),
-        jnp.stack(table_pair(last)),
+        f32(np.stack([np.cos(half_base), np.sin(half_base)])),
+        f32(np.stack([np.cos(half_spin), np.sin(half_spin)])),
         bf16(order),
     ]
     held = [
@@ -1106,14 +1177,20 @@
             pltpu.VMEM((devices // 2, 1, LANES), jnp.float32),
             pltpu.VMEM((devices, tiles, rows), jnp.int32),
             pltpu.VMEM((devices, 1, LANES), jnp.float32),
-            pltpu.VMEM((devices, tiles, 2 * rows), jnp.float32),
-            pltpu.VMEM((tiles, LANES), jnp.float32),
+            pltpu.VMEM((2, 2, 8 * rows, 2 * LANES), jnp.bfloat16),
+            pltpu.VMEM((2, 2, 2 * tiles, 8 * rows), jnp.bfloat16),
+            pltpu.VMEM((tiles, 2 * piece), jnp.float32),
+            pltpu.VMEM((groups // 4, tiles, piece), jnp.int32),
+            pltpu.VMEM((2, 1, LANES), jnp.float32),
+            pltpu.VMEM((groups // 4, tiles, piece), jnp.int32),
+            pltpu.VMEM((groups // 4, 1, LANES), jnp.float32),
             pltpu.VMEM((devices, 1, LANES), jnp.float32),
             pltpu.VMEM((devices, 1, LANES), jnp.float32),
             dma((copies,)),
             dma((copies,)),
         ]
         + [dma((devices,))] * 2
+        + [dma((2,))] * 4
         + [dma((1,))] * 8
         + [dma((4,))],
         compiler_params=pltpu.CompilerParams(

time: 81.4 us -> 71.3 us (0.88)
  Pallas kernels: 75.4 us -> 65.3 us
    pallas_call x1, Pallas kernels: 75.4 us -> 65.3 us  [step(): pl.pallas_call(lambda *refs: step_kernel(low, *refs), out_shape=(jax.Shap...]
where the time goes in v5:
time: 71.3 us; the launch traced here: 71.2 us
  Pallas kernels  65.3 us (92%)
  local copies, waits for them, and re-layouts  5.22 us (7%)
    pallas_call x1, Pallas kernels, step(): pl.pallas_call(lambda *refs: step_kernel(low, *refs), out_shape=(jax.Shap...  65.3 us
    unnamed x7, local copies, waits for them, and re-layouts  5.22 us

profile of v5, /device:TPU:0, one launch (start us, length us, event | category | flops | bytes accessed | tf_op | source)
XLA Modules:
  0.0 71.2 jit_solution(5146173498111389623)
XLA Ops:
  0.6 65.3 %step.1 = (f32[128,4096]{1,0:T(8,128)}, f32[4,64,2048]{2,1,0:T(8,128)}, f32[64,2,32]{2,1,0:T(2,128)}) custom-call(bf16[4096,256]{1,0:T(8,128)(2,1)} %bitcast.8, f32[4,64,2048]{2,1,0:T(8,128)} %refs_1_.1, f32[128,4096]{1,0:T(8,128)} %refs_2_.1, bf16[2,256,256]{2,1,0:T(8,128)(2,1)} %constant.53.refs_3_, bf16[2,256,128]{2,1,0:T(8,128)(2,1)} %constant.60.refs_4_, ...), custom_call_target="tpu_custom_call" | custom-call | tf_op jit(solution)/shard_map/step/pallas_call | solution.py:1147
  66.0 0.0 copy-start
  66.0 3.3 %copy.32 = f32[128,4096]{1,0:T(8,128)} copy(f32[128,4096]{1,0:T(8,128)} %get-tuple-element.12) | data formatting | bytes 4194304
  69.2 0.0 copy-done
  69.2 0.0 copy-start.1
  69.2 1.3 %copy.33 = f32[4,64,2048]{2,1,0:T(8,128)} copy(f32[4,64,2048]{2,1,0:T(8,128)S(1)} %copy-done) | data formatting | bytes 4194304
  70.6 0.0 copy-done.1
  70.6 0.6 copy.34
Async XLA Ops:
  66.0 3.3 %copy-start = (f32[4,64,2048]{2,1,0:T(8,128)S(1)}, f32[4,64,2048]{2,1,0:T(8,128)}, u32[]{:S(2)}) copy-start(f32[4,64,2048]{2,1,0:T(8,128)} %get-tuple-element.13) | copy-start | bytes 6291460
  69.2 1.3 %copy-start.1 = (f32[64,2,32]{2,1,0:T(2,128)S(1)}, f32[64,2,32]{2,1,0:T(2,128)}, u32[]{:S(2)}) copy-start(f32[64,2,32]{2,1,0:T(2,128)} %get-tuple-element.8) | copy-start | bytes 49156

commit v6 on v5

--- a/solution.py
+++ b/solution.py
@@ -700,65 +700,84 @@
     parts = class_tiles // LANES
     lane = lax.broadcasted_iota(jnp.int32, (1, LANES), 1)
 
-    def block_of(u):
-        return u // 2 % 2 * groups + u // 4 * 4 + u % 2 * 2
-
-    def spread_class(c):
-        for i in range(parts):
-            first = block_of(2 * i) + c
-            columns = jnp.where(lane < tiles, all_cols_ref[first], all_cols_ref[first + 2])
-            k1 = columns % low
-            k2 = columns // low
-            flip = k1 >= kept
-            k1 = jnp.where(flip, low - k1, k1)
-            k2 = jnp.where(flip, wide - 1 - k2, k2)
-            fold_ref[0, pl.ds(c * parts + i, 1), :] = (k1 * wide + k2).astype(jnp.float32)
-            fold_ref[1, pl.ds(c * parts + i, 1), :] = jnp.where(flip, -1.0, 1.0)
-        chunk = 4 * LANES
-        for j in range(class_tiles // chunk):
-            n = chunk // tiles
-            some = [block_ref[block_of(j * n + i) + c] for i in range(n)]
+    def spread(c, levels_taken):
+        for zz in levels_taken:
+            for side in range(2):
+                b = c * parts + zz * 2 + side
+                first = side * groups + zz * 4 + c
+                columns = jnp.where(lane < tiles, all_cols_ref[first], all_cols_ref[first + 2])
+                k1 = columns % low
+                k2 = columns // low
+                flip = k1 >= kept
+                k1 = jnp.where(flip, low - k1, k1)
+                k2 = jnp.where(flip, wide - 1 - k2, k2)
+                fold_ref[0, pl.ds(b, 1), :] = (k1 * wide + k2).astype(jnp.float32)
+                fold_ref[1, pl.ds(b, 1), :] = jnp.where(flip, -1.0, 1.0)
+            some = [block_ref[i // 2 * groups + zz * 4 + i % 2 * 2 + c] for i in range(4)]
             both = nt_dot(turn_ref[...], jnp.concatenate(some, axis=0))
-            for i in range(chunk // LANES):
-                b = c * parts + j * (chunk // LANES) + i
+            for side in range(2):
+                b = c * parts + zz * 2 + side
                 at = pl.ds(pl.multiple_of(b * LANES, LANES), LANES)
-                real = both[:rows, i * LANES : (i + 1) * LANES]
-                imag = both[rows:, i * LANES : (i + 1) * LANES]
+                real = both[:rows, side * LANES : (side + 1) * LANES]
+                imag = both[rows:, side * LANES : (side + 1) * LANES]
                 sign = fold_ref[1, pl.ds(b, 1), :]
                 out_real = real * phase_ref[0] - imag * phase_ref[1]
                 out_imag = (real * phase_ref[1] + imag * phase_ref[0]) * sign
                 grid_ref[:rows, at] = out_real.astype(jnp.bfloat16)
                 grid_ref[rows:, at] = out_imag.astype(jnp.bfloat16)
 
-    def folded_class(c, p):
+    def folded_sum(c, levels_taken, p):
         base = pl.multiple_of(p * 2 * wide, 2 * wide)
         row = (lax.broadcasted_iota(jnp.int32, (2 * wide, LANES), 0) + base).astype(jnp.float32)
-        hots = []
-        for i in range(parts):
-            hit = row == fold_ref[0, pl.ds(c * parts + i, 1), :]
-            hots.append(jnp.where(hit, 1.0, 0.0).astype(jnp.bfloat16))
-        hot = jnp.concatenate(hots, axis=1)
-        at = pl.ds(pl.multiple_of(c * class_tiles, class_tiles), class_tiles)
-        hot_ref[pl.ds(base, 2 * wide), at] = hot
-        return nt_dot(grid_ref[:, at], hot)
-
-    spread_class(core)
+        total = None
+        for zz in levels_taken:
+            hots = []
+            for side in range(2):
+                hit = row == fold_ref[0, pl.ds(c * parts + zz * 2 + side, 1), :]
+                hots.append(jnp.where(hit, 1.0, 0.0).astype(jnp.bfloat16))
+            hot = jnp.concatenate(hots, axis=1)
+            at = c * class_tiles + zz * 2 * LANES
+            at = pl.ds(pl.multiple_of(at, 2 * LANES), 2 * LANES)
+            hot_ref[pl.ds(base, 2 * wide), at] = hot
+            out = nt_dot(grid_ref[:, at], hot)
+            total = out if total is None else total + out
+        return total
+
+    everything = list(range(levels))
+    spread(core, everything)
 
     def scatter_own(p, carry):
-        total_ref[p] = folded_class(core, p)
+        total_ref[p] = folded_sum(core, everything, p)
         return carry
 
     lax.fori_loop(0, (kept + 1) // 2, scatter_own, 0)
-    for i in range(groups):
-        got(2 * i + 1 - core)
-    spread_class(1 - core)
+    coming = [z] + [(z + levels - k) % levels for k in far]
+
+    def from_twin(zz):
+        for i in range(4):
+            got(i // 2 * groups + zz * 4 + i % 2 * 2 + 1 - core)
+
+    for zz in coming[:-1]:
+        from_twin(zz)
+    spread(1 - core, coming[:-1])
+
+    def scatter_more(p, carry):
+        total_ref[p] = total_ref[p] + folded_sum(1 - core, coming[:-1], p)
+        return carry
+
+    lax.fori_loop(0, (kept + 1) // 2, scatter_more, 0)
+    from_twin(coming[-1])
+    spread(1 - core, coming[-1:])
 
     def scatter(p, carry):
-        folded = (total_ref[p] + folded_class(1 - core, p)).astype(jnp.bfloat16)
+        folded = (total_ref[p] + folded_sum(1 - core, coming[-1:], p)).astype(jnp.bfloat16)
+        pairs = []
         for e in range(2):
             here = slice(e * wide, (e + 1) * wide)
-            pair = jnp.concatenate([folded[:rows, here], folded[rows:, here]], axis=1)
-            mid = nn_dot(pair, inv_ref[...])
+            pairs.append(jnp.concatenate([folded[:rows, here], folded[rows:, here]], axis=1))
+        mids = nn_dot(jnp.concatenate(pairs, axis=0), inv_ref[...])
+        for e in range(2):
+            mid = mids[e * rows : (e + 1) * rows]
             k1 = p * 2 + e
             tw_real, tw_imag = tw_ref[0, pl.ds(k1, 1), :], tw_ref[1, pl.ds(k1, 1), :]
             real, imag = mid[:, :wide], mid[:, wide:]
@@ -815,17 +834,21 @@
     top.start()
     loads[8].wait()
 
-    def spectrum(k, carry):
-        out = taps_dot(half_ref[k], fwd_ref)
-        here = pl.ds(pl.multiple_of(k * wide, wide), wide)
-        upper, lower = split(out)
-        spec_ref[:rows, here] = upper[:, :wide]
-        spec_ref[rows:, here] = upper[:, wide:]
-        rest_ref[:rows, here] = lower[:, :wide]
-        rest_ref[rows:, here] = lower[:, wide:]
+    batch = (kept + 1) // 3
+
+    def spectrum(i, carry):
+        some = half_ref[pl.ds(i * batch, batch)].reshape(batch * rows, 2 * wide)
+        out = taps_dot(some, fwd_ref)
+        for e in range(batch):
+            here = pl.ds(pl.multiple_of((i * batch + e) * wide, wide), wide)
+            upper, lower = split(out[e * rows : (e + 1) * rows])
+            spec_ref[:rows, here] = upper[:, :wide]
+            spec_ref[rows:, here] = upper[:, wide:]
+            rest_ref[:rows, here] = lower[:, :wide]
+            rest_ref[rows:, here] = lower[:, wide:]
         return carry
 
-    lax.fori_loop(0, kept, spectrum, 0)
+    lax.fori_loop(0, 3, spectrum, 0)
 
     mate = x * 4 + y * 2 + core
 
@@ -833,10 +856,10 @@
         at = to_class * class_tiles + (to_z * 4 + to_x * 2 + to_y) * tiles
         at = pl.ds(pl.multiple_of(at, tiles), tiles)
         unit = unit_ref.at[to_class * parts + to_z * 2 + to_x]
-        spot, half, target = to_z * 8 + mate, to_z // 2, device(to_x, z, to_y, to_class)
+        spot, target = to_z * 8 + mate, device(to_x, z, to_y, to_class)
         return [
-            remote(picked_ref.at[at, :], got_ref.at[spot], send_p.at[0], recv_p.at[half], target),
-            remote(unit, units_ref.at[spot], send_u.at[0], recv_u.at[half], target),
+            remote(picked_ref.at[at, :], got_ref.at[spot], send_p.at[0], recv_p.at[to_z], target),
+            remote(unit, units_ref.at[spot], send_u.at[0], recv_u.at[to_z], target),
         ]
 
     def total_of(ref, send, recv, count=devices - 1, at=0):
@@ -866,7 +889,7 @@
         j = to_class * 4 + to_z
         at = pl.multiple_of(j * 2 * LANES, 2 * LANES)
         hot = hot_ref[: kept * wide, pl.ds(at, 2 * LANES)]
-        both = nn_dot(spec_ref[...], hot) + nn_dot(rest_ref[...], hot)
+        both = nn_dot(spec_ref[:, : kept * wide], hot) + nn_dot(rest_ref[:, : kept * wide], hot)
         for h in range(2):
             sign = fold_ref[1, pl.ds(2 * j + h, 1), :]
             real = both[:rows, h * LANES : (h + 1) * LANES]
@@ -922,23 +945,25 @@
             merged_ref[c, :, at] = joined_ref[c, 8:, at] + part
         return absolute
 
-    def plane_sums(n, absolute):
-        half = (z // 2 + 1 + n) % 2
-        total_of(got_ref, send_p, recv_p, 14, half).wait_recv()
-        total_of(units_ref, send_u, recv_u, 14, half).wait_recv()
-        rows_of = [units_ref[half * 16 + i] for i in range(16)]
-        units = jnp.concatenate(rows_of * (LANES // 16), axis=0).T
+    def plane_sums(taken):
+        many = len(taken) * tiles
+        rows_of = []
+        for zz in taken:
+            total_of(got_ref, send_p, recv_p, 7, zz).wait_recv()
+            total_of(units_ref, send_u, recv_u, 7, zz).wait_recv()
+            rows_of += [units_ref[zz * 8 + m] for m in range(8)]
+        units = jnp.concatenate(rows_of * (LANES // len(rows_of)), axis=0).T
         units = jnp.where(y == 0, units[:tiles], units[tiles:])
         cosine, sine = shift_ref[0], shift_ref[1]
         level_cos = half_spin_ref[0, pl.ds(4 * z, 1), :]
         level_sin = half_spin_ref[1, pl.ds(4 * z, 1), :]
-        for e in range(2):
+        for e, zz in enumerate(taken):
             strip_rows = slice(e * tiles, (e + 1) * tiles)
             for pair in range(4):
                 reals, imags = [], []
                 for side in range(2):
                     m = side * 4 + pair
-                    packed = got_ref[half * 16 + e * 8 + m]
+                    packed = got_ref[zz * 8 + m]
                     real = (packed + 32768) >> 16
                     imag = packed - (real << 16)
                     unit = units[:, e * 8 + m : e * 8 + m + 1]
@@ -956,9 +981,9 @@
                         terms_ref[1, p, strip_rows, here] = lower
         reals, imags = [], []
         for p in range(2):
-            out = nn_dot(terms_ref[0, p], sum_table_ref[0, p])
-            out = out + nn_dot(terms_ref[1, p], sum_table_ref[0, p])
-            out = out + nn_dot(terms_ref[0, p], sum_table_ref[1, p])
+            out = nn_dot(terms_ref[0, p, :many], sum_table_ref[0, p])
+            out = out + nn_dot(terms_ref[1, p, :many], sum_table_ref[0, p])
+            out = out + nn_dot(terms_ref[0, p, :many], sum_table_ref[1, p])
             part = slice(p * LANES, (p + 1) * LANES)
             turn_cos, turn_sin = level_cos[:, part], level_sin[:, part]
             real, imag = out[:, :LANES], out[:, LANES:]
@@ -970,34 +995,30 @@
         most = jnp.maximum(most, 1e-30)
         to_level = LEVELS / most
         packed = level(real * to_level) * 65536 + level(imag * to_level)
-        sums_unit_ref[half] = jnp.broadcast_to(most * (1.0 / LEVELS), (LANES, LANES)).T[:1]
-        for e in range(2):
+        unit = most * (1.0 / LEVELS)
+        for e, zz in enumerate(taken):
             strip_rows = slice(e * tiles, (e + 1) * tiles)
-            to_z = half * 2 + e
-            sums_out_ref[to_z] = packed[strip_rows]
-
-            @pl.when(to_z == z)
-            def _():
+            if zz is z:
                 own_ref[:, : 2 * LANES] = real[strip_rows]
                 own_ref[:, 2 * LANES :] = imag[strip_rows]
-
-            @pl.when(to_z != z)
-            def _():
-                target = device(x, to_z, y, core)
-                remote(
-                    sums_out_ref.at[to_z], sums_got_ref.at[z], send_z.at[0], recv_z.at[0], target
-                ).start()
-                remote(
-                    sums_unit_ref.at[half],
-                    sums_units_ref.at[z],
-                    send_w.at[0],
-                    recv_w.at[0],
-                    target,
-                ).start()
-
-        return lax.fori_loop(n * (low // 4), (n + 1) * (low // 4), cols_down, absolute)
-
-    absolute = lax.fori_loop(0, 2, plane_sums, jnp.zeros((half_rows, LANES), jnp.float32))
+                continue
+            sums_out_ref[zz] = packed[strip_rows]
+            wide_unit = jnp.broadcast_to(unit[strip_rows], (tiles, LANES))
+            sums_unit_ref[zz] = jnp.concatenate([wide_unit, wide_unit], axis=0).T[:1]
+            target = device(x, zz, y, core)
+            remote(
+                sums_out_ref.at[zz], sums_got_ref.at[z], send_z.at[0], recv_z.at[0], target
+            ).start()
+            remote(
+                sums_unit_ref.at[zz], sums_units_ref.at[z], send_w.at[0], recv_w.at[0], target
+            ).start()
+
+    plane_sums([ordered(0), ordered(1)])
+    absolute = jnp.zeros((half_rows, LANES), jnp.float32)
+    absolute = lax.fori_loop(0, low // 4, cols_down, absolute)
+    plane_sums([ordered(2)])
+    plane_sums([z])
+    absolute = lax.fori_loop(low // 4, low // 2, cols_down, absolute)
     abs_total = jnp.sum(jnp.sum(absolute, axis=0, keepdims=True), axis=1, keepdims=True)
     loads[13].wait()
 
@@ -1008,7 +1029,7 @@
     total_of(sums_units_ref, send_w, recv_w, levels - 1).wait_recv()
     units = [sums_units_ref[(z + k) % levels] for k in range(1, levels)]
     units = jnp.concatenate(units + [units[0]] * (LANES - levels + 1), axis=0).T
-    units = jnp.where(z % 2 == 0, units[:tiles], units[tiles:])
+    units = units[:tiles]
     real, imag = own_ref[:, : 2 * LANES], own_ref[:, 2 * LANES :]
     for k in range(1, levels):
         packed = sums_got_ref[(z + k) % levels]
@@ -1170,8 +1191,8 @@
             pltpu.VMEM((2 * rows, devices * tiles), jnp.bfloat16),
             pltpu.VMEM(((kept + 1) * LANES, devices * tiles), jnp.bfloat16),
             pltpu.VMEM((kept + 1, rows, 2 * LANES), jnp.float32),
-            pltpu.VMEM((2 * rows, kept * LANES), jnp.bfloat16),
-            pltpu.VMEM((2 * rows, kept * LANES), jnp.bfloat16),
+            pltpu.VMEM((2 * rows, (kept + 1) * LANES), jnp.bfloat16),
+            pltpu.VMEM((2 * rows, (kept + 1) * LANES), jnp.bfloat16),
             pltpu.VMEM((low, rows + 8, LANES), jnp.float32),
             pltpu.VMEM((devices * tiles, rows), jnp.int32),
             pltpu.VMEM((devices // 2, 1, LANES), jnp.float32),
@@ -1181,7 +1202,7 @@
             pltpu.VMEM((2, 2, 2 * tiles, 8 * rows), jnp.bfloat16),
             pltpu.VMEM((tiles, 2 * piece), jnp.float32),
             pltpu.VMEM((groups // 4, tiles, piece), jnp.int32),
-            pltpu.VMEM((2, 1, LANES), jnp.float32),
+            pltpu.VMEM((groups // 4, 1, LANES), jnp.float32),
             pltpu.VMEM((groups // 4, tiles, piece), jnp.int32),
             pltpu.VMEM((groups // 4, 1, LANES), jnp.float32),
             pltpu.VMEM((devices, 1, LANES), jnp.float32),
@@ -1190,7 +1211,7 @@
             dma((copies,)),
         ]
         + [dma((devices,))] * 2
-        + [dma((2,))] * 4
+        + [dma((groups // 4,))] * 4
         + [dma((1,))] * 8
         + [dma((4,))],
         compiler_params=pltpu.CompilerParams(

time: 71.3 us -> 72.9 us (1.022)
  Pallas kernels: 65.3 us -> 66.9 us
    pallas_call x1, Pallas kernels: 65.3 us -> 66.9 us  [step(): pl.pallas_call(lambda *refs: step_kernel(low, *refs), out_shape=(jax.Shap...]
where the time goes in v6:
time: 72.9 us; the launch traced here: 72.7 us
  Pallas kernels  66.9 us (92%)
  local copies, waits for them, and re-layouts  5.22 us (7%)
    pallas_call x1, Pallas kernels, step(): pl.pallas_call(lambda *refs: step_kernel(low, *refs), out_shape=(jax.Shap...  66.9 us
    unnamed x7, local copies, waits for them, and re-layouts  5.22 us

profile of v6, /device:TPU:0, one launch (start us, length us, event | category | flops | bytes accessed | tf_op | source)
XLA Modules:
  0.0 72.7 jit_solution(8449445947090267886)
XLA Ops:
  0.6 66.9 %step.1 = (f32[128,4096]{1,0:T(8,128)}, f32[4,64,2048]{2,1,0:T(8,128)}, f32[64,2,32]{2,1,0:T(2,128)}) custom-call(bf16[4096,256]{1,0:T(8,128)(2,1)} %bitcast.8, f32[4,64,2048]{2,1,0:T(8,128)} %refs_1_.1, f32[128,4096]{1,0:T(8,128)} %refs_2_.1, bf16[2,256,256]{2,1,0:T(8,128)(2,1)} %constant.53.refs_3_, bf16[2,256,128]{2,1,0:T(8,128)(2,1)} %constant.60.refs_4_, ...), custom_call_target="tpu_custom_call" | custom-call | tf_op jit(solution)/shard_map/step/pallas_call | solution.py:1168
  67.5 0.0 copy-start
  67.5 3.3 %copy.32 = f32[128,4096]{1,0:T(8,128)} copy(f32[128,4096]{1,0:T(8,128)} %get-tuple-element.12) | data formatting | bytes 4194304
  70.8 0.0 copy-done
  70.8 0.0 copy-start.1
  70.8 1.3 %copy.33 = f32[4,64,2048]{2,1,0:T(8,128)} copy(f32[4,64,2048]{2,1,0:T(8,128)S(1)} %copy-done) | data formatting | bytes 4194304
  72.1 0.0 copy-done.1
  72.1 0.6 copy.34
Async XLA Ops:
  67.5 3.3 %copy-start = (f32[4,64,2048]{2,1,0:T(8,128)S(1)}, f32[4,64,2048]{2,1,0:T(8,128)}, u32[]{:S(2)}) copy-start(f32[4,64,2048]{2,1,0:T(8,128)} %get-tuple-element.13) | copy-start | bytes 6291460
  70.8 1.3 %copy-start.1 = (f32[64,2,32]{2,1,0:T(2,128)S(1)}, f32[64,2,32]{2,1,0:T(2,128)}, u32[]{:S(2)}) copy-start(f32[64,2,32]{2,1,0:T(2,128)} %get-tuple-element.8) | copy-start | bytes 49156

commit v7 on v6

--- a/solution.py
+++ b/solution.py
@@ -618,11 +618,25 @@
     edge = remote(tail_ref, halo_ref, halo_sem.at[0], halo_sem.at[1], ident(after))
     edge.start()
     start(me, twin, next(slots_of))
+    for load in loads[2:8]:
+        load.wait()
+    piece = kernels_ref.shape[1]
+    spin_cos, spin_sin = spin_ref[0, pl.ds(me, 1), :], spin_ref[1, pl.ds(me, 1), :]
+    cosine = (base_ref[0] * spin_cos - base_ref[1] * spin_sin).astype(jnp.bfloat16)
+    sine = (base_ref[1] * spin_cos + base_ref[0] * spin_sin).astype(jnp.bfloat16)
+    turn_ref[:rows, :piece] = cosine
+    turn_ref[:rows, piece:] = -sine
+    turn_ref[rows:, :piece] = sine
+    turn_ref[rows:, piece:] = cosine
     line_blocks = [index(x, (z + levels - k) % levels, y, core) for k in far]
     for block in line_blocks:
         got(block)
         for target in plane:
             start(block, target, next(slots_of))
+        start(block, twin, next(slots_of))
+    for px, py in corners:
+        block = index(px, z, py, core)
+        got(block)
         start(block, twin, next(slots_of))
     edge.wait()
     for c in range(4):
@@ -645,12 +659,6 @@
 
     lax.fori_loop(0, strips, tall, 0)
 
-    for px, py in corners:
-        block = index(px, z, py, core)
-        got(block)
-        start(block, twin, next(slots_of))
-    for load in loads[2:8]:
-        load.wait()
 
     def broad(i, carry):
         there = (i + strips - 1) % strips
@@ -663,30 +671,6 @@
         return carry
 
     lax.fori_loop(0, strips // 2, broad, 0)
-    spin_cos, spin_sin = spin_ref[0, pl.ds(me, 1), :], spin_ref[1, pl.ds(me, 1), :]
-    cosine = (base_ref[0] * spin_cos - base_ref[1] * spin_sin).astype(jnp.bfloat16)
-    sine = (base_ref[1] * spin_cos + base_ref[0] * spin_sin).astype(jnp.bfloat16)
-    piece = kernels_ref.shape[1]
-    turn_ref[:rows, :piece] = cosine
-    turn_ref[:rows, piece:] = -sine
-    turn_ref[rows:, :piece] = sine
-    turn_ref[rows:, piece:] = cosine
-    for load in loads[11:13]:
-        load.wait()
-    for n in range(4):
-        spin_cos, spin_sin = half_spin_ref[0, n : n + 1, :], half_spin_ref[1, n : n + 1, :]
-        cosine = half_base_ref[0] * spin_cos - half_base_ref[1] * spin_sin
-        sine = half_base_ref[1] * spin_cos + half_base_ref[0] * spin_sin
-        for p in range(2):
-            part = slice(p * LANES, (p + 1) * LANES)
-            c, d = split(cosine[:, part]), split(sine[:, part])
-            real_rows = slice(2 * n * rows, (2 * n + 1) * rows)
-            imag_rows = slice((2 * n + 1) * rows, (2 * n + 2) * rows)
-            for e in range(2):
-                sum_table_ref[e, p, real_rows, :LANES] = c[e]
-                sum_table_ref[e, p, real_rows, LANES:] = -d[e]
-                sum_table_ref[e, p, imag_rows, :LANES] = d[e]
-                sum_table_ref[e, p, imag_rows, LANES:] = c[e]
     for n, k in enumerate(far):
         for px, py in corners:
             block = index(px, (z + levels - k) % levels, py, core)
@@ -726,28 +710,23 @@
                 grid_ref[:rows, at] = out_real.astype(jnp.bfloat16)
                 grid_ref[rows:, at] = out_imag.astype(jnp.bfloat16)
 
-    def folded_sum(c, levels_taken, p):
+    def folded_sum(c, p):
         base = pl.multiple_of(p * 2 * wide, 2 * wide)
         row = (lax.broadcasted_iota(jnp.int32, (2 * wide, LANES), 0) + base).astype(jnp.float32)
-        total = None
-        for zz in levels_taken:
-            hots = []
-            for side in range(2):
-                hit = row == fold_ref[0, pl.ds(c * parts + zz * 2 + side, 1), :]
-                hots.append(jnp.where(hit, 1.0, 0.0).astype(jnp.bfloat16))
-            hot = jnp.concatenate(hots, axis=1)
-            at = c * class_tiles + zz * 2 * LANES
-            at = pl.ds(pl.multiple_of(at, 2 * LANES), 2 * LANES)
-            hot_ref[pl.ds(base, 2 * wide), at] = hot
-            out = nt_dot(grid_ref[:, at], hot)
-            total = out if total is None else total + out
-        return total
+        hots = []
+        for i in range(parts):
+            hit = row == fold_ref[0, pl.ds(c * parts + i, 1), :]
+            hots.append(jnp.where(hit, 1.0, 0.0).astype(jnp.bfloat16))
+        hot = jnp.concatenate(hots, axis=1)
+        at = pl.ds(pl.multiple_of(c * class_tiles, class_tiles), class_tiles)
+        hot_ref[pl.ds(base, 2 * wide), at] = hot
+        return nt_dot(grid_ref[:, at], hot)
 
     everything = list(range(levels))
     spread(core, everything)
 
     def scatter_own(p, carry):
-        total_ref[p] = folded_sum(core, everything, p)
+        total_ref[p] = folded_sum(core, p)
         return carry
 
     lax.fori_loop(0, (kept + 1) // 2, scatter_own, 0)
@@ -757,20 +736,12 @@
         for i in range(4):
             got(i // 2 * groups + zz * 4 + i % 2 * 2 + 1 - core)
 
-    for zz in coming[:-1]:
+    for zz in coming:
         from_twin(zz)
-    spread(1 - core, coming[:-1])
-
-    def scatter_more(p, carry):
-        total_ref[p] = total_ref[p] + folded_sum(1 - core, coming[:-1], p)
-        return carry
-
-    lax.fori_loop(0, (kept + 1) // 2, scatter_more, 0)
-    from_twin(coming[-1])
-    spread(1 - core, coming[-1:])
+    spread(1 - core, everything)
 
     def scatter(p, carry):
-        folded = (total_ref[p] + folded_sum(1 - core, coming[-1:], p)).astype(jnp.bfloat16)
+        folded = (total_ref[p] + folded_sum(1 - core, p)).astype(jnp.bfloat16)
         pairs = []
         for e in range(2):
             here = slice(e * wide, (e + 1) * wide)
@@ -913,6 +884,22 @@
         return carry
 
     lax.fori_loop(0, devices // 4, pick, 0)
+    for load in loads[11:13]:
+        load.wait()
+    for n in range(4):
+        spin_cos, spin_sin = half_spin_ref[0, n : n + 1, :], half_spin_ref[1, n : n + 1, :]
+        cosine = half_base_ref[0] * spin_cos - half_base_ref[1] * spin_sin
+        sine = half_base_ref[1] * spin_cos + half_base_ref[0] * spin_sin
+        for p in range(2):
+            part = slice(p * LANES, (p + 1) * LANES)
+            c, d = split(cosine[:, part]), split(sine[:, part])
+            real_rows = slice(2 * n * rows, (2 * n + 1) * rows)
+            imag_rows = slice((2 * n + 1) * rows, (2 * n + 2) * rows)
+            for e in range(2):
+                sum_table_ref[e, p, real_rows, :LANES] = c[e]
+                sum_table_ref[e, p, real_rows, LANES:] = -d[e]
+                sum_table_ref[e, p, imag_rows, :LANES] = d[e]
+                sum_table_ref[e, p, imag_rows, LANES:] = c[e]
     for to_z in range(levels):
         at = core * class_tiles + (to_z * 4 + x * 2 + y) * tiles
         got_ref[to_z * 8 + mate] = picked_ref[pl.ds(pl.multiple_of(at, tiles), tiles), :]
@@ -1016,8 +1003,7 @@
     plane_sums([ordered(0), ordered(1)])
     absolute = jnp.zeros((half_rows, LANES), jnp.float32)
     absolute = lax.fori_loop(0, low // 4, cols_down, absolute)
-    plane_sums([ordered(2)])
-    plane_sums([z])
+    plane_sums([ordered(2), z])
     absolute = lax.fori_loop(low // 4, low // 2, cols_down, absolute)
     abs_total = jnp.sum(jnp.sum(absolute, axis=0, keepdims=True), axis=1, keepdims=True)
     loads[13].wait()

time: 72.9 us -> 69.5 us (0.953)
  Pallas kernels: 66.9 us -> 63.5 us
    pallas_call x1, Pallas kernels: 66.9 us -> 63.5 us  [step(): pl.pallas_call(lambda *refs: step_kernel(low, *refs), out_shape=(jax.Shap...]
where the time goes in v7:
time: 69.5 us; the launch traced here: 69.4 us
  Pallas kernels  63.5 us (91%)
  local copies, waits for them, and re-layouts  5.22 us (8%)
    pallas_call x1, Pallas kernels, step(): pl.pallas_call(lambda *refs: step_kernel(low, *refs), out_shape=(jax.Shap...  63.5 us
    unnamed x7, local copies, waits for them, and re-layouts  5.22 us

profile of v7, /device:TPU:0, one launch (start us, length us, event | category | flops | bytes accessed | tf_op | source)
XLA Modules:
  0.0 69.4 jit_solution(10785638269735475198)
XLA Ops:
  0.6 63.5 %step.1 = (f32[128,4096]{1,0:T(8,128)}, f32[4,64,2048]{2,1,0:T(8,128)}, f32[64,2,32]{2,1,0:T(2,128)}) custom-call(bf16[4096,256]{1,0:T(8,128)(2,1)} %bitcast.8, f32[4,64,2048]{2,1,0:T(8,128)} %refs_1_.1, f32[128,4096]{1,0:T(8,128)} %refs_2_.1, bf16[2,256,256]{2,1,0:T(8,128)(2,1)} %constant.53.refs_3_, bf16[2,256,128]{2,1,0:T(8,128)(2,1)} %constant.60.refs_4_, ...), custom_call_target="tpu_custom_call" | custom-call | tf_op jit(solution)/shard_map/step/pallas_call | solution.py:1154
  64.1 0.0 copy-start
  64.2 3.3 %copy.32 = f32[128,4096]{1,0:T(8,128)} copy(f32[128,4096]{1,0:T(8,128)} %get-tuple-element.12) | data formatting | bytes 4194304
  67.4 0.0 copy-done
  67.4 0.0 copy-start.1
  67.4 1.3 %copy.33 = f32[4,64,2048]{2,1,0:T(8,128)} copy(f32[4,64,2048]{2,1,0:T(8,128)S(1)} %copy-done) | data formatting | bytes 4194304
  68.7 0.0 copy-done.1
  68.7 0.6 copy.34
Async XLA Ops:
  64.1 3.3 %copy-start = (f32[4,64,2048]{2,1,0:T(8,128)S(1)}, f32[4,64,2048]{2,1,0:T(8,128)}, u32[]{:S(2)}) copy-start(f32[4,64,2048]{2,1,0:T(8,128)} %get-tuple-element.13) | copy-start | bytes 6291460
  67.4 1.3 %copy-start.1 = (f32[64,2,32]{2,1,0:T(2,128)S(1)}, f32[64,2,32]{2,1,0:T(2,128)}, u32[]{:S(2)}) copy-start(f32[64,2,32]{2,1,0:T(2,128)} %get-tuple-element.8) | copy-start | bytes 49156

commit v8 on v7

--- a/solution.py
+++ b/solution.py
@@ -710,16 +710,18 @@
                 grid_ref[:rows, at] = out_real.astype(jnp.bfloat16)
                 grid_ref[rows:, at] = out_imag.astype(jnp.bfloat16)
 
+    some = (kept + 1) // 3
+
     def folded_sum(c, p):
-        base = pl.multiple_of(p * 2 * wide, 2 * wide)
-        row = (lax.broadcasted_iota(jnp.int32, (2 * wide, LANES), 0) + base).astype(jnp.float32)
+        base = pl.multiple_of(p * some * wide, some * wide)
+        row = (lax.broadcasted_iota(jnp.int32, (some * wide, LANES), 0) + base).astype(jnp.float32)
         hots = []
         for i in range(parts):
             hit = row == fold_ref[0, pl.ds(c * parts + i, 1), :]
             hots.append(jnp.where(hit, 1.0, 0.0).astype(jnp.bfloat16))
         hot = jnp.concatenate(hots, axis=1)
         at = pl.ds(pl.multiple_of(c * class_tiles, class_tiles), class_tiles)
-        hot_ref[pl.ds(base, 2 * wide), at] = hot
+        hot_ref[pl.ds(base, some * wide), at] = hot
         return nt_dot(grid_ref[:, at], hot)
 
     everything = list(range(levels))
@@ -729,7 +731,7 @@
         total_ref[p] = folded_sum(core, p)
         return carry
 
-    lax.fori_loop(0, (kept + 1) // 2, scatter_own, 0)
+    lax.fori_loop(0, 3, scatter_own, 0)
     coming = [z] + [(z + levels - k) % levels for k in far]
 
     def from_twin(zz):
@@ -743,20 +745,20 @@
     def scatter(p, carry):
         folded = (total_ref[p] + folded_sum(1 - core, p)).astype(jnp.bfloat16)
         pairs = []
-        for e in range(2):
+        for e in range(some):
             here = slice(e * wide, (e + 1) * wide)
             pairs.append(jnp.concatenate([folded[:rows, here], folded[rows:, here]], axis=1))
         mids = nn_dot(jnp.concatenate(pairs, axis=0), inv_ref[...])
-        for e in range(2):
+        for e in range(some):
             mid = mids[e * rows : (e + 1) * rows]
-            k1 = p * 2 + e
+            k1 = p * some + e
             tw_real, tw_imag = tw_ref[0, pl.ds(k1, 1), :], tw_ref[1, pl.ds(k1, 1), :]
             real, imag = mid[:, :wide], mid[:, wide:]
             half_ref[k1, :, :wide] = real * tw_real - imag * tw_imag
             half_ref[k1, :, wide:] = real * tw_imag + imag * tw_real
         return carry
 
-    lax.fori_loop(0, (kept + 1) // 2, scatter, 0)
+    lax.fori_loop(0, 3, scatter, 0)
 
     def strip(i, carry):
         at = pl.ds(pl.multiple_of(i * 8, 8), 8)
@@ -1170,7 +1172,7 @@
             pltpu.VMEM((devices, tiles, 2 * piece), jnp.bfloat16),
             pltpu.VMEM((devices, 1, LANES), jnp.int32),
             pltpu.VMEM((2 * rows, 2 * piece), jnp.bfloat16),
-            pltpu.VMEM(((kept + 1) // 2, 2 * rows, 2 * LANES), jnp.float32),
+            pltpu.VMEM((3, 2 * rows, (kept + 1) // 3 * LANES), jnp.float32),
             pltpu.VMEM((low, rows, LANES), jnp.float32),
             pltpu.VMEM((low, rows, LANES), jnp.float32),
             pltpu.VMEM((2, devices // 2, LANES), jnp.float32),

time: 69.5 us -> 66.4 us (0.955)
  Pallas kernels: 63.5 us -> 60.4 us
    pallas_call x1, Pallas kernels: 63.5 us -> 60.4 us  [step(): pl.pallas_call(lambda *refs: step_kernel(low, *refs), out_shape=(jax.Shap...]
where the time goes in v8:
time: 66.4 us; the launch traced here: 66.2 us
  Pallas kernels  60.4 us (91%)
  local copies, waits for them, and re-layouts  5.22 us (8%)
    pallas_call x1, Pallas kernels, step(): pl.pallas_call(lambda *refs: step_kernel(low, *refs), out_shape=(jax.Shap...  60.4 us
    unnamed x7, local copies, waits for them, and re-layouts  5.22 us

profile of v8, /device:TPU:0, one launch (start us, length us, event | category | flops | bytes accessed | tf_op | source)
XLA Modules:
  0.0 66.2 jit_solution(17286070232763034680)
XLA Ops:
  0.6 60.4 %step.1 = (f32[128,4096]{1,0:T(8,128)}, f32[4,64,2048]{2,1,0:T(8,128)}, f32[64,2,32]{2,1,0:T(2,128)}) custom-call(bf16[4096,256]{1,0:T(8,128)(2,1)} %bitcast.8, f32[4,64,2048]{2,1,0:T(8,128)} %refs_1_.1, f32[128,4096]{1,0:T(8,128)} %refs_2_.1, bf16[2,256,256]{2,1,0:T(8,128)(2,1)} %constant.53.refs_3_, bf16[2,256,128]{2,1,0:T(8,128)(2,1)} %constant.60.refs_4_, ...), custom_call_target="tpu_custom_call" | custom-call | tf_op jit(solution)/shard_map/step/pallas_call | solution.py:1156
  61.0 0.0 copy-start
  61.0 3.3 %copy.32 = f32[128,4096]{1,0:T(8,128)} copy(f32[128,4096]{1,0:T(8,128)} %get-tuple-element.12) | data formatting | bytes 4194304
  64.3 0.0 copy-done
  64.3 0.0 copy-start.1
  64.3 1.3 %copy.33 = f32[4,64,2048]{2,1,0:T(8,128)} copy(f32[4,64,2048]{2,1,0:T(8,128)S(1)} %copy-done) | data formatting | bytes 4194304
  65.6 0.0 copy-done.1
  65.6 0.6 copy.34
Async XLA Ops:
  61.0 3.3 %copy-start = (f32[4,64,2048]{2,1,0:T(8,128)S(1)}, f32[4,64,2048]{2,1,0:T(8,128)}, u32[]{:S(2)}) copy-start(f32[4,64,2048]{2,1,0:T(8,128)} %get-tuple-element.13) | copy-start | bytes 6291460
  64.3 1.3 %copy-start.1 = (f32[64,2,32]{2,1,0:T(2,128)S(1)}, f32[64,2,32]{2,1,0:T(2,128)}, u32[]{:S(2)}) copy-start(f32[64,2,32]{2,1,0:T(2,128)} %get-tuple-element.8) | copy-start | bytes 49156
